TPU v7x, 256 devices: a whole 4x4x8 slice. The times are simulated.
256 devices in a mesh: gx: 8 (over x, core), gy: 8 (over z), gz: 4 (over y).
Axes of the slice: x: 4, y: 4, z: 8, core: 2. Of those that a mesh axis runs over, the one named last changes fastest.
Arguments:
- pair_list: int32 [8192, 2], P(('gx', 'gy', 'gz')), may hold values from 0 to 63, all different within a row; in each aligned block of 32 rows (0 to 31, 32 to 63, ...) at most 2 rows name the same one
- rank_bucket: int32 [8192], P(('gx', 'gy', 'gz')), may hold values from 0 to 2
- amplitudes: bfloat16 [8192, 36864], P(('gx', 'gy', 'gz')), may hold values from -0.4375 to 0.4375
- intersects: bfloat16 [8192, 36864], P(('gx', 'gy', 'gz')), may hold values from -0.4375 to 0.4375
- integrals: bfloat16 [8192, 36864], P(('gx', 'gy', 'gz')), may hold values from -6 to 6
- exchange_blocks: bfloat16 [64, 36864], P(('gx', 'gy')), may hold values from -0.4375 to 0.4375
Outputs:
- residuals: bfloat16 [8192, 36864], P(('gx', 'gy', 'gz'))
Inputs may be any that keep to these rules, and one draw needn't show every extreme that they name: `pair_list`: each row names two different occupied orbitals; within the rows of one device no orbital is named more than 2 times, a bound that some block reaches on some devices. `rank_bucket`: bucket b keeps the leading (b + 1) * 64 PNOs.
All inputs are finite; a program needn't handle non-finite values.
Results may differ from a plain program's by a relative error of at most 0.013.
Values may be sent and summed in bfloat16 or wider, within the bound.
No kernel may reach another device: no remote copies, remote signals or barrier semaphores. Data moves between devices by JAX's collectives and lax.ppermute only.
A program may use at most 128 MiB of HBM per device.

v0:
```python
import jax
import jax.numpy as jnp
from jax import lax
from jax.experimental import pallas as pl
from jax.experimental.pallas import tpu as pltpu
from jax.sharding import Mesh
from jax.sharding import PartitionSpec as P

RSTEP = 64
R = 192
Q = 48
QP = 72
STEP = 8
AXES = ("gx_0", "gx_1", "gy", "gz")
GX_GY = ("gx_0", "gx_1", "gy")
BF16 = jnp.bfloat16
F32 = jnp.float32


def device_number(x, c, z, y):
    return ((x * 2 + c) * 8 + z) * 4 + y


def pairs_of(move):
    out = []
    for x in range(4):
        for c in range(2):
            for z in range(8):
                for y in range(4):
                    out.append((device_number(x, c, z, y), device_number(*move(x, c, z, y))))
    return out


def stage_a(array, d):
    return lax.ppermute(
        array, AXES, pairs_of(lambda x, c, z, y: (x ^ d, c, z, y) if c == 0 else (x, c, z, y ^ d))
    )


def stage_b(array, d):
    return lax.ppermute(
        array, AXES, pairs_of(lambda x, c, z, y: (x, c, z, y ^ d) if c == 0 else (x ^ d, c, z, y))
    )


def stage_z(array, d):
    return lax.ppermute(array, AXES, pairs_of(lambda x, c, z, y: (x, c, z ^ d, y)))


def stage_c(array):
    return lax.ppermute(array, AXES, pairs_of(lambda x, c, z, y: (x, c ^ 1, z, y)))


def slot_of(k, q, at_ref):
    x, c, z, y = (at_ref[i] for i in range(4))
    core = (k >> 3) & 1
    dx, dq, dz = (k >> 4) ^ x, q ^ y, (k & 7) ^ z
    a = jnp.where(core == 0, dx, dq)
    b = jnp.where(core == 0, dq, dx)
    return (((core ^ c) * 4 + a) * 4 + b) * 8 + (dz & 1) * 4 + (dz >> 1)


def packed_quarter(block, q):
    rows = block[q * Q : (q + 1) * Q]
    right = jnp.concatenate([rows[: Q // 2, 128:], rows[Q // 2 :, 128:]], axis=1)
    return jnp.concatenate([rows[:, :128], right], axis=0)


def unpacked_quarter(piece):
    right = piece[Q:]
    right = jnp.concatenate([right[:, :64], right[:, 64:]], axis=0)
    return jnp.concatenate([piece[:Q], right], axis=1)


def masks(rank):
    rows = lax.broadcasted_iota(jnp.int32, (R, R), 0)
    cols = lax.broadcasted_iota(jnp.int32, (R, R), 1)
    return (rows < rank) & (cols < rank)


def dot(a, b, dims):
    return lax.dot_general(a, b, (dims, ((), ())), preferred_element_type=F32)


VLIM = 20

SMEM = pl.BlockSpec(memory_space=pltpu.SMEM)
VMEM = pl.BlockSpec(memory_space=pltpu.VMEM)
GROUP = (4, 8, QP, 128)


def call(kernel, n_smem, n_vmem, out_shape, scratch, flops, limit_mib):
    return pl.pallas_call(
        kernel,
        in_specs=[SMEM] * n_smem + [VMEM] * n_vmem,
        out_specs=jax.tree.map(lambda _: VMEM, out_shape),
        out_shape=out_shape,
        scratch_shapes=scratch,
        compiler_params=pltpu.CompilerParams(vmem_limit_bytes=limit_mib << 20),
        cost_estimate=pl.CostEstimate(flops=flops, transcendentals=0, bytes_accessed=1 << 20),
    )


def each_pair(pairs, work):
    def step(n, _):
        for i in range(STEP):
            work(n * STEP + i)
        return _

    lax.fori_loop(0, pairs // STEP, step, 0)


def project_kernel(ends_ref, rank_ref, at_ref, s_ref, m_ref, p_ref, *rest):
    out_refs, sums_ref = rest[:8], rest[8]
    sums_ref[...] = jnp.zeros_like(sums_ref)

    def work(pair):
        inside = masks((rank_ref[pair] + 1) * RSTEP)
        masked = jnp.where(inside, m_ref[pair].astype(F32), 0.0).astype(BF16)
        half = dot(s_ref[pair], masked, ((1,), (0,))).astype(BF16)
        full = dot(half, s_ref[pair], ((1,), (1,)))
        p_ref[pair] = full.astype(BF16)
        for q in range(4):
            piece = packed_quarter(full, q).astype(BF16)
            for e in range(2):
                slot = slot_of(ends_ref[e, pair], q, at_ref)
                sums_ref[slot] = sums_ref[slot] + piece

    each_pair(s_ref.shape[0], work)
    for n in range(8):
        out_refs[n][...] = sums_ref[n * 32 : (n + 1) * 32].reshape(GROUP)


def project(ends, rank, at, s, m):
    pairs = s.shape[0]
    return call(
        project_kernel,
        3,
        2,
        [jax.ShapeDtypeStruct((pairs, R, R), BF16)] + [jax.ShapeDtypeStruct(GROUP, BF16)] * 8,
        [pltpu.VMEM((256, QP, 128), BF16)],
        pairs * 4 * R**3,
        VLIM,
    )(ends, rank, at, s, m)


def base_kernel(rank_ref, m_ref, v_ref, base_ref):
    def work(pair):
        inside = masks((rank_ref[pair] + 1) * RSTEP)
        masked = jnp.where(inside, m_ref[pair].astype(F32), 0.0).astype(BF16)
        base_ref[pair] = v_ref[pair].astype(F32) + dot(masked, v_ref[pair], ((1,), (0,)))

    each_pair(m_ref.shape[0], work)


def base_of(rank, m, v):
    pairs = m.shape[0]
    return call(
        base_kernel, 1, 2, jax.ShapeDtypeStruct((pairs, R, R), F32), [], pairs * 2 * R**3, VLIM
    )(rank, m, v)


def own_kernel(ends_ref, at_ref, p_ref, *rest):
    group_refs, own_ref, held_ref = rest[:8], rest[8], rest[9]
    for n in range(8):
        held_ref[n * 32 : (n + 1) * 32] = group_refs[n][...].reshape(32, QP, 128)

    def work(pair):
        quarters = []
        for q in range(4):
            first = held_ref[slot_of(ends_ref[0, pair], q, at_ref)].astype(F32)
            second = held_ref[slot_of(ends_ref[1, pair], q, at_ref)].astype(F32)
            quarters.append(unpacked_quarter(first + second))
        both = jnp.concatenate(quarters, axis=0).astype(BF16)
        own = dot(p_ref[pair], both, ((1,), (0,)))
        for q in range(4):
            own_ref[pair, q] = packed_quarter(own, q).astype(BF16)

    each_pair(p_ref.shape[0], work)


def own_of(ends, at, p, groups):
    pairs = p.shape[0]
    return call(
        own_kernel,
        2,
        9,
        jax.ShapeDtypeStruct((pairs, 4, QP, 128), BF16),
        [pltpu.VMEM((256, QP, 128), BF16)],
        pairs * 2 * R**3,
        VLIM,
    )(ends, at, p, *groups)


def couple_kernel(d0_ref, d1_ref, d2_ref, d3_ref, x0_ref, x1_ref, x2_ref, x3_ref, c_ref):
    for t, x_ref in enumerate((x0_ref, x1_ref, x2_ref, x3_ref)):
        total = d0_ref[t].astype(F32) + d1_ref[t ^ 1].astype(F32)
        total = total + (d2_ref[t ^ 2].astype(F32) + d3_ref[t ^ 3].astype(F32))
        domain = unpacked_quarter(total).astype(BF16)
        block = [unpacked_quarter(x_ref[q].astype(F32)) for q in range(4)]
        block = jnp.concatenate(block, axis=0).astype(BF16)
        c_ref[t] = packed_quarter(dot(domain, block, ((1,), (0,))), 0).astype(BF16)


def couple(parts, near):
    return call(
        couple_kernel, 0, 8, jax.ShapeDtypeStruct((4, QP, 128), BF16), [], 8 * Q * R * R, VLIM
    )(*parts, *near)


def finish_kernel(ends_ref, rank_ref, at_ref, s_ref, own_ref, base_ref, *rest):
    group_refs, out_ref, held_ref = rest[:8], rest[8], rest[9]
    for n in range(8):
        held_ref[n * 32 : (n + 1) * 32] = group_refs[n][...].reshape(32, QP, 128)

    def work(pair):
        quarters = []
        for q in range(4):
            first = held_ref[slot_of(ends_ref[0, pair], q, at_ref)].astype(F32)
            second = held_ref[slot_of(ends_ref[1, pair], q, at_ref)].astype(F32)
            quarters.append(unpacked_quarter((first + second) - own_ref[pair, q].astype(F32)))
        combined = jnp.concatenate(quarters, axis=0).astype(BF16)
        half = dot(s_ref[pair], combined, ((0,), (0,))).astype(BF16)
        total = base_ref[pair] + dot(half, s_ref[pair], ((1,), (0,)))
        inside = masks((rank_ref[pair] + 1) * RSTEP)
        out_ref[pair] = jnp.where(inside, total, 0.0).astype(BF16)

    each_pair(s_ref.shape[0], work)


def finish(ends, rank, at, s, own, base, groups):
    pairs = s.shape[0]
    return call(
        finish_kernel,
        3,
        11,
        jax.ShapeDtypeStruct((pairs, R, R), BF16),
        [pltpu.VMEM((256, QP, 128), BF16)],
        pairs * 4 * R**3,
        VLIM,
    )(ends, rank, at, s, own, base, *groups)


def added(*arrays):
    total = arrays[0].astype(F32)
    for a in arrays[1:]:
        total = total + a.astype(F32)
    return total.astype(BF16)


def sent_to_all(mine):
    both = jnp.concatenate([mine, stage_z(mine, 1)], axis=0)
    group = [both] + [stage_b(both, d) for d in (1, 2, 3)]
    group = jnp.stack(group, axis=0)
    groups = [group] + [stage_a(group, d) for d in (2, 1, 3)]
    groups = [groups[0], groups[2], groups[1], groups[3]]
    return groups + [stage_c(groups[n]) for n in range(4)]


def whole_step(pair_list, rank_bucket, amplitudes, intersects, integrals, exchange_blocks):
    pairs = amplitudes.shape[0]
    at = jnp.stack([lax.axis_index(a) for a in AXES]).astype(jnp.int32)
    y = lax.axis_index("gz")
    ends = pair_list.T

    block = exchange_blocks.reshape(R, R)
    block = jnp.stack([packed_quarter(block, q) for q in range(4)], axis=0)
    near = [block] + [stage_z(block, 2 * d) for d in (1, 2, 3)]
    quarters = [lax.dynamic_slice_in_dim(b, y, 1, axis=0) for b in near]
    quarters = jnp.concatenate(quarters, axis=0)
    blocks = sent_to_all(quarters)

    m = amplitudes.reshape(pairs, R, R)
    s = intersects.reshape(pairs, R, R)
    p, *sums = project(ends, rank_bucket, at, s, m)
    v = integrals.reshape(pairs, R, R)
    base = base_of(rank_bucket, m, v)

    sums = [added(sums[a], stage_c(sums[4 + a])) for a in (2, 1, 3, 0)]
    moved = [stage_a(sums[n], d) for n, d in enumerate((2, 1, 3))]
    sums = added(sums[3], *moved)
    sums = added(sums[0], *[stage_b(sums[d], d) for d in (1, 2, 3)])
    sums = added(sums[:4], stage_z(sums[4:], 1))
    parts = [sums] + [stage_z(sums, 2 * d) for d in (1, 2, 3)]
    coupled = couple(parts, near)
    own = own_of(ends, at, p, blocks)
    groups = sent_to_all(coupled)
    out = finish(ends, rank_bucket, at, s, own, base, groups)
    return out.reshape(pairs, R * R)


def solution(mesh):
    torus = Mesh(mesh.devices.reshape(4, 2, mesh.shape["gy"], mesh.shape["gz"]), AXES)
    everywhere = P(AXES, None)
    return jax.shard_map(
        whole_step,
        mesh=torus,
        in_specs=(everywhere, P(AXES), everywhere, everywhere, everywhere, P(GX_GY, None)),
        out_specs=everywhere,
        check_vma=False,
    )
```

profile of v0, /device:TPU:1, one launch (start us, length us, event | category | flops | bytes accessed | tf_op | source)
XLA Modules:
  0.0 168.7 jit_solution(17582615656766262452)
XLA Ops:
  0.0 4.9 %reshape.19.s_ref = bf16[32,192,192]{2,1,0:T(8,128)(2,1)S(1)} reshape(bf16[32,36864]{1,0:T(8,128)(2,1)} %param.9) | data formatting | bytes 4718592 | tf_op jit(solution)/shard_map/reshape | solution.py:274
  5.0 6.1 %reshape.20.m_ref = bf16[32,192,192]{2,1,0:T(8,128)(2,1)} reshape(bf16[32,36864]{1,0:T(8,128)(2,1)} %param.8) | data formatting | bytes 4718592 | tf_op jit(solution)/shard_map/reshape | solution.py:273
  13.1 6.2 %shard_map.64 = (bf16[32,192,192]{2,1,0:T(8,128)(2,1)S(1)}, bf16[4,8,72,128]{3,2,1,0:T(8,128)(2,1)S(1)}, bf16[4,8,72,128]{3,2,1,0:T(8,128)(2,1)S(1)}, bf16[4,8,7...) custom-call(s32[2,32]{1,0:T(2,128)S(1)} %bitcast.33, ...), custom_call_target="tpu_custom_call" | custom-call | flops 905969664 | bytes 1048576 | tf_op jit(solution)/shard_map/pallas_call | solution.py:136
  24.3 3.2 %collective-permute-start.15 = (bf16[4,8,72,128]{3,2,1,0:T(8,128)(2,1)}, bf16[4,8,72,128]{3,2,1,0:T(8,128)(2,1)}, u32[]{:S(2)}, u32[]{:S(2)}) collective-permute-start(bf16[4,8,72,128]{3,2,1,0:T(8,128)(2,1)} %get-tuple-element.18), channel_id=1, source_target_pairs={{0,32},{1,33},{2,34},{3,35},{4,36},{5,37},{6,38},{7,39},{8,40},{9,... | collective-permute-start | bytes 1769480 | tf_op jit(solution)/shard_map/ppermute | solution.py:51
  41.0 2.8 %collective-permute-done.x1_ref = bf16[4,72,128]{2,1,0:T(8,128)(2,1)S(1)} collective-permute-done((bf16[4,72,128]{2,1,0:T(8,128)(2,1)S(1)}, bf16[4,72,128]{2,1,0:T(8,128)(2,1)S(1)}, u32[]{:S(2)}, u32[]{:S(2)}) %collective-permute-start) | collective-permute-done | bytes 73760 | tf_op jit(solution)/shard_map/ppermute | solution.py:47
  43.8 7.5 %collective-permute-start.1 = (bf16[4,72,128]{2,1,0:T(8,128)(2,1)S(1)}, bf16[4,72,128]{2,1,0:T(8,128)(2,1)S(1)}, u32[]{:S(2)}, u32[]{:S(2)}) collective-permute-start(bf16[4,72,128]{2,1,0:T(8,128)(2,1)S(1)} %pad_maximum_fusion.3.x0_ref), channel_id=1, source_target_pairs={{0,16},{1,17},{2,18},{3,19},{4,20},{5,21},{6,22},{7,23},{8,24},{9,... | collective-permute-start | bytes 221192 | tf_op jit(solution)/shard_map/ppermute | solution.py:47
  55.4 3.1 %collective-permute-done.2.x3_ref = bf16[4,72,128]{2,1,0:T(8,128)(2,1)S(1)} collective-permute-done((bf16[4,72,128]{2,1,0:T(8,128)(2,1)S(1)}, bf16[4,72,128]{2,1,0:T(8,128)(2,1)S(1)}, u32[]{:S(2)}, u32[]{:S(2)}) %collective-permute-start.2) | collective-permute-done | bytes 73760 | tf_op jit(solution)/shard_map/ppermute | solution.py:47
  63.9 2.6 %collective-permute-start.22 = (bf16[8,72,128]{2,1,0:T(8,128)(2,1)S(1)}, bf16[8,72,128]{2,1,0:T(8,128)(2,1)S(1)}, u32[]{:S(2)}, u32[]{:S(2)}) collective-permute-start(bf16[8,72,128]{2,1,0:T(8,128)(2,1)S(1)} %get-tuple-element.37), channel_id=1, source_target_pairs={{0,2},{1,3},{2,0},{3,1},{4,6},{5,7},{6,4},{7,5},{8,10},{9,11},{10,... | collective-permute-start | bytes 442376 | tf_op jit(solution)/shard_map/ppermute | solution.py:41
  66.8 3.6 %collective-permute-start.5 = (bf16[8,72,128]{2,1,0:T(8,128)(2,1)S(1)}, bf16[8,72,128]{2,1,0:T(8,128)(2,1)S(1)}, u32[]{:S(2)}, u32[]{:S(2)}) collective-permute-start(bf16[8,72,128]{2,1,0:T(8,128)(2,1)S(1)} %constant_dynamic-update-slice_fusion), channel_id=1, source_target_pairs={{0,2},{1,3},{2,0},{3,1},{4,6},{5,7},{6,4},{7,5},{8,10},{9,11},{10,... | collective-permute-start | bytes 442376 | tf_op jit(solution)/shard_map/ppermute | solution.py:41
  72.4 2.3 %collective-permute-done.5 = bf16[8,72,128]{2,1,0:T(8,128)(2,1)S(1)} collective-permute-done((bf16[8,72,128]{2,1,0:T(8,128)(2,1)S(1)}, bf16[8,72,128]{2,1,0:T(8,128)(2,1)S(1)}, u32[]{:S(2)}, u32[]{:S(2)}) %collective-permute-start.5) | collective-permute-done | bytes 147488 | tf_op jit(solution)/shard_map/ppermute | solution.py:41
  80.0 4.4 %collective-permute-start.26 = (bf16[4,72,128]{2,1,0:T(8,128)(2,1)S(1)}, bf16[4,72,128]{2,1,0:T(8,128)(2,1)S(1)}, u32[]{:S(2)}, u32[]{:S(2)}) collective-permute-start(bf16[4,72,128]{2,1,0:T(8,128)(2,1)S(1)} %add_convert_fusion.5.d0_ref), channel_id=1, source_target_pairs={{0,16},{1,17},{2,18},{3,19},{4,20},{5,21},{6,22},{7,23},{8,24},{9,... | collective-permute-start | bytes 221192 | tf_op jit(solution)/shard_map/ppermute | solution.py:47
  85.9 6.6 %collective-permute-start.10 = (bf16[4,8,72,128]{3,2,1,0:T(8,128)(2,1)S(1)}, bf16[4,8,72,128]{3,2,1,0:T(8,128)(2,1)S(1)}, u32[]{:S(2)}, u32[]{:S(2)}) collective-permute-start(bf16[4,8,72,128]{3,2,1,0:T(8,128)(2,1)S(1)} %pad_maximum_fusion.rest_0_), channel_id=1, source_target_pairs={{0,32},{1,33},{2,34},{3,35},{4,36},{5,37},{6,38},{7,39},{8,40},{9,... | collective-permute-start | bytes 1769480 | tf_op jit(solution)/shard_map/ppermute | solution.py:51
  92.5 2.5 %collective-permute-start.27 = (bf16[4,72,128]{2,1,0:T(8,128)(2,1)S(1)}, bf16[4,72,128]{2,1,0:T(8,128)(2,1)S(1)}, u32[]{:S(2)}, u32[]{:S(2)}) collective-permute-start(bf16[4,72,128]{2,1,0:T(8,128)(2,1)S(1)} %add_convert_fusion.5.d0_ref), channel_id=1, source_target_pairs={{0,24},{1,25},{2,26},{3,27},{4,28},{5,29},{6,30},{7,31},{8,16},{9,... | collective-permute-start | bytes 221192 | tf_op jit(solution)/shard_map/ppermute | solution.py:47
  95.0 3.1 %collective-permute-done.27.d3_ref = bf16[4,72,128]{2,1,0:T(8,128)(2,1)S(1)} collective-permute-done((bf16[4,72,128]{2,1,0:T(8,128)(2,1)S(1)}, bf16[4,72,128]{2,1,0:T(8,128)(2,1)S(1)}, u32[]{:S(2)}, u32[]{:S(2)}) %collective-permute-start.27) | collective-permute-done | bytes 73760 | tf_op jit(solution)/shard_map/ppermute | solution.py:47
  98.8 3.3 %collective-permute-done.28 = bf16[4,72,128]{2,1,0:T(8,128)(2,1)S(1)} collective-permute-done((bf16[4,72,128]{2,1,0:T(8,128)(2,1)S(1)}, bf16[4,72,128]{2,1,0:T(8,128)(2,1)S(1)}, u32[]{:S(2)}, u32[]{:S(2)}) %collective-permute-start.28) | collective-permute-done | bytes 73760 | tf_op jit(solution)/shard_map/ppermute | solution.py:47
  102.3 3.7 %collective-permute-start.30 = (bf16[8,72,128]{2,1,0:T(8,128)(2,1)S(1)}, bf16[8,72,128]{2,1,0:T(8,128)(2,1)S(1)}, u32[]{:S(2)}, u32[]{:S(2)}) collective-permute-start(bf16[8,72,128]{2,1,0:T(8,128)(2,1)S(1)} %get-tuple-element.39), channel_id=1, source_target_pairs={{0,2},{1,3},{2,0},{3,1},{4,6},{5,7},{6,4},{7,5},{8,10},{9,11},{10,... | collective-permute-start | bytes 442376 | tf_op jit(solution)/shard_map/ppermute | solution.py:41
  106.6 6.7 %collective-permute-start.11 = (bf16[4,8,72,128]{3,2,1,0:T(8,128)(2,1)S(1)}, bf16[4,8,72,128]{3,2,1,0:T(8,128)(2,1)S(1)}, u32[]{:S(2)}, u32[]{:S(2)}) collective-permute-start(bf16[4,8,72,128]{3,2,1,0:T(8,128)(2,1)S(1)} %collective-permute-done.7.rest_1_), channel_id=1, source_target_pairs={{0,32},{1,33},{2,34},{3,35},{4,36},{5,37},{6,38},{7,39},{8,40},{9,... | collective-permute-start | bytes 1769480 | tf_op jit(solution)/shard_map/ppermute | solution.py:51
  127.6 5.8 %collective-permute-done.33.rest_2_ = bf16[4,8,72,128]{3,2,1,0:T(8,128)(2,1)} collective-permute-done((bf16[4,8,72,128]{3,2,1,0:T(8,128)(2,1)}, bf16[4,8,72,128]{3,2,1,0:T(8,128)(2,1)}, u32[]{:S(2)}, u32[]{:S(2)}) %collective-permute-start.33) | collective-permute-done | bytes 589856 | tf_op jit(solution)/shard_map/ppermute | solution.py:35
  133.4 3.7 %collective-permute-done.34.rest_3_ = bf16[4,8,72,128]{3,2,1,0:T(8,128)(2,1)} collective-permute-done((bf16[4,8,72,128]{3,2,1,0:T(8,128)(2,1)}, bf16[4,8,72,128]{3,2,1,0:T(8,128)(2,1)}, u32[]{:S(2)}, u32[]{:S(2)}) %collective-permute-start.34) | collective-permute-done | bytes 589856 | tf_op jit(solution)/shard_map/ppermute | solution.py:35
  137.5 6.1 %reshape.21.v_ref = bf16[32,192,192]{2,1,0:T(8,128)(2,1)} reshape(bf16[32,36864]{1,0:T(8,128)(2,1)} %param.10) | data formatting | bytes 4718592 | tf_op jit(solution)/shard_map/reshape | solution.py:276
  147.4 2.4 %shard_map.66.base_ref = f32[32,192,192]{2,1,0:T(8,128)S(1)} custom-call(s32[32]{0:T(128)S(1)} %copy-done.25, bf16[32,192,192]{2,1,0:T(8,128)(2,1)S(1)} %copy-done.1, bf16[32,192,192]{2,1,0:T(8,128)(2,1)S(1)} %copy-done.3), custom_call_target="tpu_custom_call" | custom-call | flops 452984832 | bytes 1048576 | tf_op jit(solution)/shard_map/pallas_call | solution.py:158
  150.2 4.6 %shard_map.65.own_ref = bf16[32,4,72,128]{3,2,1,0:T(8,128)(2,1)S(1)} custom-call(s32[2,32]{1,0:T(2,128)S(1)} %bitcast.34, s32[4]{0:T(128)S(1)} %pad_add_fusion.at_ref, bf16[32,192,192]{2,1,0:T(8,128)(2,1)S(1)} %copy-done.5, bf16[4,8,72,128]{3,2,1,0:T(8,128)(2,1)S(1)} %copy-done.7, bf16[4,8,72,128]{3,2,1,0:T(8,128)(2,1)S(1)} %copy-done.15, ...), custom_call_target="tpu_custom_call" | custom-call | flops 452984832 | bytes 1048576 | tf_op jit(solution)/shard_map/pallas_call | solution.py:184
  154.9 6.0 %shard_map.68 = bf16[32,192,192]{2,1,0:T(8,128)(2,1)S(1)} custom-call(s32[2,32]{1,0:T(2,128)S(1)} %bitcast.35, s32[32]{0:T(128)S(1)} %copy-done.25, s32[4]{0:T(128)S(1)} %pad_add_fusion.at_ref, bf16[32,192,192]{2,1,0:T(8,128)(2,1)S(1)} %reshape.19.s_ref, bf16[32,4,72,128]{3,2,1,0:T(8,128)(2,1)S(1)} %shard_map.65.own_ref, ...), custom_call_target="tpu_custom_call" | custom-call | flops 905969664 | bytes 1048576 | tf_op jit(solution)/shard_map/pallas_call | solution.py:233
  162.5 6.2 %reshape.22 = bf16[32,36864]{1,0:T(8,128)(2,1)} reshape(bf16[32,192,192]{2,1,0:T(8,128)(2,1)} %copy-done.2) | data formatting | bytes 4718592 | tf_op jit(solution)/shard_map/reshape | solution.py:289
  (151 shorter events, 60.9 us)
Async XLA Ops:
  28.0 32.5 %collective-permute-start.14 = (bf16[4,8,72,128]{3,2,1,0:T(8,128)(2,1)}, bf16[4,8,72,128]{3,2,1,0:T(8,128)(2,1)}, u32[]{:S(2)}, u32[]{:S(2)}) collective-permute-start(bf16[4,8,72,128]{3,2,1,0:T(8,128)(2,1)} %get-tuple-element.16), channel_id=1, source_target_pairs={{0,32},{1,33},{2,34},{3,35},{4,36},{5,37},{6,38},{7,39},{8,40},{9,... | collective-permute-start | bytes 1769480 | tf_op jit(solution)/shard_map/ppermute | solution.py:51
  31.7 28.8 %collective-permute-start.16 = (bf16[4,8,72,128]{3,2,1,0:T(8,128)(2,1)}, bf16[4,8,72,128]{3,2,1,0:T(8,128)(2,1)}, u32[]{:S(2)}, u32[]{:S(2)}) collective-permute-start(bf16[4,8,72,128]{3,2,1,0:T(8,128)(2,1)} %add_convert_fusion.3), channel_id=1, source_target_pairs={{0,128},{1,129},{2,130},{3,131},{4,132},{5,133},{6,134},{7,135},{8... | collective-permute-start | bytes 1769480 | tf_op jit(solution)/shard_map/ppermute | solution.py:35
  35.0 25.5 %collective-permute-start.18 = (bf16[4,8,72,128]{3,2,1,0:T(8,128)(2,1)}, bf16[4,8,72,128]{3,2,1,0:T(8,128)(2,1)}, u32[]{:S(2)}, u32[]{:S(2)}) collective-permute-start(bf16[4,8,72,128]{3,2,1,0:T(8,128)(2,1)} %add_convert_fusion.2), channel_id=1, source_target_pairs={{0,64},{1,65},{2,66},{3,67},{4,68},{5,69},{6,70},{7,71},{8,72},{9,... | collective-permute-start | bytes 1769480 | tf_op jit(solution)/shard_map/ppermute | solution.py:35
  37.5 23.0 %collective-permute-start.20 = (bf16[4,8,72,128]{3,2,1,0:T(8,128)(2,1)}, bf16[4,8,72,128]{3,2,1,0:T(8,128)(2,1)}, u32[]{:S(2)}, u32[]{:S(2)}) collective-permute-start(bf16[4,8,72,128]{3,2,1,0:T(8,128)(2,1)} %add_convert_fusion.1), channel_id=1, source_target_pairs={{0,192},{1,193},{2,194},{3,195},{4,196},{5,197},{6,198},{7,199},{8... | collective-permute-start | bytes 1769480 | tf_op jit(solution)/shard_map/ppermute | solution.py:35
  43.8 9.3 %collective-permute-start.1 = (bf16[4,72,128]{2,1,0:T(8,128)(2,1)S(1)}, bf16[4,72,128]{2,1,0:T(8,128)(2,1)S(1)}, u32[]{:S(2)}, u32[]{:S(2)}) collective-permute-start(bf16[4,72,128]{2,1,0:T(8,128)(2,1)S(1)} %pad_maximum_fusion.3.x0_ref), channel_id=1, source_target_pairs={{0,16},{1,17},{2,18},{3,19},{4,20},{5,21},{6,22},{7,23},{8,24},{9,... | collective-permute-start | bytes 221192 | tf_op jit(solution)/shard_map/ppermute | solution.py:47
  58.5 8.2 %collective-permute-start.3 = (bf16[4,72,128]{2,1,0:T(8,128)(2,1)S(1)}, bf16[4,72,128]{2,1,0:T(8,128)(2,1)S(1)}, u32[]{:S(2)}, u32[]{:S(2)}) collective-permute-start(bf16[4,72,128]{2,1,0:T(8,128)(2,1)S(1)} %pad_maximum_fusion.4), channel_id=1, source_target_pairs={{0,4},{1,5},{2,6},{3,7},{4,0},{5,1},{6,2},{7,3},{8,12},{9,13},{10,... | collective-permute-start | bytes 221192 | tf_op jit(solution)/shard_map/ppermute | solution.py:47
  66.8 7.9 %collective-permute-start.5 = (bf16[8,72,128]{2,1,0:T(8,128)(2,1)S(1)}, bf16[8,72,128]{2,1,0:T(8,128)(2,1)S(1)}, u32[]{:S(2)}, u32[]{:S(2)}) collective-permute-start(bf16[8,72,128]{2,1,0:T(8,128)(2,1)S(1)} %constant_dynamic-update-slice_fusion), channel_id=1, source_target_pairs={{0,2},{1,3},{2,0},{3,1},{4,6},{5,7},{6,4},{7,5},{8,10},{9,11},{10,... | collective-permute-start | bytes 442376 | tf_op jit(solution)/shard_map/ppermute | solution.py:41
  76.4 25.8 %collective-permute-start.7 = (bf16[4,8,72,128]{3,2,1,0:T(8,128)(2,1)S(1)}, bf16[4,8,72,128]{3,2,1,0:T(8,128)(2,1)S(1)}, u32[]{:S(2)}, u32[]{:S(2)}) collective-permute-start(bf16[4,8,72,128]{3,2,1,0:T(8,128)(2,1)S(1)} %pad_maximum_fusion.rest_0_), channel_id=1, source_target_pairs={{0,64},{1,65},{2,66},{3,67},{4,68},{5,69},{6,70},{7,71},{8,72},{9,... | collective-permute-start | bytes 1769480 | tf_op jit(solution)/shard_map/ppermute | solution.py:35
  76.5 29.4 %collective-permute-start.8 = (bf16[4,8,72,128]{3,2,1,0:T(8,128)(2,1)S(1)}, bf16[4,8,72,128]{3,2,1,0:T(8,128)(2,1)S(1)}, u32[]{:S(2)}, u32[]{:S(2)}) collective-permute-start(bf16[4,8,72,128]{3,2,1,0:T(8,128)(2,1)S(1)} %pad_maximum_fusion.rest_0_), channel_id=1, source_target_pairs={{0,128},{1,129},{2,130},{3,131},{4,132},{5,133},{6,134},{7,135},{8... | collective-permute-start | bytes 1769480 | tf_op jit(solution)/shard_map/ppermute | solution.py:35
  80.0 12.5 %collective-permute-start.26 = (bf16[4,72,128]{2,1,0:T(8,128)(2,1)S(1)}, bf16[4,72,128]{2,1,0:T(8,128)(2,1)S(1)}, u32[]{:S(2)}, u32[]{:S(2)}) collective-permute-start(bf16[4,72,128]{2,1,0:T(8,128)(2,1)S(1)} %add_convert_fusion.5.d0_ref), channel_id=1, source_target_pairs={{0,16},{1,17},{2,18},{3,19},{4,20},{5,21},{6,22},{7,23},{8,24},{9,... | collective-permute-start | bytes 221192 | tf_op jit(solution)/shard_map/ppermute | solution.py:47
  84.4 33.2 %collective-permute-start.9 = (bf16[4,8,72,128]{3,2,1,0:T(8,128)(2,1)S(1)}, bf16[4,8,72,128]{3,2,1,0:T(8,128)(2,1)}, u32[]{:S(2)}, u32[]{:S(2)}) collective-permute-start(bf16[4,8,72,128]{3,2,1,0:T(8,128)(2,1)S(1)} %pad_maximum_fusion.rest_0_), channel_id=1, source_target_pairs={{0,192},{1,193},{2,194},{3,195},{4,196},{5,197},{6,198},{7,199},{8... | collective-permute-start | bytes 1769480 | tf_op jit(solution)/shard_map/ppermute | solution.py:35
  85.9 33.5 %collective-permute-start.10 = (bf16[4,8,72,128]{3,2,1,0:T(8,128)(2,1)S(1)}, bf16[4,8,72,128]{3,2,1,0:T(8,128)(2,1)S(1)}, u32[]{:S(2)}, u32[]{:S(2)}) collective-permute-start(bf16[4,8,72,128]{3,2,1,0:T(8,128)(2,1)S(1)} %pad_maximum_fusion.rest_0_), channel_id=1, source_target_pairs={{0,32},{1,33},{2,34},{3,35},{4,36},{5,37},{6,38},{7,39},{8,40},{9,... | collective-permute-start | bytes 1769480 | tf_op jit(solution)/shard_map/ppermute | solution.py:51
  102.3 11.1 %collective-permute-start.30 = (bf16[8,72,128]{2,1,0:T(8,128)(2,1)S(1)}, bf16[8,72,128]{2,1,0:T(8,128)(2,1)S(1)}, u32[]{:S(2)}, u32[]{:S(2)}) collective-permute-start(bf16[8,72,128]{2,1,0:T(8,128)(2,1)S(1)} %get-tuple-element.39), channel_id=1, source_target_pairs={{0,2},{1,3},{2,0},{3,1},{4,6},{5,7},{6,4},{7,5},{8,10},{9,11},{10,... | collective-permute-start | bytes 442376 | tf_op jit(solution)/shard_map/ppermute | solution.py:41
  106.0 9.0 %collective-permute-start.31 = (bf16[8,72,128]{2,1,0:T(8,128)(2,1)S(1)}, bf16[8,72,128]{2,1,0:T(8,128)(2,1)S(1)}, u32[]{:S(2)}, u32[]{:S(2)}) collective-permute-start(bf16[8,72,128]{2,1,0:T(8,128)(2,1)S(1)} %get-tuple-element.39), channel_id=1, source_target_pairs={{0,3},{1,2},{2,1},{3,0},{4,7},{5,6},{6,5},{7,4},{8,11},{9,10},{10,... | collective-permute-start | bytes 442376 | tf_op jit(solution)/shard_map/ppermute | solution.py:41
  106.6 14.3 %collective-permute-start.11 = (bf16[4,8,72,128]{3,2,1,0:T(8,128)(2,1)S(1)}, bf16[4,8,72,128]{3,2,1,0:T(8,128)(2,1)S(1)}, u32[]{:S(2)}, u32[]{:S(2)}) collective-permute-start(bf16[4,8,72,128]{3,2,1,0:T(8,128)(2,1)S(1)} %collective-permute-done.7.rest_1_), channel_id=1, source_target_pairs={{0,32},{1,33},{2,34},{3,35},{4,36},{5,37},{6,38},{7,39},{8,40},{9,... | collective-permute-start | bytes 1769480 | tf_op jit(solution)/shard_map/ppermute | solution.py:51
  113.3 10.5 %collective-permute-start.12 = (bf16[4,8,72,128]{3,2,1,0:T(8,128)(2,1)S(1)}, bf16[4,8,72,128]{3,2,1,0:T(8,128)(2,1)S(1)}, u32[]{:S(2)}, u32[]{:S(2)}) collective-permute-start(bf16[4,8,72,128]{3,2,1,0:T(8,128)(2,1)S(1)} %collective-permute-done.8.rest_2_), channel_id=1, source_target_pairs={{0,32},{1,33},{2,34},{3,35},{4,36},{5,37},{6,38},{7,39},{8,40},{9,... | collective-permute-start | bytes 1769480 | tf_op jit(solution)/shard_map/ppermute | solution.py:51
  115.9 9.6 %collective-permute-start.32 = (bf16[4,8,72,128]{3,2,1,0:T(8,128)(2,1)}, bf16[4,8,72,128]{3,2,1,0:T(8,128)(2,1)}, u32[]{:S(2)}, u32[]{:S(2)}) collective-permute-start(bf16[4,8,72,128]{3,2,1,0:T(8,128)(2,1)} %pad_maximum_fusion.1.rest_0_), channel_id=1, source_target_pairs={{0,64},{1,65},{2,66},{3,67},{4,68},{5,69},{6,70},{7,71},{8,72},{9,... | collective-permute-start | bytes 1769480 | tf_op jit(solution)/shard_map/ppermute | solution.py:35
  117.6 15.8 %collective-permute-start.33 = (bf16[4,8,72,128]{3,2,1,0:T(8,128)(2,1)}, bf16[4,8,72,128]{3,2,1,0:T(8,128)(2,1)}, u32[]{:S(2)}, u32[]{:S(2)}) collective-permute-start(bf16[4,8,72,128]{3,2,1,0:T(8,128)(2,1)} %pad_maximum_fusion.1.rest_0_), channel_id=1, source_target_pairs={{0,128},{1,129},{2,130},{3,131},{4,132},{5,133},{6,134},{7,135},{8... | collective-permute-start | bytes 1769480 | tf_op jit(solution)/shard_map/ppermute | solution.py:35
  120.2 16.8 %collective-permute-start.34 = (bf16[4,8,72,128]{3,2,1,0:T(8,128)(2,1)}, bf16[4,8,72,128]{3,2,1,0:T(8,128)(2,1)}, u32[]{:S(2)}, u32[]{:S(2)}) collective-permute-start(bf16[4,8,72,128]{3,2,1,0:T(8,128)(2,1)} %pad_maximum_fusion.1.rest_0_), channel_id=1, source_target_pairs={{0,192},{1,193},{2,194},{3,195},{4,196},{5,197},{6,198},{7,199},{8... | collective-permute-start | bytes 1769480 | tf_op jit(solution)/shard_map/ppermute | solution.py:35
  121.7 28.0 %collective-permute-start.13 = (bf16[4,8,72,128]{3,2,1,0:T(8,128)(2,1)}, bf16[4,8,72,128]{3,2,1,0:T(8,128)(2,1)}, u32[]{:S(2)}, u32[]{:S(2)}) collective-permute-start(bf16[4,8,72,128]{3,2,1,0:T(8,128)(2,1)} %collective-permute-done.9.rest_3_), channel_id=1, source_target_pairs={{0,32},{1,33},{2,34},{3,35},{4,36},{5,37},{6,38},{7,39},{8,40},{9,... | collective-permute-start | bytes 1769480 | tf_op jit(solution)/shard_map/ppermute | solution.py:51
  124.6 30.2 %collective-permute-start.35 = (bf16[4,8,72,128]{3,2,1,0:T(8,128)(2,1)}, bf16[4,8,72,128]{3,2,1,0:T(8,128)(2,1)}, u32[]{:S(2)}, u32[]{:S(2)}) collective-permute-start(bf16[4,8,72,128]{3,2,1,0:T(8,128)(2,1)} %pad_maximum_fusion.1.rest_0_), channel_id=1, source_target_pairs={{0,32},{1,33},{2,34},{3,35},{4,36},{5,37},{6,38},{7,39},{8,40},{9,... | collective-permute-start | bytes 1769480 | tf_op jit(solution)/shard_map/ppermute | solution.py:51
  125.5 29.4 %collective-permute-start.36 = (bf16[4,8,72,128]{3,2,1,0:T(8,128)(2,1)}, bf16[4,8,72,128]{3,2,1,0:T(8,128)(2,1)}, u32[]{:S(2)}, u32[]{:S(2)}) collective-permute-start(bf16[4,8,72,128]{3,2,1,0:T(8,128)(2,1)} %collective-permute-done.32.rest_1_), channel_id=1, source_target_pairs={{0,32},{1,33},{2,34},{3,35},{4,36},{5,37},{6,38},{7,39},{8,40},{9,... | collective-permute-start | bytes 1769480 | tf_op jit(solution)/shard_map/ppermute | solution.py:51
  133.4 21.5 %collective-permute-start.37 = (bf16[4,8,72,128]{3,2,1,0:T(8,128)(2,1)}, bf16[4,8,72,128]{3,2,1,0:T(8,128)(2,1)}, u32[]{:S(2)}, u32[]{:S(2)}) collective-permute-start(bf16[4,8,72,128]{3,2,1,0:T(8,128)(2,1)} %collective-permute-done.33.rest_2_), channel_id=1, source_target_pairs={{0,32},{1,33},{2,34},{3,35},{4,36},{5,37},{6,38},{7,39},{8,40},{9,... | collective-permute-start | bytes 1769480 | tf_op jit(solution)/shard_map/ppermute | solution.py:51
  137.1 17.8 %collective-permute-start.38 = (bf16[4,8,72,128]{3,2,1,0:T(8,128)(2,1)}, bf16[4,8,72,128]{3,2,1,0:T(8,128)(2,1)}, u32[]{:S(2)}, u32[]{:S(2)}) collective-permute-start(bf16[4,8,72,128]{3,2,1,0:T(8,128)(2,1)} %collective-permute-done.34.rest_3_), channel_id=1, source_target_pairs={{0,32},{1,33},{2,34},{3,35},{4,36},{5,37},{6,38},{7,39},{8,40},{9,... | collective-permute-start | bytes 1769480 | tf_op jit(solution)/shard_map/ppermute | solution.py:51
  (42 other events, 226.7 us)
where the time goes:
time: 169 us
  starting transfers between devices  68.5 us (41%)
  local copies, waits for them, and re-layouts  39.5 us (23%)
  waiting for transfers between devices  30.9 us (18%)
  Pallas kernels  19.5 us (12%)
  other arithmetic  9.95 us (6%)
    ppermute x12, starting transfers between devices, stage_c(): lax.ppermute(array, AXES, pairs_of(lambda x, c, z, y: (x, c ^ 1, z, y)))  23.3 us
    ppermute x9, starting transfers between devices, stage_z(): lax.ppermute(array, AXES, pairs_of(lambda x, c, z, y: (x, c, z ^ d, y)))  22.1 us
    unnamed x58, local copies, waits for them, and re-layouts  15.3 us
    ppermute x9, waiting for transfers between devices, stage_z(): lax.ppermute(array, AXES, pairs_of(lambda x, c, z, y: (x, c, z ^ d, y)))  14.2 us
    ppermute x9, starting transfers between devices, stage_b(): lax.ppermute(array, AXES, pairs_of(lambda x, c, z, y: (x, c, z, y ^ d) if...  11.8 us
    ppermute x9, starting transfers between devices, stage_a(): lax.ppermute(array, AXES, pairs_of(lambda x, c, z, y: (x ^ d, c, z, y) if...  11.2 us
    ppermute x9, waiting for transfers between devices, stage_a(): lax.ppermute(array, AXES, pairs_of(lambda x, c, z, y: (x ^ d, c, z, y) if...  10.3 us
    convert_element_type x6, other arithmetic, added(): return total.astype(BF16)  8.69 us
  transfers between devices with their start and end apart: 39, of which 13 were waited for; matrix products, arithmetic and copies ran while one was open for 10% of the time, Pallas kernels for 4%

commit v1 on v0

--- a/solution.py
+++ b/solution.py
@@ -10,6 +10,7 @@
 R = 192
 Q = 48
 QP = 72
+CHUNKS = R * R // 128
 STEP = 8
 AXES = ("gx_0", "gx_1", "gy", "gz")
 GX_GY = ("gx_0", "gx_1", "gy")
@@ -82,7 +83,7 @@
     return lax.dot_general(a, b, (dims, ((), ())), preferred_element_type=F32)
 
 
-VLIM = 20
+VLIM = 14
 
 SMEM = pl.BlockSpec(memory_space=pltpu.SMEM)
 VMEM = pl.BlockSpec(memory_space=pltpu.VMEM)
@@ -108,6 +109,60 @@
         return _
 
     lax.fori_loop(0, pairs // STEP, step, 0)
+
+
+def relay_kernel(x_ref, o_ref, flat_ref, left_ref, right_ref):
+    low = lax.broadcasted_iota(jnp.int32, (R // 2, 128), 1) < 64
+
+    def work(g, _):
+        rows = pl.ds(pl.multiple_of(g * 8, 8), 8)
+        for j in range(CHUNKS):
+            flat_ref[j * 8 : j * 8 + 8] = x_ref[rows, j * 128 : j * 128 + 128].astype(F32)
+        for i in range(8):
+            first, second, third = (
+                flat_ref[pl.ds(n * 8 + i, R // 2, stride=24), :] for n in range(3)
+            )
+            second_turned, third_turned = pltpu.roll(second, 64, 1), pltpu.roll(third, 64, 1)
+            left_ref[i, pl.ds(0, R // 2, stride=2), :] = first
+            right_ref[i, pl.ds(0, R // 2, stride=2), :] = second
+            left_ref[i, pl.ds(1, R // 2, stride=2), :] = jnp.where(low, second_turned, third_turned)
+            right_ref[i, pl.ds(1, R // 2, stride=2), :] = third_turned
+            o_ref[g * 8 + i, :, :128] = left_ref[i].astype(BF16)
+            o_ref[g * 8 + i, :, 128:] = right_ref[i][:, :64].astype(BF16)
+        return _
+
+    lax.fori_loop(0, x_ref.shape[0] // 8, work, 0)
+
+
+def relay(x):
+    pairs = x.shape[0]
+    return call(
+        relay_kernel,
+        0,
+        1,
+        jax.ShapeDtypeStruct((pairs, R, R), BF16),
+        [
+            pltpu.VMEM((CHUNKS * 8, 128), F32),
+            pltpu.VMEM((8, R, 128), F32),
+            pltpu.VMEM((8, R, 128), F32),
+        ],
+        1 << 24,
+        VLIM,
+    )(x)
+
+
+def lay_out(block, i, flat_ref, left_ref, right_ref):
+    low = lax.broadcasted_iota(jnp.int32, (R // 2, 128), 1) < 64
+    left_ref[i] = block[:, :128]
+    right_ref[i, :, :64] = block[:, 128:]
+    even = pl.ds(0, R // 2, stride=2)
+    odd = pl.ds(1, R // 2, stride=2)
+    turned = pltpu.roll(left_ref[i, odd, :], 64, 1)
+    flat_ref[pl.ds(i, R // 2, stride=24), :] = left_ref[i, even, :]
+    flat_ref[pl.ds(8 + i, R // 2, stride=24), :] = jnp.where(low, right_ref[i, even, :], turned)
+    flat_ref[pl.ds(16 + i, R // 2, stride=24), :] = jnp.where(
+        low, turned, pltpu.roll(right_ref[i, odd, :], 64, 1)
+    )
 
 
 def project_kernel(ends_ref, rank_ref, at_ref, s_ref, m_ref, p_ref, *rest):
@@ -210,22 +265,30 @@
 
 def finish_kernel(ends_ref, rank_ref, at_ref, s_ref, own_ref, base_ref, *rest):
     group_refs, out_ref, held_ref = rest[:8], rest[8], rest[9]
+    flat_ref, left_ref, right_ref = rest[10:]
     for n in range(8):
         held_ref[n * 32 : (n + 1) * 32] = group_refs[n][...].reshape(32, QP, 128)
-
-    def work(pair):
-        quarters = []
-        for q in range(4):
-            first = held_ref[slot_of(ends_ref[0, pair], q, at_ref)].astype(F32)
-            second = held_ref[slot_of(ends_ref[1, pair], q, at_ref)].astype(F32)
-            quarters.append(unpacked_quarter((first + second) - own_ref[pair, q].astype(F32)))
-        combined = jnp.concatenate(quarters, axis=0).astype(BF16)
-        half = dot(s_ref[pair], combined, ((0,), (0,))).astype(BF16)
-        total = base_ref[pair] + dot(half, s_ref[pair], ((1,), (0,)))
-        inside = masks((rank_ref[pair] + 1) * RSTEP)
-        out_ref[pair] = jnp.where(inside, total, 0.0).astype(BF16)
-
-    each_pair(s_ref.shape[0], work)
+    right_ref[...] = jnp.zeros_like(right_ref)
+
+    def work(g, _):
+        for i in range(8):
+            pair = g * 8 + i
+            quarters = []
+            for q in range(4):
+                first = held_ref[slot_of(ends_ref[0, pair], q, at_ref)].astype(F32)
+                second = held_ref[slot_of(ends_ref[1, pair], q, at_ref)].astype(F32)
+                quarters.append(unpacked_quarter((first + second) - own_ref[pair, q].astype(F32)))
+            combined = jnp.concatenate(quarters, axis=0).astype(BF16)
+            half = dot(s_ref[pair], combined, ((0,), (0,))).astype(BF16)
+            total = base_ref[pair] + dot(half, s_ref[pair], ((1,), (0,)))
+            inside = masks((rank_ref[pair] + 1) * RSTEP)
+            lay_out(jnp.where(inside, total, 0.0), i, flat_ref, left_ref, right_ref)
+        rows = pl.ds(pl.multiple_of(g * 8, 8), 8)
+        for j in range(CHUNKS):
+            out_ref[rows, j * 128 : j * 128 + 128] = flat_ref[j * 8 : j * 8 + 8].astype(BF16)
+        return _
+
+    lax.fori_loop(0, s_ref.shape[0] // 8, work, 0)
 
 
 def finish(ends, rank, at, s, own, base, groups):
@@ -234,8 +297,13 @@
         finish_kernel,
         3,
         11,
-        jax.ShapeDtypeStruct((pairs, R, R), BF16),
-        [pltpu.VMEM((256, QP, 128), BF16)],
+        jax.ShapeDtypeStruct((pairs, R * R), BF16),
+        [
+            pltpu.VMEM((256, QP, 128), BF16),
+            pltpu.VMEM((CHUNKS * 8, 128), F32),
+            pltpu.VMEM((8, R, 128), F32),
+            pltpu.VMEM((8, R, 128), F32),
+        ],
         pairs * 4 * R**3,
         VLIM,
     )(ends, rank, at, s, own, base, *groups)
@@ -258,7 +326,6 @@
 
 
 def whole_step(pair_list, rank_bucket, amplitudes, intersects, integrals, exchange_blocks):
-    pairs = amplitudes.shape[0]
     at = jnp.stack([lax.axis_index(a) for a in AXES]).astype(jnp.int32)
     y = lax.axis_index("gz")
     ends = pair_list.T
@@ -270,10 +337,10 @@
     quarters = jnp.concatenate(quarters, axis=0)
     blocks = sent_to_all(quarters)
 
-    m = amplitudes.reshape(pairs, R, R)
-    s = intersects.reshape(pairs, R, R)
+    m = relay(amplitudes)
+    s = relay(intersects)
     p, *sums = project(ends, rank_bucket, at, s, m)
-    v = integrals.reshape(pairs, R, R)
+    v = relay(integrals)
     base = base_of(rank_bucket, m, v)
 
     sums = [added(sums[a], stage_c(sums[4 + a])) for a in (2, 1, 3, 0)]
@@ -285,8 +352,7 @@
     coupled = couple(parts, near)
     own = own_of(ends, at, p, blocks)
     groups = sent_to_all(coupled)
-    out = finish(ends, rank_bucket, at, s, own, base, groups)
-    return out.reshape(pairs, R * R)
+    return finish(ends, rank_bucket, at, s, own, base, groups)
 
 
 def solution(mesh):

time: 169 us -> 143 us (0.85)
  local copies, waits for them, and re-layouts: 39.5 us -> 7.59 us
  Pallas kernels: 19.5 us -> 25.3 us
    reshape x4 -> x0, local copies, waits for them, and re-layouts: 23.3 us -> none  [the longest x1 6.17 us: whole_step(): return out.reshape(pairs, R * R)]
    unnamed x58 -> x36, local copies, waits for them, and re-layouts: 15.3 us -> 6.73 us
    pallas_call x1 -> x4, Pallas kernels: 5.98 us -> 12.5 us  [the longest x1 6.69 us: finish(): call(finish_kernel, 3, 11, jax.ShapeDtypeStruct((pairs, R * R), BF16), [p...]
  transfers between devices with their start and end apart: 39 -> 39, of which waited for: 13 -> 13; matrix products, arithmetic and copies ran while one was open for 10% -> 7% of each run, Pallas kernels for 4% -> 6%
where the time goes in v1:
time: 143 us
  starting transfers between devices  68.9 us (48%)
  waiting for transfers between devices  31.9 us (22%)
  Pallas kernels  25.3 us (18%)
  other arithmetic  9.05 us (6%)
  local copies, waits for them, and re-layouts  7.59 us (5%)
    ppermute x12, starting transfers between devices, stage_c(): lax.ppermute(array, AXES, pairs_of(lambda x, c, z, y: (x, c ^ 1, z, y)))  23.6 us
    ppermute x9, starting transfers between devices, stage_z(): lax.ppermute(array, AXES, pairs_of(lambda x, c, z, y: (x, c, z ^ d, y)))  22.1 us
    ppermute x9, waiting for transfers between devices, stage_z(): lax.ppermute(array, AXES, pairs_of(lambda x, c, z, y: (x, c, z ^ d, y)))  14 us
    ppermute x9, starting transfers between devices, stage_b(): lax.ppermute(array, AXES, pairs_of(lambda x, c, z, y: (x, c, z, y ^ d) if...  11.8 us
    ppermute x9, waiting for transfers between devices, stage_a(): lax.ppermute(array, AXES, pairs_of(lambda x, c, z, y: (x ^ d, c, z, y) if...  11.5 us
    ppermute x9, starting transfers between devices, stage_a(): lax.ppermute(array, AXES, pairs_of(lambda x, c, z, y: (x ^ d, c, z, y) if...  11.3 us
    convert_element_type x6, other arithmetic, added(): return total.astype(BF16)  8.61 us
    unnamed x36, local copies, waits for them, and re-layouts  6.73 us
  transfers between devices with their start and end apart: 39, of which 13 were waited for; matrix products, arithmetic and copies ran while one was open for 7% of the time, Pallas kernels for 6%

profile of v1, /device:TPU:1, one launch (start us, length us, event | category | flops | bytes accessed | tf_op | source)
XLA Modules:
  0.0 143.0 jit_solution(2109592020233364986)
XLA Ops:
  5.7 6.3 %shard_map.66 = (bf16[32,192,192]{2,1,0:T(8,128)(2,1)S(1)}, bf16[4,8,72,128]{3,2,1,0:T(8,128)(2,1)S(1)}, bf16[4,8,72,128]{3,2,1,0:T(8,128)(2,1)S(1)}, bf16[4,8,7...) custom-call(s32[2,32]{1,0:T(2,128)S(1)} %bitcast.33, ...), custom_call_target="tpu_custom_call" | custom-call | flops 905969664 | bytes 1048576 | tf_op jit(solution)/shard_map/pallas_call | solution.py:191
  16.9 3.2 %collective-permute-start.15 = (bf16[4,8,72,128]{3,2,1,0:T(8,128)(2,1)}, bf16[4,8,72,128]{3,2,1,0:T(8,128)(2,1)}, u32[]{:S(2)}, u32[]{:S(2)}) collective-permute-start(bf16[4,8,72,128]{3,2,1,0:T(8,128)(2,1)} %get-tuple-element.18), channel_id=1, source_target_pairs={{0,32},{1,33},{2,34},{3,35},{4,36},{5,37},{6,38},{7,39},{8,40},{9,... | collective-permute-start | bytes 1769480 | tf_op jit(solution)/shard_map/ppermute | solution.py:52
  22.1 2.2 %add_convert_fusion.3 = bf16[4,8,72,128]{3,2,1,0:T(8,128)(2,1)} fusion(bf16[4,8,72,128]{3,2,1,0:T(8,128)(2,1)} %collective-permute-done.15, bf16[4,8,72,128]{3,2,1,0:T(8,128)(2,1)} %copy-done.12), kind=kLoop, calls=%fused_computation.3 | loop fusion | flops 1179648 | bytes 1769472 | tf_op jit(solution)/shard_map/convert_element_type | solution.py:316
  33.5 2.8 %collective-permute-done.x1_ref = bf16[4,72,128]{2,1,0:T(8,128)(2,1)S(1)} collective-permute-done((bf16[4,72,128]{2,1,0:T(8,128)(2,1)S(1)}, bf16[4,72,128]{2,1,0:T(8,128)(2,1)S(1)}, u32[]{:S(2)}, u32[]{:S(2)}) %collective-permute-start) | collective-permute-done | bytes 73760 | tf_op jit(solution)/shard_map/ppermute | solution.py:48
  36.3 7.4 %collective-permute-start.1 = (bf16[4,72,128]{2,1,0:T(8,128)(2,1)S(1)}, bf16[4,72,128]{2,1,0:T(8,128)(2,1)S(1)}, u32[]{:S(2)}, u32[]{:S(2)}) collective-permute-start(bf16[4,72,128]{2,1,0:T(8,128)(2,1)S(1)} %pad_maximum_fusion.3.x0_ref), channel_id=1, source_target_pairs={{0,16},{1,17},{2,18},{3,19},{4,20},{5,21},{6,22},{7,23},{8,24},{9,... | collective-permute-start | bytes 221192 | tf_op jit(solution)/shard_map/ppermute | solution.py:48
  45.6 2.3 %collective-permute-start.2 = (bf16[4,72,128]{2,1,0:T(8,128)(2,1)S(1)}, bf16[4,72,128]{2,1,0:T(8,128)(2,1)S(1)}, u32[]{:S(2)}, u32[]{:S(2)}) collective-permute-start(bf16[4,72,128]{2,1,0:T(8,128)(2,1)S(1)} %pad_maximum_fusion.3.x0_ref), channel_id=1, source_target_pairs={{0,24},{1,25},{2,26},{3,27},{4,28},{5,29},{6,30},{7,31},{8,16},{9,... | collective-permute-start | bytes 221192 | tf_op jit(solution)/shard_map/ppermute | solution.py:48
  47.9 3.1 %collective-permute-done.2.x3_ref = bf16[4,72,128]{2,1,0:T(8,128)(2,1)S(1)} collective-permute-done((bf16[4,72,128]{2,1,0:T(8,128)(2,1)S(1)}, bf16[4,72,128]{2,1,0:T(8,128)(2,1)S(1)}, u32[]{:S(2)}, u32[]{:S(2)}) %collective-permute-start.2) | collective-permute-done | bytes 73760 | tf_op jit(solution)/shard_map/ppermute | solution.py:48
  56.5 2.6 %collective-permute-start.22 = (bf16[8,72,128]{2,1,0:T(8,128)(2,1)S(1)}, bf16[8,72,128]{2,1,0:T(8,128)(2,1)S(1)}, u32[]{:S(2)}, u32[]{:S(2)}) collective-permute-start(bf16[8,72,128]{2,1,0:T(8,128)(2,1)S(1)} %get-tuple-element.37), channel_id=1, source_target_pairs={{0,2},{1,3},{2,0},{3,1},{4,6},{5,7},{6,4},{7,5},{8,10},{9,11},{10,... | collective-permute-start | bytes 442376 | tf_op jit(solution)/shard_map/ppermute | solution.py:42
  59.3 3.7 %collective-permute-start.5 = (bf16[8,72,128]{2,1,0:T(8,128)(2,1)S(1)}, bf16[8,72,128]{2,1,0:T(8,128)(2,1)S(1)}, u32[]{:S(2)}, u32[]{:S(2)}) collective-permute-start(bf16[8,72,128]{2,1,0:T(8,128)(2,1)S(1)} %constant_dynamic-update-slice_fusion), channel_id=1, source_target_pairs={{0,2},{1,3},{2,0},{3,1},{4,6},{5,7},{6,4},{7,5},{8,10},{9,11},{10,... | collective-permute-start | bytes 442376 | tf_op jit(solution)/shard_map/ppermute | solution.py:42
  64.9 2.3 %collective-permute-done.5 = bf16[8,72,128]{2,1,0:T(8,128)(2,1)S(1)} collective-permute-done((bf16[8,72,128]{2,1,0:T(8,128)(2,1)S(1)}, bf16[8,72,128]{2,1,0:T(8,128)(2,1)S(1)}, u32[]{:S(2)}, u32[]{:S(2)}) %collective-permute-start.5) | collective-permute-done | bytes 147488 | tf_op jit(solution)/shard_map/ppermute | solution.py:42
  69.1 2.2 %collective-permute-start.8 = (bf16[4,8,72,128]{3,2,1,0:T(8,128)(2,1)S(1)}, bf16[4,8,72,128]{3,2,1,0:T(8,128)(2,1)S(1)}, u32[]{:S(2)}, u32[]{:S(2)}) collective-permute-start(bf16[4,8,72,128]{3,2,1,0:T(8,128)(2,1)S(1)} %pad_maximum_fusion.rest_0_), channel_id=1, source_target_pairs={{0,128},{1,129},{2,130},{3,131},{4,132},{5,133},{6,134},{7,135},{8... | collective-permute-start | bytes 1769480 | tf_op jit(solution)/shard_map/ppermute | solution.py:36
  72.5 4.4 %collective-permute-start.26 = (bf16[4,72,128]{2,1,0:T(8,128)(2,1)S(1)}, bf16[4,72,128]{2,1,0:T(8,128)(2,1)S(1)}, u32[]{:S(2)}, u32[]{:S(2)}) collective-permute-start(bf16[4,72,128]{2,1,0:T(8,128)(2,1)S(1)} %add_convert_fusion.5.d0_ref), channel_id=1, source_target_pairs={{0,16},{1,17},{2,18},{3,19},{4,20},{5,21},{6,22},{7,23},{8,24},{9,... | collective-permute-start | bytes 221192 | tf_op jit(solution)/shard_map/ppermute | solution.py:48
  78.4 6.6 %collective-permute-start.10 = (bf16[4,8,72,128]{3,2,1,0:T(8,128)(2,1)S(1)}, bf16[4,8,72,128]{3,2,1,0:T(8,128)(2,1)S(1)}, u32[]{:S(2)}, u32[]{:S(2)}) collective-permute-start(bf16[4,8,72,128]{3,2,1,0:T(8,128)(2,1)S(1)} %pad_maximum_fusion.rest_0_), channel_id=1, source_target_pairs={{0,32},{1,33},{2,34},{3,35},{4,36},{5,37},{6,38},{7,39},{8,40},{9,... | collective-permute-start | bytes 1769480 | tf_op jit(solution)/shard_map/ppermute | solution.py:52
  85.0 2.5 %collective-permute-start.27 = (bf16[4,72,128]{2,1,0:T(8,128)(2,1)S(1)}, bf16[4,72,128]{2,1,0:T(8,128)(2,1)S(1)}, u32[]{:S(2)}, u32[]{:S(2)}) collective-permute-start(bf16[4,72,128]{2,1,0:T(8,128)(2,1)S(1)} %add_convert_fusion.5.d0_ref), channel_id=1, source_target_pairs={{0,24},{1,25},{2,26},{3,27},{4,28},{5,29},{6,30},{7,31},{8,16},{9,... | collective-permute-start | bytes 221192 | tf_op jit(solution)/shard_map/ppermute | solution.py:48
  87.5 3.1 %collective-permute-done.27.d3_ref = bf16[4,72,128]{2,1,0:T(8,128)(2,1)S(1)} collective-permute-done((bf16[4,72,128]{2,1,0:T(8,128)(2,1)S(1)}, bf16[4,72,128]{2,1,0:T(8,128)(2,1)S(1)}, u32[]{:S(2)}, u32[]{:S(2)}) %collective-permute-start.27) | collective-permute-done | bytes 73760 | tf_op jit(solution)/shard_map/ppermute | solution.py:48
  91.3 3.2 %collective-permute-done.28 = bf16[4,72,128]{2,1,0:T(8,128)(2,1)S(1)} collective-permute-done((bf16[4,72,128]{2,1,0:T(8,128)(2,1)S(1)}, bf16[4,72,128]{2,1,0:T(8,128)(2,1)S(1)}, u32[]{:S(2)}, u32[]{:S(2)}) %collective-permute-start.28) | collective-permute-done | bytes 73760 | tf_op jit(solution)/shard_map/ppermute | solution.py:48
  94.7 3.7 %collective-permute-start.30 = (bf16[8,72,128]{2,1,0:T(8,128)(2,1)S(1)}, bf16[8,72,128]{2,1,0:T(8,128)(2,1)S(1)}, u32[]{:S(2)}, u32[]{:S(2)}) collective-permute-start(bf16[8,72,128]{2,1,0:T(8,128)(2,1)S(1)} %get-tuple-element.39), channel_id=1, source_target_pairs={{0,2},{1,3},{2,0},{3,1},{4,6},{5,7},{6,4},{7,5},{8,10},{9,11},{10,... | collective-permute-start | bytes 442376 | tf_op jit(solution)/shard_map/ppermute | solution.py:42
  98.9 6.9 %collective-permute-start.11 = (bf16[4,8,72,128]{3,2,1,0:T(8,128)(2,1)S(1)}, bf16[4,8,72,128]{3,2,1,0:T(8,128)(2,1)S(1)}, u32[]{:S(2)}, u32[]{:S(2)}) collective-permute-start(bf16[4,8,72,128]{3,2,1,0:T(8,128)(2,1)S(1)} %collective-permute-done.7.rest_1_), channel_id=1, source_target_pairs={{0,32},{1,33},{2,34},{3,35},{4,36},{5,37},{6,38},{7,39},{8,40},{9,... | collective-permute-start | bytes 1769480 | tf_op jit(solution)/shard_map/ppermute | solution.py:52
  114.0 2.9 %collective-permute-done.32.rest_1_ = bf16[4,8,72,128]{3,2,1,0:T(8,128)(2,1)S(1)} collective-permute-done((bf16[4,8,72,128]{3,2,1,0:T(8,128)(2,1)S(1)}, bf16[4,8,72,128]{3,2,1,0:T(8,128)(2,1)S(1)}, u32[]{:S(2)}, u32[]{:S(2)}) %collective-permute-start.32) | collective-permute-done | bytes 589856 | tf_op jit(solution)/shard_map/ppermute | solution.py:36
  119.1 5.8 %collective-permute-done.33.rest_2_ = bf16[4,8,72,128]{3,2,1,0:T(8,128)(2,1)S(1)} collective-permute-done((bf16[4,8,72,128]{3,2,1,0:T(8,128)(2,1)S(1)}, bf16[4,8,72,128]{3,2,1,0:T(8,128)(2,1)S(1)}, u32[]{:S(2)}, u32[]{:S(2)}) %collective-permute-start.33) | collective-permute-done | bytes 589856 | tf_op jit(solution)/shard_map/ppermute | solution.py:36
  124.9 2.8 %collective-permute-done.34.rest_3_ = bf16[4,8,72,128]{3,2,1,0:T(8,128)(2,1)S(1)} collective-permute-done((bf16[4,8,72,128]{3,2,1,0:T(8,128)(2,1)S(1)}, bf16[4,8,72,128]{3,2,1,0:T(8,128)(2,1)S(1)}, u32[]{:S(2)}, u32[]{:S(2)}) %collective-permute-start.34) | collective-permute-done | bytes 589856 | tf_op jit(solution)/shard_map/ppermute | solution.py:36
  130.1 2.3 %shard_map.69.base_ref = f32[32,192,192]{2,1,0:T(8,128)S(1)} custom-call(s32[32]{0:T(128)S(1)} %copy-done.14, bf16[32,192,192]{2,1,0:T(8,128)(2,1)S(1)} %copy-done.1, bf16[32,192,192]{2,1,0:T(8,128)(2,1)S(1)} %shard_map.68.v_ref), custom_call_target="tpu_custom_call" | custom-call | flops 452984832 | bytes 1048576 | tf_op jit(solution)/shard_map/pallas_call | solution.py:213
  132.4 3.9 %shard_map.67.own_ref = bf16[32,4,72,128]{3,2,1,0:T(8,128)(2,1)S(1)} custom-call(s32[2,32]{1,0:T(2,128)S(1)} %bitcast.34, s32[4]{0:T(128)S(1)} %pad_add_fusion.at_ref, bf16[32,192,192]{2,1,0:T(8,128)(2,1)S(1)} %copy-done.3, bf16[4,8,72,128]{3,2,1,0:T(8,128)(2,1)S(1)} %pad_maximum_fusion.rest_0_, bf16[4,8,72,128]{3,2,1,0:T(8,128)(2,1)S(1)} %collective-permute-done.7.rest_1_, ...), custom_call_target="tpu_custom_call" | custom-call | flops 452984832 | bytes 1048576 | tf_op jit(solution)/shard_map/pallas_call | solution.py:239
  136.3 6.7 %shard_map.71 = bf16[32,36864]{1,0:T(8,128)(2,1)} custom-call(s32[2,32]{1,0:T(2,128)S(1)} %bitcast.35, s32[32]{0:T(128)S(1)} %copy-done.14, s32[4]{0:T(128)S(1)} %pad_add_fusion.at_ref, bf16[32,192,192]{2,1,0:T(8,128)(2,1)S(1)} %shard_map.64.s_ref, bf16[32,4,72,128]{3,2,1,0:T(8,128)(2,1)S(1)} %shard_map.67.own_ref, f32[32,192,192]{2,1,0:T(8,128)S(1)} %shard_map.69.base_ref, ...), custom_call_target="tpu_custom_call" | custom-call | flops 905969664 | bytes 1048576 | tf_op jit(solution)/shard_map/pallas_call | solution.py:296
  (128 shorter events, 49.8 us)
Async XLA Ops:
  20.6 32.4 %collective-permute-start.14 = (bf16[4,8,72,128]{3,2,1,0:T(8,128)(2,1)}, bf16[4,8,72,128]{3,2,1,0:T(8,128)(2,1)}, u32[]{:S(2)}, u32[]{:S(2)}) collective-permute-start(bf16[4,8,72,128]{3,2,1,0:T(8,128)(2,1)} %get-tuple-element.16), channel_id=1, source_target_pairs={{0,32},{1,33},{2,34},{3,35},{4,36},{5,37},{6,38},{7,39},{8,40},{9,... | collective-permute-start | bytes 1769480 | tf_op jit(solution)/shard_map/ppermute | solution.py:52
  24.3 28.7 %collective-permute-start.16 = (bf16[4,8,72,128]{3,2,1,0:T(8,128)(2,1)}, bf16[4,8,72,128]{3,2,1,0:T(8,128)(2,1)}, u32[]{:S(2)}, u32[]{:S(2)}) collective-permute-start(bf16[4,8,72,128]{3,2,1,0:T(8,128)(2,1)} %add_convert_fusion.3), channel_id=1, source_target_pairs={{0,128},{1,129},{2,130},{3,131},{4,132},{5,133},{6,134},{7,135},{8... | collective-permute-start | bytes 1769480 | tf_op jit(solution)/shard_map/ppermute | solution.py:36
  27.6 25.5 %collective-permute-start.18 = (bf16[4,8,72,128]{3,2,1,0:T(8,128)(2,1)}, bf16[4,8,72,128]{3,2,1,0:T(8,128)(2,1)}, u32[]{:S(2)}, u32[]{:S(2)}) collective-permute-start(bf16[4,8,72,128]{3,2,1,0:T(8,128)(2,1)} %add_convert_fusion.2), channel_id=1, source_target_pairs={{0,64},{1,65},{2,66},{3,67},{4,68},{5,69},{6,70},{7,71},{8,72},{9,... | collective-permute-start | bytes 1769480 | tf_op jit(solution)/shard_map/ppermute | solution.py:36
  30.1 23.0 %collective-permute-start.20 = (bf16[4,8,72,128]{3,2,1,0:T(8,128)(2,1)}, bf16[4,8,72,128]{3,2,1,0:T(8,128)(2,1)}, u32[]{:S(2)}, u32[]{:S(2)}) collective-permute-start(bf16[4,8,72,128]{3,2,1,0:T(8,128)(2,1)} %add_convert_fusion.1), channel_id=1, source_target_pairs={{0,192},{1,193},{2,194},{3,195},{4,196},{5,197},{6,198},{7,199},{8... | collective-permute-start | bytes 1769480 | tf_op jit(solution)/shard_map/ppermute | solution.py:36
  36.3 9.3 %collective-permute-start.1 = (bf16[4,72,128]{2,1,0:T(8,128)(2,1)S(1)}, bf16[4,72,128]{2,1,0:T(8,128)(2,1)S(1)}, u32[]{:S(2)}, u32[]{:S(2)}) collective-permute-start(bf16[4,72,128]{2,1,0:T(8,128)(2,1)S(1)} %pad_maximum_fusion.3.x0_ref), channel_id=1, source_target_pairs={{0,16},{1,17},{2,18},{3,19},{4,20},{5,21},{6,22},{7,23},{8,24},{9,... | collective-permute-start | bytes 221192 | tf_op jit(solution)/shard_map/ppermute | solution.py:48
  51.0 8.2 %collective-permute-start.3 = (bf16[4,72,128]{2,1,0:T(8,128)(2,1)S(1)}, bf16[4,72,128]{2,1,0:T(8,128)(2,1)S(1)}, u32[]{:S(2)}, u32[]{:S(2)}) collective-permute-start(bf16[4,72,128]{2,1,0:T(8,128)(2,1)S(1)} %pad_maximum_fusion.4), channel_id=1, source_target_pairs={{0,4},{1,5},{2,6},{3,7},{4,0},{5,1},{6,2},{7,3},{8,12},{9,13},{10,... | collective-permute-start | bytes 221192 | tf_op jit(solution)/shard_map/ppermute | solution.py:48
  59.3 7.9 %collective-permute-start.5 = (bf16[8,72,128]{2,1,0:T(8,128)(2,1)S(1)}, bf16[8,72,128]{2,1,0:T(8,128)(2,1)S(1)}, u32[]{:S(2)}, u32[]{:S(2)}) collective-permute-start(bf16[8,72,128]{2,1,0:T(8,128)(2,1)S(1)} %constant_dynamic-update-slice_fusion), channel_id=1, source_target_pairs={{0,2},{1,3},{2,0},{3,1},{4,6},{5,7},{6,4},{7,5},{8,10},{9,11},{10,... | collective-permute-start | bytes 442376 | tf_op jit(solution)/shard_map/ppermute | solution.py:42
  69.0 25.7 %collective-permute-start.7 = (bf16[4,8,72,128]{3,2,1,0:T(8,128)(2,1)S(1)}, bf16[4,8,72,128]{3,2,1,0:T(8,128)(2,1)S(1)}, u32[]{:S(2)}, u32[]{:S(2)}) collective-permute-start(bf16[4,8,72,128]{3,2,1,0:T(8,128)(2,1)S(1)} %pad_maximum_fusion.rest_0_), channel_id=1, source_target_pairs={{0,64},{1,65},{2,66},{3,67},{4,68},{5,69},{6,70},{7,71},{8,72},{9,... | collective-permute-start | bytes 1769480 | tf_op jit(solution)/shard_map/ppermute | solution.py:36
  69.1 29.3 %collective-permute-start.8 = (bf16[4,8,72,128]{3,2,1,0:T(8,128)(2,1)S(1)}, bf16[4,8,72,128]{3,2,1,0:T(8,128)(2,1)S(1)}, u32[]{:S(2)}, u32[]{:S(2)}) collective-permute-start(bf16[4,8,72,128]{3,2,1,0:T(8,128)(2,1)S(1)} %pad_maximum_fusion.rest_0_), channel_id=1, source_target_pairs={{0,128},{1,129},{2,130},{3,131},{4,132},{5,133},{6,134},{7,135},{8... | collective-permute-start | bytes 1769480 | tf_op jit(solution)/shard_map/ppermute | solution.py:36
  72.5 12.5 %collective-permute-start.26 = (bf16[4,72,128]{2,1,0:T(8,128)(2,1)S(1)}, bf16[4,72,128]{2,1,0:T(8,128)(2,1)S(1)}, u32[]{:S(2)}, u32[]{:S(2)}) collective-permute-start(bf16[4,72,128]{2,1,0:T(8,128)(2,1)S(1)} %add_convert_fusion.5.d0_ref), channel_id=1, source_target_pairs={{0,16},{1,17},{2,18},{3,19},{4,20},{5,21},{6,22},{7,23},{8,24},{9,... | collective-permute-start | bytes 221192 | tf_op jit(solution)/shard_map/ppermute | solution.py:48
  76.9 32.5 %collective-permute-start.9 = (bf16[4,8,72,128]{3,2,1,0:T(8,128)(2,1)S(1)}, bf16[4,8,72,128]{3,2,1,0:T(8,128)(2,1)S(1)}, u32[]{:S(2)}, u32[]{:S(2)}) collective-permute-start(bf16[4,8,72,128]{3,2,1,0:T(8,128)(2,1)S(1)} %pad_maximum_fusion.rest_0_), channel_id=1, source_target_pairs={{0,192},{1,193},{2,194},{3,195},{4,196},{5,197},{6,198},{7,199},{8... | collective-permute-start | bytes 1769480 | tf_op jit(solution)/shard_map/ppermute | solution.py:36
  78.4 32.8 %collective-permute-start.10 = (bf16[4,8,72,128]{3,2,1,0:T(8,128)(2,1)S(1)}, bf16[4,8,72,128]{3,2,1,0:T(8,128)(2,1)S(1)}, u32[]{:S(2)}, u32[]{:S(2)}) collective-permute-start(bf16[4,8,72,128]{3,2,1,0:T(8,128)(2,1)S(1)} %pad_maximum_fusion.rest_0_), channel_id=1, source_target_pairs={{0,32},{1,33},{2,34},{3,35},{4,36},{5,37},{6,38},{7,39},{8,40},{9,... | collective-permute-start | bytes 1769480 | tf_op jit(solution)/shard_map/ppermute | solution.py:52
  94.7 11.2 %collective-permute-start.30 = (bf16[8,72,128]{2,1,0:T(8,128)(2,1)S(1)}, bf16[8,72,128]{2,1,0:T(8,128)(2,1)S(1)}, u32[]{:S(2)}, u32[]{:S(2)}) collective-permute-start(bf16[8,72,128]{2,1,0:T(8,128)(2,1)S(1)} %get-tuple-element.39), channel_id=1, source_target_pairs={{0,2},{1,3},{2,0},{3,1},{4,6},{5,7},{6,4},{7,5},{8,10},{9,11},{10,... | collective-permute-start | bytes 442376 | tf_op jit(solution)/shard_map/ppermute | solution.py:42
  98.4 9.1 %collective-permute-start.31 = (bf16[8,72,128]{2,1,0:T(8,128)(2,1)S(1)}, bf16[8,72,128]{2,1,0:T(8,128)(2,1)S(1)}, u32[]{:S(2)}, u32[]{:S(2)}) collective-permute-start(bf16[8,72,128]{2,1,0:T(8,128)(2,1)S(1)} %get-tuple-element.39), channel_id=1, source_target_pairs={{0,3},{1,2},{2,1},{3,0},{4,7},{5,6},{6,5},{7,4},{8,11},{9,10},{10,... | collective-permute-start | bytes 442376 | tf_op jit(solution)/shard_map/ppermute | solution.py:42
  98.9 13.0 %collective-permute-start.11 = (bf16[4,8,72,128]{3,2,1,0:T(8,128)(2,1)S(1)}, bf16[4,8,72,128]{3,2,1,0:T(8,128)(2,1)S(1)}, u32[]{:S(2)}, u32[]{:S(2)}) collective-permute-start(bf16[4,8,72,128]{3,2,1,0:T(8,128)(2,1)S(1)} %collective-permute-done.7.rest_1_), channel_id=1, source_target_pairs={{0,32},{1,33},{2,34},{3,35},{4,36},{5,37},{6,38},{7,39},{8,40},{9,... | collective-permute-start | bytes 1769480 | tf_op jit(solution)/shard_map/ppermute | solution.py:52
  105.8 8.1 %collective-permute-start.12 = (bf16[4,8,72,128]{3,2,1,0:T(8,128)(2,1)S(1)}, bf16[4,8,72,128]{3,2,1,0:T(8,128)(2,1)S(1)}, u32[]{:S(2)}, u32[]{:S(2)}) collective-permute-start(bf16[4,8,72,128]{3,2,1,0:T(8,128)(2,1)S(1)} %collective-permute-done.8.rest_2_), channel_id=1, source_target_pairs={{0,32},{1,33},{2,34},{3,35},{4,36},{5,37},{6,38},{7,39},{8,40},{9,... | collective-permute-start | bytes 1769480 | tf_op jit(solution)/shard_map/ppermute | solution.py:52
  107.6 9.3 %collective-permute-start.32 = (bf16[4,8,72,128]{3,2,1,0:T(8,128)(2,1)S(1)}, bf16[4,8,72,128]{3,2,1,0:T(8,128)(2,1)S(1)}, u32[]{:S(2)}, u32[]{:S(2)}) collective-permute-start(bf16[4,8,72,128]{3,2,1,0:T(8,128)(2,1)S(1)} %pad_maximum_fusion.1.rest_0_), channel_id=1, source_target_pairs={{0,64},{1,65},{2,66},{3,67},{4,68},{5,69},{6,70},{7,71},{8,72},{9,... | collective-permute-start | bytes 1769480 | tf_op jit(solution)/shard_map/ppermute | solution.py:36
  109.4 15.5 %collective-permute-start.33 = (bf16[4,8,72,128]{3,2,1,0:T(8,128)(2,1)S(1)}, bf16[4,8,72,128]{3,2,1,0:T(8,128)(2,1)S(1)}, u32[]{:S(2)}, u32[]{:S(2)}) collective-permute-start(bf16[4,8,72,128]{3,2,1,0:T(8,128)(2,1)S(1)} %pad_maximum_fusion.1.rest_0_), channel_id=1, source_target_pairs={{0,128},{1,129},{2,130},{3,131},{4,132},{5,133},{6,134},{7,135},{8... | collective-permute-start | bytes 1769480 | tf_op jit(solution)/shard_map/ppermute | solution.py:36
  111.2 16.5 %collective-permute-start.34 = (bf16[4,8,72,128]{3,2,1,0:T(8,128)(2,1)S(1)}, bf16[4,8,72,128]{3,2,1,0:T(8,128)(2,1)S(1)}, u32[]{:S(2)}, u32[]{:S(2)}) collective-permute-start(bf16[4,8,72,128]{3,2,1,0:T(8,128)(2,1)S(1)} %pad_maximum_fusion.1.rest_0_), channel_id=1, source_target_pairs={{0,192},{1,193},{2,194},{3,195},{4,196},{5,197},{6,198},{7,199},{8... | collective-permute-start | bytes 1769480 | tf_op jit(solution)/shard_map/ppermute | solution.py:36
  111.9 20.5 %collective-permute-start.13 = (bf16[4,8,72,128]{3,2,1,0:T(8,128)(2,1)S(1)}, bf16[4,8,72,128]{3,2,1,0:T(8,128)(2,1)S(1)}, u32[]{:S(2)}, u32[]{:S(2)}) collective-permute-start(bf16[4,8,72,128]{3,2,1,0:T(8,128)(2,1)S(1)} %collective-permute-done.9.rest_3_), channel_id=1, source_target_pairs={{0,32},{1,33},{2,34},{3,35},{4,36},{5,37},{6,38},{7,39},{8,40},{9,... | collective-permute-start | bytes 1769480 | tf_op jit(solution)/shard_map/ppermute | solution.py:52
  113.9 22.4 %collective-permute-start.35 = (bf16[4,8,72,128]{3,2,1,0:T(8,128)(2,1)S(1)}, bf16[4,8,72,128]{3,2,1,0:T(8,128)(2,1)S(1)}, u32[]{:S(2)}, u32[]{:S(2)}) collective-permute-start(bf16[4,8,72,128]{3,2,1,0:T(8,128)(2,1)S(1)} %pad_maximum_fusion.1.rest_0_), channel_id=1, source_target_pairs={{0,32},{1,33},{2,34},{3,35},{4,36},{5,37},{6,38},{7,39},{8,40},{9,... | collective-permute-start | bytes 1769480 | tf_op jit(solution)/shard_map/ppermute | solution.py:52
  116.9 19.4 %collective-permute-start.36 = (bf16[4,8,72,128]{3,2,1,0:T(8,128)(2,1)S(1)}, bf16[4,8,72,128]{3,2,1,0:T(8,128)(2,1)S(1)}, u32[]{:S(2)}, u32[]{:S(2)}) collective-permute-start(bf16[4,8,72,128]{3,2,1,0:T(8,128)(2,1)S(1)} %collective-permute-done.32.rest_1_), channel_id=1, source_target_pairs={{0,32},{1,33},{2,34},{3,35},{4,36},{5,37},{6,38},{7,39},{8,40},{9,... | collective-permute-start | bytes 1769480 | tf_op jit(solution)/shard_map/ppermute | solution.py:52
  124.9 11.5 %collective-permute-start.37 = (bf16[4,8,72,128]{3,2,1,0:T(8,128)(2,1)S(1)}, bf16[4,8,72,128]{3,2,1,0:T(8,128)(2,1)S(1)}, u32[]{:S(2)}, u32[]{:S(2)}) collective-permute-start(bf16[4,8,72,128]{3,2,1,0:T(8,128)(2,1)S(1)} %collective-permute-done.33.rest_2_), channel_id=1, source_target_pairs={{0,32},{1,33},{2,34},{3,35},{4,36},{5,37},{6,38},{7,39},{8,40},{9,... | collective-permute-start | bytes 1769480 | tf_op jit(solution)/shard_map/ppermute | solution.py:52
  127.7 8.6 %collective-permute-start.38 = (bf16[4,8,72,128]{3,2,1,0:T(8,128)(2,1)S(1)}, bf16[4,8,72,128]{3,2,1,0:T(8,128)(2,1)S(1)}, u32[]{:S(2)}, u32[]{:S(2)}) collective-permute-start(bf16[4,8,72,128]{3,2,1,0:T(8,128)(2,1)S(1)} %collective-permute-done.34.rest_3_), channel_id=1, source_target_pairs={{0,32},{1,33},{2,34},{3,35},{4,36},{5,37},{6,38},{7,39},{8,40},{9,... | collective-permute-start | bytes 1769480 | tf_op jit(solution)/shard_map/ppermute | solution.py:52
  (31 other events, 189.9 us)

commit v2 on v1

--- a/solution.py
+++ b/solution.py
@@ -87,17 +87,18 @@
 
 SMEM = pl.BlockSpec(memory_space=pltpu.SMEM)
 VMEM = pl.BlockSpec(memory_space=pltpu.VMEM)
+HBM = pl.BlockSpec(memory_space=pltpu.HBM)
 GROUP = (4, 8, QP, 128)
 
 
-def call(kernel, n_smem, n_vmem, out_shape, scratch, flops, limit_mib):
+def call(kernel, in_specs, out_shape, out_specs, scratch, flops):
     return pl.pallas_call(
         kernel,
-        in_specs=[SMEM] * n_smem + [VMEM] * n_vmem,
-        out_specs=jax.tree.map(lambda _: VMEM, out_shape),
+        in_specs=in_specs,
+        out_specs=out_specs,
         out_shape=out_shape,
         scratch_shapes=scratch,
-        compiler_params=pltpu.CompilerParams(vmem_limit_bytes=limit_mib << 20),
+        compiler_params=pltpu.CompilerParams(vmem_limit_bytes=VLIM << 20),
         cost_estimate=pl.CostEstimate(flops=flops, transcendentals=0, bytes_accessed=1 << 20),
     )
 
@@ -138,17 +139,58 @@
     pairs = x.shape[0]
     return call(
         relay_kernel,
-        0,
-        1,
+        [VMEM],
         jax.ShapeDtypeStruct((pairs, R, R), BF16),
+        VMEM,
         [
             pltpu.VMEM((CHUNKS * 8, 128), F32),
             pltpu.VMEM((8, R, 128), F32),
             pltpu.VMEM((8, R, 128), F32),
         ],
         1 << 24,
-        VLIM,
     )(x)
+
+
+def pack_kernel(x_ref, o_ref, flat_ref, left_ref, right_ref):
+    low = lax.broadcasted_iota(jnp.int32, (R // 2, 128), 1) < 64
+    for j in range(CHUNKS):
+        flat_ref[j : j + 1] = x_ref[:, j * 128 : j * 128 + 128].astype(F32)
+    first, second, third = (flat_ref[pl.ds(n, R // 2, stride=3), :] for n in range(3))
+    second_turned, third_turned = pltpu.roll(second, 64, 1), pltpu.roll(third, 64, 1)
+    left_ref[pl.ds(0, R // 2, stride=2), :] = first
+    right_ref[pl.ds(0, R // 2, stride=2), :] = second
+    left_ref[pl.ds(1, R // 2, stride=2), :] = jnp.where(low, second_turned, third_turned)
+    right_ref[pl.ds(1, R // 2, stride=2), :] = third_turned
+    block = jnp.concatenate([left_ref[...], right_ref[:, :64]], axis=1)
+    for q in range(4):
+        o_ref[q] = packed_quarter(block, q).astype(BF16)
+
+
+def pack(x):
+    return call(
+        pack_kernel,
+        [VMEM],
+        jax.ShapeDtypeStruct((4, QP, 128), BF16),
+        VMEM,
+        [pltpu.VMEM((CHUNKS, 128), F32), pltpu.VMEM((R, 128), F32), pltpu.VMEM((R, 128), F32)],
+        1 << 33,
+    )(x)
+
+
+def choose_kernel(at_ref, *refs):
+    for n in range(4):
+        refs[4][n] = refs[n][at_ref[3]]
+
+
+def choose(at, near):
+    return call(
+        choose_kernel,
+        [SMEM] + [VMEM] * 4,
+        jax.ShapeDtypeStruct((4, QP, 128), BF16),
+        VMEM,
+        [],
+        1 << 20,
+    )(at, *near)
 
 
 def lay_out(block, i, flat_ref, left_ref, right_ref):
@@ -190,12 +232,11 @@
     pairs = s.shape[0]
     return call(
         project_kernel,
-        3,
-        2,
+        [SMEM] * 3 + [VMEM] * 2,
         [jax.ShapeDtypeStruct((pairs, R, R), BF16)] + [jax.ShapeDtypeStruct(GROUP, BF16)] * 8,
+        [VMEM] * 9,
         [pltpu.VMEM((256, QP, 128), BF16)],
         pairs * 4 * R**3,
-        VLIM,
     )(ends, rank, at, s, m)
 
 
@@ -211,7 +252,12 @@
 def base_of(rank, m, v):
     pairs = m.shape[0]
     return call(
-        base_kernel, 1, 2, jax.ShapeDtypeStruct((pairs, R, R), F32), [], pairs * 2 * R**3, VLIM
+        base_kernel,
+        [SMEM, VMEM, VMEM],
+        jax.ShapeDtypeStruct((pairs, R, R), F32),
+        VMEM,
+        [],
+        pairs * 2 * R**3,
     )(rank, m, v)
 
 
@@ -238,12 +284,11 @@
     pairs = p.shape[0]
     return call(
         own_kernel,
-        2,
-        9,
+        [SMEM] * 2 + [VMEM] * 9,
         jax.ShapeDtypeStruct((pairs, 4, QP, 128), BF16),
+        VMEM,
         [pltpu.VMEM((256, QP, 128), BF16)],
         pairs * 2 * R**3,
-        VLIM,
     )(ends, at, p, *groups)
 
 
@@ -259,16 +304,21 @@
 
 def couple(parts, near):
     return call(
-        couple_kernel, 0, 8, jax.ShapeDtypeStruct((4, QP, 128), BF16), [], 8 * Q * R * R, VLIM
+        couple_kernel, [VMEM] * 8, jax.ShapeDtypeStruct((4, QP, 128), BF16), VMEM, [], 8 * Q * R * R
     )(*parts, *near)
 
 
 def finish_kernel(ends_ref, rank_ref, at_ref, s_ref, own_ref, base_ref, *rest):
     group_refs, out_ref, held_ref = rest[:8], rest[8], rest[9]
-    flat_ref, left_ref, right_ref = rest[10:]
+    flat_ref, left_ref, right_ref, rows_ref, sem = rest[10:]
+    groups = s_ref.shape[0] // 8
     for n in range(8):
         held_ref[n * 32 : (n + 1) * 32] = group_refs[n][...].reshape(32, QP, 128)
     right_ref[...] = jnp.zeros_like(right_ref)
+
+    def send(g):
+        rows = pl.ds(pl.multiple_of(g * 8, 8), 8)
+        return pltpu.make_async_copy(rows_ref.at[g], out_ref.at[rows], sem.at[g])
 
     def work(g, _):
         for i in range(8):
@@ -283,29 +333,32 @@
             total = base_ref[pair] + dot(half, s_ref[pair], ((1,), (0,)))
             inside = masks((rank_ref[pair] + 1) * RSTEP)
             lay_out(jnp.where(inside, total, 0.0), i, flat_ref, left_ref, right_ref)
-        rows = pl.ds(pl.multiple_of(g * 8, 8), 8)
         for j in range(CHUNKS):
-            out_ref[rows, j * 128 : j * 128 + 128] = flat_ref[j * 8 : j * 8 + 8].astype(BF16)
+            rows_ref[g, :, j * 128 : j * 128 + 128] = flat_ref[j * 8 : j * 8 + 8].astype(BF16)
+        send(g).start()
         return _
 
-    lax.fori_loop(0, s_ref.shape[0] // 8, work, 0)
+    lax.fori_loop(0, groups, work, 0)
+    for g in range(groups):
+        send(g).wait()
 
 
 def finish(ends, rank, at, s, own, base, groups):
     pairs = s.shape[0]
     return call(
         finish_kernel,
-        3,
-        11,
+        [SMEM] * 3 + [VMEM] * 11,
         jax.ShapeDtypeStruct((pairs, R * R), BF16),
+        HBM,
         [
             pltpu.VMEM((256, QP, 128), BF16),
             pltpu.VMEM((CHUNKS * 8, 128), F32),
             pltpu.VMEM((8, R, 128), F32),
             pltpu.VMEM((8, R, 128), F32),
+            pltpu.VMEM((pairs // 8, 8, R * R), BF16),
+            pltpu.SemaphoreType.DMA((pairs // 8,)),
         ],
         pairs * 4 * R**3,
-        VLIM,
     )(ends, rank, at, s, own, base, *groups)
 
 
@@ -327,14 +380,13 @@
 
 def whole_step(pair_list, rank_bucket, amplitudes, intersects, integrals, exchange_blocks):
     at = jnp.stack([lax.axis_index(a) for a in AXES]).astype(jnp.int32)
-    y = lax.axis_index("gz")
     ends = pair_list.T
 
-    block = exchange_blocks.reshape(R, R)
-    block = jnp.stack([packed_quarter(block, q) for q in range(4)], axis=0)
-    near = [block] + [stage_z(block, 2 * d) for d in (1, 2, 3)]
-    quarters = [lax.dynamic_slice_in_dim(b, y, 1, axis=0) for b in near]
-    quarters = jnp.concatenate(quarters, axis=0)
+    block = pack(exchange_blocks)
+    pair = jnp.stack([block, stage_z(block, 2)])
+    far = stage_z(pair, 6)
+    near = [pair[0], pair[1], far[1], far[0]]
+    quarters = choose(at, near)
     blocks = sent_to_all(quarters)
 
     m = relay(amplitudes)

time: 143 us -> 124 us (0.87)
  other arithmetic: 9.05 us -> 1.26 us
  local copies, waits for them, and re-layouts: 7.59 us -> 1.75 us
  waiting for transfers between devices: 31.9 us -> 29.3 us
  starting transfers between devices: 68.9 us -> 67 us
    convert_element_type x6, other arithmetic: 8.61 us -> 0.96 us  [added(): return total.astype(BF16)]
    unnamed x36 -> x12, local copies, waits for them, and re-layouts: 6.73 us -> 1.69 us
    ppermute x9 -> x8, starting transfers between devices: 22.1 us -> 19.8 us  [stage_z(): lax.ppermute(array, AXES, pairs_of(lambda x, c, z, y: (x, c, z ^ d, y)))]
    ppermute x9, waiting for transfers between devices: 11.5 us -> 9.36 us  [stage_a(): lax.ppermute(array, AXES, pairs_of(lambda x, c, z, y: (x ^ d, c, z, y) if...]
    ppermute x9 -> x8, waiting for transfers between devices: 14 us -> 12.9 us  [stage_z(): lax.ppermute(array, AXES, pairs_of(lambda x, c, z, y: (x, c, z ^ d, y)))]
    pallas_call x8 -> x10, Pallas kernels: 25.3 us -> 24.4 us  [the longest x1 6.18 us: finish(): call(finish_kernel, [SMEM] * 3 + [VMEM] * 11, jax.ShapeDtypeStruct((pairs...]
  transfers between devices with their start and end apart: 39 -> 38, of which waited for: 13 -> 14; matrix products, arithmetic and copies ran while one was open for 7% -> 1% of each run, Pallas kernels for 6% -> 7%
where the time goes in v2:
time: 124 us
  starting transfers between devices  67 us (54%)
  waiting for transfers between devices  29.3 us (24%)
  Pallas kernels  24.4 us (20%)
  local copies, waits for them, and re-layouts  1.75 us (1%)
  other arithmetic  1.26 us (1%)
    ppermute x12, starting transfers between devices, stage_c(): lax.ppermute(array, AXES, pairs_of(lambda x, c, z, y: (x, c ^ 1, z, y)))  23.8 us
    ppermute x8, starting transfers between devices, stage_z(): lax.ppermute(array, AXES, pairs_of(lambda x, c, z, y: (x, c, z ^ d, y)))  19.8 us
    ppermute x8, waiting for transfers between devices, stage_z(): lax.ppermute(array, AXES, pairs_of(lambda x, c, z, y: (x, c, z ^ d, y)))  12.9 us
    ppermute x9, starting transfers between devices, stage_b(): lax.ppermute(array, AXES, pairs_of(lambda x, c, z, y: (x, c, z, y ^ d) if...  11.8 us
    ppermute x9, starting transfers between devices, stage_a(): lax.ppermute(array, AXES, pairs_of(lambda x, c, z, y: (x ^ d, c, z, y) if...  11.6 us
    ppermute x9, waiting for transfers between devices, stage_a(): lax.ppermute(array, AXES, pairs_of(lambda x, c, z, y: (x ^ d, c, z, y) if...  9.36 us
    pallas_call x1, Pallas kernels, finish(): call(finish_kernel, [SMEM] * 3 + [VMEM] * 11, jax.ShapeDtypeStruct((pairs...  6.18 us
    ppermute x9, waiting for transfers between devices, stage_b(): lax.ppermute(array, AXES, pairs_of(lambda x, c, z, y: (x, c, z, y ^ d) if...  5.99 us
  transfers between devices with their start and end apart: 38, of which 14 were waited for; matrix products, arithmetic and copies ran while one was open for 1% of the time, Pallas kernels for 7%

profile of v2, /device:TPU:1, one launch (start us, length us, event | category | flops | bytes accessed | tf_op | source)
XLA Modules:
  0.0 124.2 jit_solution(6790389630184792890)
XLA Ops:
  5.7 5.1 %shard_map.66 = (bf16[32,192,192]{2,1,0:T(8,128)(2,1)S(1)}, bf16[4,8,72,128]{3,2,1,0:T(8,128)(2,1)S(1)}, bf16[4,8,72,128]{3,2,1,0:T(8,128)(2,1)S(1)}, bf16[4,8,7...) custom-call(s32[2,32]{1,0:T(2,128)S(1)} %bitcast.34, ...), custom_call_target="tpu_custom_call" | custom-call | flops 905969664 | bytes 1048576 | tf_op jit(solution)/shard_map/pallas_call | solution.py:233
  10.7 3.3 %collective-permute-start.14 = (bf16[4,8,72,128]{3,2,1,0:T(8,128)(2,1)S(1)}, bf16[4,8,72,128]{3,2,1,0:T(8,128)(2,1)S(1)}, u32[]{:S(2)}, u32[]{:S(2)}) collective-permute-start(bf16[4,8,72,128]{3,2,1,0:T(8,128)(2,1)S(1)} %get-tuple-element.18), channel_id=1, source_target_pairs={{0,32},{1,33},{2,34},{3,35},{4,36},{5,37},{6,38},{7,39},{8,40},{9,... | collective-permute-start | bytes 1769480 | tf_op jit(solution)/shard_map/ppermute | solution.py:52
  21.9 2.5 %collective-permute-done.refs_1_.x1_ref = bf16[4,72,128]{2,1,0:T(8,128)(2,1)S(1)} collective-permute-done((bf16[4,72,128]{2,1,0:T(8,128)(2,1)S(1)}, bf16[4,72,128]{2,1,0:T(8,128)(2,1)S(1)}, u32[]{:S(2)}, u32[]{:S(2)}) %collective-permute-start) | collective-permute-done | bytes 73760 | tf_op jit(solution)/shard_map/ppermute | solution.py:48
  24.4 5.1 %collective-permute-start.1 = (bf16[2,4,72,128]{3,2,1,0:T(8,128)(2,1)S(1)}, bf16[2,4,72,128]{3,2,1,0:T(8,128)(2,1)S(1)}, u32[]{:S(2)}, u32[]{:S(2)}) collective-permute-start(bf16[2,4,72,128]{3,2,1,0:T(8,128)(2,1)S(1)} %pad_maximum_fusion.2), channel_id=1, source_target_pairs={{0,24},{1,25},{2,26},{3,27},{4,28},{5,29},{6,30},{7,31},{8,16},{9,... | collective-permute-start | bytes 442376 | tf_op jit(solution)/shard_map/ppermute | solution.py:48
  29.4 2.9 %collective-permute-done.1 = bf16[2,4,72,128]{3,2,1,0:T(8,128)(2,1)S(1)} collective-permute-done((bf16[2,4,72,128]{3,2,1,0:T(8,128)(2,1)S(1)}, bf16[2,4,72,128]{3,2,1,0:T(8,128)(2,1)S(1)}, u32[]{:S(2)}, u32[]{:S(2)}) %collective-permute-start.1) | collective-permute-done | bytes 147488 | tf_op jit(solution)/shard_map/ppermute | solution.py:48
  32.9 6.2 %collective-permute-start.2 = (bf16[4,72,128]{2,1,0:T(8,128)(2,1)S(1)}, bf16[4,72,128]{2,1,0:T(8,128)(2,1)S(1)}, u32[]{:S(2)}, u32[]{:S(2)}) collective-permute-start(bf16[4,72,128]{2,1,0:T(8,128)(2,1)S(1)} %shard_map.68), channel_id=1, source_target_pairs={{0,4},{1,5},{2,6},{3,7},{4,0},{5,1},{6,2},{7,3},{8,12},{9,13},{10,... | collective-permute-start | bytes 221192 | tf_op jit(solution)/shard_map/ppermute | solution.py:48
  40.8 2.4 %collective-permute-start.21 = (bf16[8,72,128]{2,1,0:T(8,128)(2,1)S(1)}, bf16[8,72,128]{2,1,0:T(8,128)(2,1)S(1)}, u32[]{:S(2)}, u32[]{:S(2)}) collective-permute-start(bf16[8,72,128]{2,1,0:T(8,128)(2,1)S(1)} %get-tuple-element.25), channel_id=1, source_target_pairs={{0,2},{1,3},{2,0},{3,1},{4,6},{5,7},{6,4},{7,5},{8,10},{9,11},{10,... | collective-permute-start | bytes 442376 | tf_op jit(solution)/shard_map/ppermute | solution.py:42
  43.6 3.7 %collective-permute-start.4 = (bf16[8,72,128]{2,1,0:T(8,128)(2,1)S(1)}, bf16[8,72,128]{2,1,0:T(8,128)(2,1)S(1)}, u32[]{:S(2)}, u32[]{:S(2)}) collective-permute-start(bf16[8,72,128]{2,1,0:T(8,128)(2,1)S(1)} %get-tuple-element.29), channel_id=1, source_target_pairs={{0,2},{1,3},{2,0},{3,1},{4,6},{5,7},{6,4},{7,5},{8,10},{9,11},{10,... | collective-permute-start | bytes 442376 | tf_op jit(solution)/shard_map/ppermute | solution.py:42
  49.4 2.2 %collective-permute-done.4 = bf16[8,72,128]{2,1,0:T(8,128)(2,1)S(1)} collective-permute-done((bf16[8,72,128]{2,1,0:T(8,128)(2,1)S(1)}, bf16[8,72,128]{2,1,0:T(8,128)(2,1)S(1)}, u32[]{:S(2)}, u32[]{:S(2)}) %collective-permute-start.4) | collective-permute-done | bytes 147488 | tf_op jit(solution)/shard_map/ppermute | solution.py:42
  53.4 2.5 %collective-permute-start.7 = (bf16[4,8,72,128]{3,2,1,0:T(8,128)(2,1)S(1)}, bf16[4,8,72,128]{3,2,1,0:T(8,128)(2,1)S(1)}, u32[]{:S(2)}, u32[]{:S(2)}) collective-permute-start(bf16[4,8,72,128]{3,2,1,0:T(8,128)(2,1)S(1)} %pad_maximum_fusion.rest_0_), channel_id=1, source_target_pairs={{0,128},{1,129},{2,130},{3,131},{4,132},{5,133},{6,134},{7,135},{8... | collective-permute-start | bytes 1769480 | tf_op jit(solution)/shard_map/ppermute | solution.py:36
  61.5 3.7 %collective-permute-start.9 = (bf16[4,8,72,128]{3,2,1,0:T(8,128)(2,1)S(1)}, bf16[4,8,72,128]{3,2,1,0:T(8,128)(2,1)S(1)}, u32[]{:S(2)}, u32[]{:S(2)}) collective-permute-start(bf16[4,8,72,128]{3,2,1,0:T(8,128)(2,1)S(1)} %pad_maximum_fusion.rest_0_), channel_id=1, source_target_pairs={{0,32},{1,33},{2,34},{3,35},{4,36},{5,37},{6,38},{7,39},{8,40},{9,... | collective-permute-start | bytes 1769480 | tf_op jit(solution)/shard_map/ppermute | solution.py:52
  65.2 2.5 %collective-permute-start.26 = (bf16[4,72,128]{2,1,0:T(8,128)(2,1)S(1)}, bf16[4,72,128]{2,1,0:T(8,128)(2,1)S(1)}, u32[]{:S(2)}, u32[]{:S(2)}) collective-permute-start(bf16[4,72,128]{2,1,0:T(8,128)(2,1)S(1)} %add_convert_fusion.5.d0_ref), channel_id=1, source_target_pairs={{0,24},{1,25},{2,26},{3,27},{4,28},{5,29},{6,30},{7,31},{8,16},{9,... | collective-permute-start | bytes 221192 | tf_op jit(solution)/shard_map/ppermute | solution.py:48
  67.7 3.1 %collective-permute-done.26.d3_ref = bf16[4,72,128]{2,1,0:T(8,128)(2,1)S(1)} collective-permute-done((bf16[4,72,128]{2,1,0:T(8,128)(2,1)S(1)}, bf16[4,72,128]{2,1,0:T(8,128)(2,1)S(1)}, u32[]{:S(2)}, u32[]{:S(2)}) %collective-permute-start.26) | collective-permute-done | bytes 73760 | tf_op jit(solution)/shard_map/ppermute | solution.py:48
  73.2 2.3 %collective-permute-done.27 = bf16[4,72,128]{2,1,0:T(8,128)(2,1)S(1)} collective-permute-done((bf16[4,72,128]{2,1,0:T(8,128)(2,1)S(1)}, bf16[4,72,128]{2,1,0:T(8,128)(2,1)S(1)}, u32[]{:S(2)}, u32[]{:S(2)}) %collective-permute-start.27) | collective-permute-done | bytes 73760 | tf_op jit(solution)/shard_map/ppermute | solution.py:48
  76.0 2.4 %collective-permute-start.29 = (bf16[8,72,128]{2,1,0:T(8,128)(2,1)S(1)}, bf16[8,72,128]{2,1,0:T(8,128)(2,1)S(1)}, u32[]{:S(2)}, u32[]{:S(2)}) collective-permute-start(bf16[8,72,128]{2,1,0:T(8,128)(2,1)S(1)} %get-tuple-element.27), channel_id=1, source_target_pairs={{0,2},{1,3},{2,0},{3,1},{4,6},{5,7},{6,4},{7,5},{8,10},{9,11},{10,... | collective-permute-start | bytes 442376 | tf_op jit(solution)/shard_map/ppermute | solution.py:42
  79.9 6.2 %collective-permute-start.10 = (bf16[4,8,72,128]{3,2,1,0:T(8,128)(2,1)S(1)}, bf16[4,8,72,128]{3,2,1,0:T(8,128)(2,1)S(1)}, u32[]{:S(2)}, u32[]{:S(2)}) collective-permute-start(bf16[4,8,72,128]{3,2,1,0:T(8,128)(2,1)S(1)} %collective-permute-done.6.rest_1_), channel_id=1, source_target_pairs={{0,32},{1,33},{2,34},{3,35},{4,36},{5,37},{6,38},{7,39},{8,40},{9,... | collective-permute-start | bytes 1769480 | tf_op jit(solution)/shard_map/ppermute | solution.py:52
  86.1 2.3 %collective-permute-start.11 = (bf16[4,8,72,128]{3,2,1,0:T(8,128)(2,1)S(1)}, bf16[4,8,72,128]{3,2,1,0:T(8,128)(2,1)S(1)}, u32[]{:S(2)}, u32[]{:S(2)}) collective-permute-start(bf16[4,8,72,128]{3,2,1,0:T(8,128)(2,1)S(1)} %collective-permute-done.7.rest_2_), channel_id=1, source_target_pairs={{0,32},{1,33},{2,34},{3,35},{4,36},{5,37},{6,38},{7,39},{8,40},{9,... | collective-permute-start | bytes 1769480 | tf_op jit(solution)/shard_map/ppermute | solution.py:52
  92.5 2.5 %collective-permute-start.12 = (bf16[4,8,72,128]{3,2,1,0:T(8,128)(2,1)S(1)}, bf16[4,8,72,128]{3,2,1,0:T(8,128)(2,1)S(1)}, u32[]{:S(2)}, u32[]{:S(2)}) collective-permute-start(bf16[4,8,72,128]{3,2,1,0:T(8,128)(2,1)S(1)} %collective-permute-done.8.rest_3_), channel_id=1, source_target_pairs={{0,32},{1,33},{2,34},{3,35},{4,36},{5,37},{6,38},{7,39},{8,40},{9,... | collective-permute-start | bytes 1769480 | tf_op jit(solution)/shard_map/ppermute | solution.py:52
  95.1 2.6 %collective-permute-done.31.rest_1_ = bf16[4,8,72,128]{3,2,1,0:T(8,128)(2,1)S(1)} collective-permute-done((bf16[4,8,72,128]{3,2,1,0:T(8,128)(2,1)S(1)}, bf16[4,8,72,128]{3,2,1,0:T(8,128)(2,1)S(1)}, u32[]{:S(2)}, u32[]{:S(2)}) %collective-permute-start.31) | collective-permute-done | bytes 589856 | tf_op jit(solution)/shard_map/ppermute | solution.py:36
  97.6 2.5 %collective-permute-start.35 = (bf16[4,8,72,128]{3,2,1,0:T(8,128)(2,1)S(1)}, bf16[4,8,72,128]{3,2,1,0:T(8,128)(2,1)S(1)}, u32[]{:S(2)}, u32[]{:S(2)}) collective-permute-start(bf16[4,8,72,128]{3,2,1,0:T(8,128)(2,1)S(1)} %collective-permute-done.31.rest_1_), channel_id=1, source_target_pairs={{0,32},{1,33},{2,34},{3,35},{4,36},{5,37},{6,38},{7,39},{8,40},{9,... | collective-permute-start | bytes 1769480 | tf_op jit(solution)/shard_map/ppermute | solution.py:52
  100.1 5.2 %collective-permute-done.32.rest_2_ = bf16[4,8,72,128]{3,2,1,0:T(8,128)(2,1)S(1)} collective-permute-done((bf16[4,8,72,128]{3,2,1,0:T(8,128)(2,1)S(1)}, bf16[4,8,72,128]{3,2,1,0:T(8,128)(2,1)S(1)}, u32[]{:S(2)}, u32[]{:S(2)}) %collective-permute-start.32) | collective-permute-done | bytes 589856 | tf_op jit(solution)/shard_map/ppermute | solution.py:36
  111.5 2.4 %shard_map.71.base_ref = f32[32,192,192]{2,1,0:T(8,128)S(1)} custom-call(s32[32]{0:T(128)S(1)} %copy-done.4, bf16[32,192,192]{2,1,0:T(8,128)(2,1)S(1)} %shard_map.65.m_ref, bf16[32,192,192]{2,1,0:T(8,128)(2,1)S(1)} %shard_map.70.v_ref), custom_call_target="tpu_custom_call" | custom-call | flops 452984832 | bytes 1048576 | tf_op jit(solution)/shard_map/pallas_call | solution.py:254
  113.9 3.9 %shard_map.69.own_ref = bf16[32,4,72,128]{3,2,1,0:T(8,128)(2,1)S(1)} custom-call(s32[2,32]{1,0:T(2,128)S(1)} %bitcast.35, s32[4]{0:T(128)S(1)} %pad_add_fusion.at_ref, bf16[32,192,192]{2,1,0:T(8,128)(2,1)S(1)} %get-tuple-element.14.p_ref, bf16[4,8,72,128]{3,2,1,0:T(8,128)(2,1)S(1)} %pad_maximum_fusion.rest_0_, ...), custom_call_target="tpu_custom_call" | custom-call | flops 452984832 | bytes 1048576 | tf_op jit(solution)/shard_map/pallas_call | solution.py:285
  117.8 6.2 %shard_map.73 = bf16[32,36864]{1,0:T(8,128)(2,1)} custom-call(s32[2,32]{1,0:T(2,128)S(1)} %bitcast.36, s32[32]{0:T(128)S(1)} %copy-done.4, s32[4]{0:T(128)S(1)} %pad_add_fusion.at_ref, bf16[32,192,192]{2,1,0:T(8,128)(2,1)S(1)} %shard_map.64.s_ref, bf16[32,4,72,128]{3,2,1,0:T(8,128)(2,1)S(1)} %shard_map.69.own_ref, f32[32,192,192]{2,1,0:T(8,128)S(1)} %shard_map.71.base_ref, ...), custom_call_target="tpu_custom_call" | custom-call | flops 905969664 | bytes 1048576 | tf_op jit(solution)/shard_map/pallas_call | solution.py:348
  (89 shorter events, 40.4 us)
Async XLA Ops:
  14.5 24.5 %collective-permute-start.13 = (bf16[4,8,72,128]{3,2,1,0:T(8,128)(2,1)S(1)}, bf16[4,8,72,128]{3,2,1,0:T(8,128)(2,1)S(1)}, u32[]{:S(2)}, u32[]{:S(2)}) collective-permute-start(bf16[4,8,72,128]{3,2,1,0:T(8,128)(2,1)S(1)} %get-tuple-element.16), channel_id=1, source_target_pairs={{0,32},{1,33},{2,34},{3,35},{4,36},{5,37},{6,38},{7,39},{8,40},{9,... | collective-permute-start | bytes 1769480 | tf_op jit(solution)/shard_map/ppermute | solution.py:52
  15.8 23.2 %collective-permute-start.15 = (bf16[4,8,72,128]{3,2,1,0:T(8,128)(2,1)S(1)}, bf16[4,8,72,128]{3,2,1,0:T(8,128)(2,1)S(1)}, u32[]{:S(2)}, u32[]{:S(2)}) collective-permute-start(bf16[4,8,72,128]{3,2,1,0:T(8,128)(2,1)S(1)} %add_convert_fusion.3), channel_id=1, source_target_pairs={{0,128},{1,129},{2,130},{3,131},{4,132},{5,133},{6,134},{7,135},{8... | collective-permute-start | bytes 1769480 | tf_op jit(solution)/shard_map/ppermute | solution.py:36
  17.3 21.7 %collective-permute-start.17 = (bf16[4,8,72,128]{3,2,1,0:T(8,128)(2,1)S(1)}, bf16[4,8,72,128]{3,2,1,0:T(8,128)(2,1)S(1)}, u32[]{:S(2)}, u32[]{:S(2)}) collective-permute-start(bf16[4,8,72,128]{3,2,1,0:T(8,128)(2,1)S(1)} %add_convert_fusion.2), channel_id=1, source_target_pairs={{0,64},{1,65},{2,66},{3,67},{4,68},{5,69},{6,70},{7,71},{8,72},{9,... | collective-permute-start | bytes 1769480 | tf_op jit(solution)/shard_map/ppermute | solution.py:36
  17.9 21.1 %collective-permute-start.19 = (bf16[4,8,72,128]{3,2,1,0:T(8,128)(2,1)S(1)}, bf16[4,8,72,128]{3,2,1,0:T(8,128)(2,1)S(1)}, u32[]{:S(2)}, u32[]{:S(2)}) collective-permute-start(bf16[4,8,72,128]{3,2,1,0:T(8,128)(2,1)S(1)} %add_convert_fusion.1), channel_id=1, source_target_pairs={{0,192},{1,193},{2,194},{3,195},{4,196},{5,197},{6,198},{7,199},{8... | collective-permute-start | bytes 1769480 | tf_op jit(solution)/shard_map/ppermute | solution.py:36
  24.4 7.9 %collective-permute-start.1 = (bf16[2,4,72,128]{3,2,1,0:T(8,128)(2,1)S(1)}, bf16[2,4,72,128]{3,2,1,0:T(8,128)(2,1)S(1)}, u32[]{:S(2)}, u32[]{:S(2)}) collective-permute-start(bf16[2,4,72,128]{3,2,1,0:T(8,128)(2,1)S(1)} %pad_maximum_fusion.2), channel_id=1, source_target_pairs={{0,24},{1,25},{2,26},{3,27},{4,28},{5,29},{6,30},{7,31},{8,16},{9,... | collective-permute-start | bytes 442376 | tf_op jit(solution)/shard_map/ppermute | solution.py:48
  32.9 10.6 %collective-permute-start.2 = (bf16[4,72,128]{2,1,0:T(8,128)(2,1)S(1)}, bf16[4,72,128]{2,1,0:T(8,128)(2,1)S(1)}, u32[]{:S(2)}, u32[]{:S(2)}) collective-permute-start(bf16[4,72,128]{2,1,0:T(8,128)(2,1)S(1)} %shard_map.68), channel_id=1, source_target_pairs={{0,4},{1,5},{2,6},{3,7},{4,0},{5,1},{6,2},{7,3},{8,12},{9,13},{10,... | collective-permute-start | bytes 221192 | tf_op jit(solution)/shard_map/ppermute | solution.py:48
  43.6 8.1 %collective-permute-start.4 = (bf16[8,72,128]{2,1,0:T(8,128)(2,1)S(1)}, bf16[8,72,128]{2,1,0:T(8,128)(2,1)S(1)}, u32[]{:S(2)}, u32[]{:S(2)}) collective-permute-start(bf16[8,72,128]{2,1,0:T(8,128)(2,1)S(1)} %get-tuple-element.29), channel_id=1, source_target_pairs={{0,2},{1,3},{2,0},{3,1},{4,6},{5,7},{6,4},{7,5},{8,10},{9,11},{10,... | collective-permute-start | bytes 442376 | tf_op jit(solution)/shard_map/ppermute | solution.py:42
  53.3 22.7 %collective-permute-start.6 = (bf16[4,8,72,128]{3,2,1,0:T(8,128)(2,1)S(1)}, bf16[4,8,72,128]{3,2,1,0:T(8,128)(2,1)S(1)}, u32[]{:S(2)}, u32[]{:S(2)}) collective-permute-start(bf16[4,8,72,128]{3,2,1,0:T(8,128)(2,1)S(1)} %pad_maximum_fusion.rest_0_), channel_id=1, source_target_pairs={{0,64},{1,65},{2,66},{3,67},{4,68},{5,69},{6,70},{7,71},{8,72},{9,... | collective-permute-start | bytes 1769480 | tf_op jit(solution)/shard_map/ppermute | solution.py:36
  53.4 25.0 %collective-permute-start.7 = (bf16[4,8,72,128]{3,2,1,0:T(8,128)(2,1)S(1)}, bf16[4,8,72,128]{3,2,1,0:T(8,128)(2,1)S(1)}, u32[]{:S(2)}, u32[]{:S(2)}) collective-permute-start(bf16[4,8,72,128]{3,2,1,0:T(8,128)(2,1)S(1)} %pad_maximum_fusion.rest_0_), channel_id=1, source_target_pairs={{0,128},{1,129},{2,130},{3,131},{4,132},{5,133},{6,134},{7,135},{8... | collective-permute-start | bytes 1769480 | tf_op jit(solution)/shard_map/ppermute | solution.py:36
  56.6 8.6 %collective-permute-start.25 = (bf16[4,72,128]{2,1,0:T(8,128)(2,1)S(1)}, bf16[4,72,128]{2,1,0:T(8,128)(2,1)S(1)}, u32[]{:S(2)}, u32[]{:S(2)}) collective-permute-start(bf16[4,72,128]{2,1,0:T(8,128)(2,1)S(1)} %add_convert_fusion.5.d0_ref), channel_id=1, source_target_pairs={{0,16},{1,17},{2,18},{3,19},{4,20},{5,21},{6,22},{7,23},{8,24},{9,... | collective-permute-start | bytes 221192 | tf_op jit(solution)/shard_map/ppermute | solution.py:48
  57.9 31.8 %collective-permute-start.8 = (bf16[4,8,72,128]{3,2,1,0:T(8,128)(2,1)S(1)}, bf16[4,8,72,128]{3,2,1,0:T(8,128)(2,1)S(1)}, u32[]{:S(2)}, u32[]{:S(2)}) collective-permute-start(bf16[4,8,72,128]{3,2,1,0:T(8,128)(2,1)S(1)} %pad_maximum_fusion.rest_0_), channel_id=1, source_target_pairs={{0,192},{1,193},{2,194},{3,195},{4,196},{5,197},{6,198},{7,199},{8... | collective-permute-start | bytes 1769480 | tf_op jit(solution)/shard_map/ppermute | solution.py:36
  61.5 29.9 %collective-permute-start.9 = (bf16[4,8,72,128]{3,2,1,0:T(8,128)(2,1)S(1)}, bf16[4,8,72,128]{3,2,1,0:T(8,128)(2,1)S(1)}, u32[]{:S(2)}, u32[]{:S(2)}) collective-permute-start(bf16[4,8,72,128]{3,2,1,0:T(8,128)(2,1)S(1)} %pad_maximum_fusion.rest_0_), channel_id=1, source_target_pairs={{0,32},{1,33},{2,34},{3,35},{4,36},{5,37},{6,38},{7,39},{8,40},{9,... | collective-permute-start | bytes 1769480 | tf_op jit(solution)/shard_map/ppermute | solution.py:52
  76.0 10.1 %collective-permute-start.29 = (bf16[8,72,128]{2,1,0:T(8,128)(2,1)S(1)}, bf16[8,72,128]{2,1,0:T(8,128)(2,1)S(1)}, u32[]{:S(2)}, u32[]{:S(2)}) collective-permute-start(bf16[8,72,128]{2,1,0:T(8,128)(2,1)S(1)} %get-tuple-element.27), channel_id=1, source_target_pairs={{0,2},{1,3},{2,0},{3,1},{4,6},{5,7},{6,4},{7,5},{8,10},{9,11},{10,... | collective-permute-start | bytes 442376 | tf_op jit(solution)/shard_map/ppermute | solution.py:42
  78.3 10.1 %collective-permute-start.30 = (bf16[8,72,128]{2,1,0:T(8,128)(2,1)S(1)}, bf16[8,72,128]{2,1,0:T(8,128)(2,1)S(1)}, u32[]{:S(2)}, u32[]{:S(2)}) collective-permute-start(bf16[8,72,128]{2,1,0:T(8,128)(2,1)S(1)} %get-tuple-element.27), channel_id=1, source_target_pairs={{0,3},{1,2},{2,1},{3,0},{4,7},{5,6},{6,5},{7,4},{8,11},{9,10},{10,... | collective-permute-start | bytes 442376 | tf_op jit(solution)/shard_map/ppermute | solution.py:42
  79.9 12.5 %collective-permute-start.10 = (bf16[4,8,72,128]{3,2,1,0:T(8,128)(2,1)S(1)}, bf16[4,8,72,128]{3,2,1,0:T(8,128)(2,1)S(1)}, u32[]{:S(2)}, u32[]{:S(2)}) collective-permute-start(bf16[4,8,72,128]{3,2,1,0:T(8,128)(2,1)S(1)} %collective-permute-done.6.rest_1_), channel_id=1, source_target_pairs={{0,32},{1,33},{2,34},{3,35},{4,36},{5,37},{6,38},{7,39},{8,40},{9,... | collective-permute-start | bytes 1769480 | tf_op jit(solution)/shard_map/ppermute | solution.py:52
  86.1 8.9 %collective-permute-start.11 = (bf16[4,8,72,128]{3,2,1,0:T(8,128)(2,1)S(1)}, bf16[4,8,72,128]{3,2,1,0:T(8,128)(2,1)S(1)}, u32[]{:S(2)}, u32[]{:S(2)}) collective-permute-start(bf16[4,8,72,128]{3,2,1,0:T(8,128)(2,1)S(1)} %collective-permute-done.7.rest_2_), channel_id=1, source_target_pairs={{0,32},{1,33},{2,34},{3,35},{4,36},{5,37},{6,38},{7,39},{8,40},{9,... | collective-permute-start | bytes 1769480 | tf_op jit(solution)/shard_map/ppermute | solution.py:52
  88.5 9.1 %collective-permute-start.31 = (bf16[4,8,72,128]{3,2,1,0:T(8,128)(2,1)S(1)}, bf16[4,8,72,128]{3,2,1,0:T(8,128)(2,1)S(1)}, u32[]{:S(2)}, u32[]{:S(2)}) collective-permute-start(bf16[4,8,72,128]{3,2,1,0:T(8,128)(2,1)S(1)} %pad_maximum_fusion.1.rest_0_), channel_id=1, source_target_pairs={{0,64},{1,65},{2,66},{3,67},{4,68},{5,69},{6,70},{7,71},{8,72},{9,... | collective-permute-start | bytes 1769480 | tf_op jit(solution)/shard_map/ppermute | solution.py:36
  89.6 15.7 %collective-permute-start.32 = (bf16[4,8,72,128]{3,2,1,0:T(8,128)(2,1)S(1)}, bf16[4,8,72,128]{3,2,1,0:T(8,128)(2,1)S(1)}, u32[]{:S(2)}, u32[]{:S(2)}) collective-permute-start(bf16[4,8,72,128]{3,2,1,0:T(8,128)(2,1)S(1)} %pad_maximum_fusion.1.rest_0_), channel_id=1, source_target_pairs={{0,128},{1,129},{2,130},{3,131},{4,132},{5,133},{6,134},{7,135},{8... | collective-permute-start | bytes 1769480 | tf_op jit(solution)/shard_map/ppermute | solution.py:36
  91.4 16.6 %collective-permute-start.33 = (bf16[4,8,72,128]{3,2,1,0:T(8,128)(2,1)S(1)}, bf16[4,8,72,128]{3,2,1,0:T(8,128)(2,1)S(1)}, u32[]{:S(2)}, u32[]{:S(2)}) collective-permute-start(bf16[4,8,72,128]{3,2,1,0:T(8,128)(2,1)S(1)} %pad_maximum_fusion.1.rest_0_), channel_id=1, source_target_pairs={{0,192},{1,193},{2,194},{3,195},{4,196},{5,197},{6,198},{7,199},{8... | collective-permute-start | bytes 1769480 | tf_op jit(solution)/shard_map/ppermute | solution.py:36
  92.5 21.4 %collective-permute-start.12 = (bf16[4,8,72,128]{3,2,1,0:T(8,128)(2,1)S(1)}, bf16[4,8,72,128]{3,2,1,0:T(8,128)(2,1)S(1)}, u32[]{:S(2)}, u32[]{:S(2)}) collective-permute-start(bf16[4,8,72,128]{3,2,1,0:T(8,128)(2,1)S(1)} %collective-permute-done.8.rest_3_), channel_id=1, source_target_pairs={{0,32},{1,33},{2,34},{3,35},{4,36},{5,37},{6,38},{7,39},{8,40},{9,... | collective-permute-start | bytes 1769480 | tf_op jit(solution)/shard_map/ppermute | solution.py:52
  95.0 22.8 %collective-permute-start.34 = (bf16[4,8,72,128]{3,2,1,0:T(8,128)(2,1)S(1)}, bf16[4,8,72,128]{3,2,1,0:T(8,128)(2,1)S(1)}, u32[]{:S(2)}, u32[]{:S(2)}) collective-permute-start(bf16[4,8,72,128]{3,2,1,0:T(8,128)(2,1)S(1)} %pad_maximum_fusion.1.rest_0_), channel_id=1, source_target_pairs={{0,32},{1,33},{2,34},{3,35},{4,36},{5,37},{6,38},{7,39},{8,40},{9,... | collective-permute-start | bytes 1769480 | tf_op jit(solution)/shard_map/ppermute | solution.py:52
  97.6 20.1 %collective-permute-start.35 = (bf16[4,8,72,128]{3,2,1,0:T(8,128)(2,1)S(1)}, bf16[4,8,72,128]{3,2,1,0:T(8,128)(2,1)S(1)}, u32[]{:S(2)}, u32[]{:S(2)}) collective-permute-start(bf16[4,8,72,128]{3,2,1,0:T(8,128)(2,1)S(1)} %collective-permute-done.31.rest_1_), channel_id=1, source_target_pairs={{0,32},{1,33},{2,34},{3,35},{4,36},{5,37},{6,38},{7,39},{8,40},{9,... | collective-permute-start | bytes 1769480 | tf_op jit(solution)/shard_map/ppermute | solution.py:52
  105.3 12.4 %collective-permute-start.36 = (bf16[4,8,72,128]{3,2,1,0:T(8,128)(2,1)S(1)}, bf16[4,8,72,128]{3,2,1,0:T(8,128)(2,1)S(1)}, u32[]{:S(2)}, u32[]{:S(2)}) collective-permute-start(bf16[4,8,72,128]{3,2,1,0:T(8,128)(2,1)S(1)} %collective-permute-done.32.rest_2_), channel_id=1, source_target_pairs={{0,32},{1,33},{2,34},{3,35},{4,36},{5,37},{6,38},{7,39},{8,40},{9,... | collective-permute-start | bytes 1769480 | tf_op jit(solution)/shard_map/ppermute | solution.py:52
  108.0 9.8 %collective-permute-start.37 = (bf16[4,8,72,128]{3,2,1,0:T(8,128)(2,1)S(1)}, bf16[4,8,72,128]{3,2,1,0:T(8,128)(2,1)S(1)}, u32[]{:S(2)}, u32[]{:S(2)}) collective-permute-start(bf16[4,8,72,128]{3,2,1,0:T(8,128)(2,1)S(1)} %collective-permute-done.33.rest_3_), channel_id=1, source_target_pairs={{0,32},{1,33},{2,34},{3,35},{4,36},{5,37},{6,38},{7,39},{8,40},{9,... | collective-permute-start | bytes 1769480 | tf_op jit(solution)/shard_map/ppermute | solution.py:52
  (20 other events, 138.9 us)

commit v3 on v2

--- a/solution.py
+++ b/solution.py
@@ -11,6 +11,7 @@
 Q = 48
 QP = 72
 CHUNKS = R * R // 128
+EVEN = (0, 3, 5, 6)
 STEP = 8
 AXES = ("gx_0", "gx_1", "gy", "gz")
 GX_GY = ("gx_0", "gx_1", "gy")
@@ -58,7 +59,8 @@
     dx, dq, dz = (k >> 4) ^ x, q ^ y, (k & 7) ^ z
     a = jnp.where(core == 0, dx, dq)
     b = jnp.where(core == 0, dq, dx)
-    return (((core ^ c) * 4 + a) * 4 + b) * 8 + (dz & 1) * 4 + (dz >> 1)
+    odd = (dz ^ (dz >> 1) ^ (dz >> 2)) & 1
+    return (((core ^ c) * 4 + a) * 4 + b) * 8 + odd * 4 + (dz >> 1)
 
 
 def packed_quarter(block, q):
@@ -88,6 +90,7 @@
 SMEM = pl.BlockSpec(memory_space=pltpu.SMEM)
 VMEM = pl.BlockSpec(memory_space=pltpu.VMEM)
 HBM = pl.BlockSpec(memory_space=pltpu.HBM)
+ANY = pl.BlockSpec(memory_space=pl.ANY)
 GROUP = (4, 8, QP, 128)
 
 
@@ -193,6 +196,14 @@
     )(at, *near)
 
 
+def copy_kernel(x_ref, o_ref):
+    o_ref[...] = x_ref[...]
+
+
+def copied(x):
+    return call(copy_kernel, [VMEM], jax.ShapeDtypeStruct(x.shape, x.dtype), VMEM, [], 1)(x)
+
+
 def lay_out(block, i, flat_ref, left_ref, right_ref):
     low = lax.broadcasted_iota(jnp.int32, (R // 2, 128), 1) < 64
     left_ref[i] = block[:, :128]
@@ -207,9 +218,17 @@
     )
 
 
-def project_kernel(ends_ref, rank_ref, at_ref, s_ref, m_ref, p_ref, *rest):
-    out_refs, sums_ref = rest[:8], rest[8]
+def project_kernel(ends_in, rank_in, at_in, s_ref, m_ref, p_ref, *rest):
+    out_refs, sums_ref, ends_ref, rank_ref, at_ref, sem = rest[:8], *rest[8:]
+    copies = [
+        pltpu.make_async_copy(a, b, sem.at[n])
+        for n, (a, b) in enumerate(((ends_in, ends_ref), (rank_in, rank_ref), (at_in, at_ref)))
+    ]
+    for copy in copies:
+        copy.start()
     sums_ref[...] = jnp.zeros_like(sums_ref)
+    for copy in copies:
+        copy.wait()
 
     def work(pair):
         inside = masks((rank_ref[pair] + 1) * RSTEP)
@@ -232,10 +251,12 @@
     pairs = s.shape[0]
     return call(
         project_kernel,
-        [SMEM] * 3 + [VMEM] * 2,
+        [ANY] * 3 + [VMEM] * 2,
         [jax.ShapeDtypeStruct((pairs, R, R), BF16)] + [jax.ShapeDtypeStruct(GROUP, BF16)] * 8,
         [VMEM] * 9,
-        [pltpu.VMEM((256, QP, 128), BF16)],
+        [pltpu.VMEM((256, QP, 128), BF16)]
+        + [pltpu.SMEM(f.shape, jnp.int32) for f in (ends, rank, at)]
+        + [pltpu.SemaphoreType.DMA((3,))],
         pairs * 4 * R**3,
     )(ends, rank, at, s, m)
 
@@ -308,13 +329,21 @@
     )(*parts, *near)
 
 
-def finish_kernel(ends_ref, rank_ref, at_ref, s_ref, own_ref, base_ref, *rest):
+def finish_kernel(ends_in, rank_in, at_in, s_ref, own_ref, base_ref, *rest):
     group_refs, out_ref, held_ref = rest[:8], rest[8], rest[9]
-    flat_ref, left_ref, right_ref, rows_ref, sem = rest[10:]
+    flat_ref, left_ref, right_ref, rows_ref, sem, ends_ref, rank_ref, at_ref, facts_sem = rest[10:]
     groups = s_ref.shape[0] // 8
+    copies = [
+        pltpu.make_async_copy(a, b, facts_sem.at[n])
+        for n, (a, b) in enumerate(((ends_in, ends_ref), (rank_in, rank_ref), (at_in, at_ref)))
+    ]
+    for copy in copies:
+        copy.start()
     for n in range(8):
         held_ref[n * 32 : (n + 1) * 32] = group_refs[n][...].reshape(32, QP, 128)
     right_ref[...] = jnp.zeros_like(right_ref)
+    for copy in copies:
+        copy.wait()
 
     def send(g):
         rows = pl.ds(pl.multiple_of(g * 8, 8), 8)
@@ -347,7 +376,7 @@
     pairs = s.shape[0]
     return call(
         finish_kernel,
-        [SMEM] * 3 + [VMEM] * 11,
+        [ANY] * 3 + [VMEM] * 11,
         jax.ShapeDtypeStruct((pairs, R * R), BF16),
         HBM,
         [
@@ -357,6 +386,10 @@
             pltpu.VMEM((8, R, 128), F32),
             pltpu.VMEM((pairs // 8, 8, R * R), BF16),
             pltpu.SemaphoreType.DMA((pairs // 8,)),
+            pltpu.SMEM(ends.shape, jnp.int32),
+            pltpu.SMEM(rank.shape, jnp.int32),
+            pltpu.SMEM(at.shape, jnp.int32),
+            pltpu.SemaphoreType.DMA((3,)),
         ],
         pairs * 4 * R**3,
     )(ends, rank, at, s, own, base, *groups)
@@ -383,8 +416,8 @@
     ends = pair_list.T
 
     block = pack(exchange_blocks)
-    pair = jnp.stack([block, stage_z(block, 2)])
-    far = stage_z(pair, 6)
+    pair = jnp.stack([block, stage_z(block, EVEN[1])])
+    far = stage_z(pair, EVEN[3])
     near = [pair[0], pair[1], far[1], far[0]]
     quarters = choose(at, near)
     blocks = sent_to_all(quarters)
@@ -395,12 +428,13 @@
     v = relay(integrals)
     base = base_of(rank_bucket, m, v)
 
-    sums = [added(sums[a], stage_c(sums[4 + a])) for a in (2, 1, 3, 0)]
-    moved = [stage_a(sums[n], d) for n, d in enumerate((2, 1, 3))]
+    sums = [added(sums[a], stage_c(sums[4 + a])) for a in (1, 3, 2, 0)]
+    moved = [stage_a(sums[n], d) for n, d in enumerate((1, 3, 2))]
     sums = added(sums[3], *moved)
     sums = added(sums[0], *[stage_b(sums[d], d) for d in (1, 2, 3)])
     sums = added(sums[:4], stage_z(sums[4:], 1))
-    parts = [sums] + [stage_z(sums, 2 * d) for d in (1, 2, 3)]
+    parts = [sums] + [stage_z(sums, EVEN[d]) for d in (1, 2, 3)]
+    near[0] = copied(near[0])
     coupled = couple(parts, near)
     own = own_of(ends, at, p, blocks)
     groups = sent_to_all(coupled)

time: 124 us -> 124 us (level)
  waiting for transfers between devices: 29.3 us -> 34.4 us
  starting transfers between devices: 67 us -> 62 us
    ppermute x8, starting transfers between devices: 19.8 us -> 14.7 us  [stage_z(): lax.ppermute(array, AXES, pairs_of(lambda x, c, z, y: (x, c, z ^ d, y)))]
    ppermute x8, waiting for transfers between devices: 12.9 us -> 17.1 us  [stage_z(): lax.ppermute(array, AXES, pairs_of(lambda x, c, z, y: (x, c, z ^ d, y)))]
    pallas_call x2 -> x3, Pallas kernels: 11.2 us -> 10.7 us  [the longest x1 5.91 us: finish(): call(finish_kernel, [ANY] * 3 + [VMEM] * 11, jax.ShapeDtypeStruct((pairs,...]
  transfers between devices with their start and end apart: 38 -> 38, of which waited for: 14 -> 15; matrix products, arithmetic and copies ran while one was open for 1% -> 1% of each run, Pallas kernels for 7% -> 8%
where the time goes in v3:
time: 124 us
  starting transfers between devices  62 us (50%)
  waiting for transfers between devices  34.4 us (28%)
  Pallas kernels  23.9 us (19%)
  local copies, waits for them, and re-layouts  1.75 us (1%)
  other arithmetic  1.25 us (1%)
    ppermute x12, starting transfers between devices, stage_c(): lax.ppermute(array, AXES, pairs_of(lambda x, c, z, y: (x, c ^ 1, z, y)))  24.1 us
    ppermute x8, waiting for transfers between devices, stage_z(): lax.ppermute(array, AXES, pairs_of(lambda x, c, z, y: (x, c, z ^ d, y)))  17.1 us
    ppermute x8, starting transfers between devices, stage_z(): lax.ppermute(array, AXES, pairs_of(lambda x, c, z, y: (x, c, z ^ d, y)))  14.7 us
    ppermute x9, starting transfers between devices, stage_b(): lax.ppermute(array, AXES, pairs_of(lambda x, c, z, y: (x, c, z, y ^ d) if...  11.8 us
    ppermute x9, starting transfers between devices, stage_a(): lax.ppermute(array, AXES, pairs_of(lambda x, c, z, y: (x ^ d, c, z, y) if...  11.3 us
    ppermute x9, waiting for transfers between devices, stage_a(): lax.ppermute(array, AXES, pairs_of(lambda x, c, z, y: (x ^ d, c, z, y) if...  9.52 us
    ppermute x9, waiting for transfers between devices, stage_b(): lax.ppermute(array, AXES, pairs_of(lambda x, c, z, y: (x, c, z, y ^ d) if...  6.15 us
    pallas_call x1, Pallas kernels, finish(): call(finish_kernel, [ANY] * 3 + [VMEM] * 11, jax.ShapeDtypeStruct((pairs,...  5.91 us
  transfers between devices with their start and end apart: 38, of which 15 were waited for; matrix products, arithmetic and copies ran while one was open for 1% of the time, Pallas kernels for 8%

profile of v3, /device:TPU:1, one launch (start us, length us, event | category | flops | bytes accessed | tf_op | source)
XLA Modules:
  0.0 123.8 jit_solution(7591447900230804695)
XLA Ops:
  3.6 1.9 %shard_map.65.m_ref = bf16[32,192,192]{2,1,0:T(8,128)(2,1)S(1)} custom-call(bf16[32,36864]{1,0:T(8,128)(2,1)S(1)} %copy-done.1), custom_call_target="tpu_custom_call" | custom-call | flops 16777216 | bytes 1048576 | tf_op jit(solution)/shard_map/pallas_call | solution.py:143
  5.7 4.8 %shard_map.66 = (bf16[32,192,192]{2,1,0:T(8,128)(2,1)S(1)}, bf16[4,8,72,128]{3,2,1,0:T(8,128)(2,1)S(1)}, bf16[4,8,72,128]{3,2,1,0:T(8,128)(2,1)S(1)}, bf16[4,8,7...) custom-call(s32[2,32]{1,0:T(2,128)S(1)} %bitcast.34, ...), custom_call_target="tpu_custom_call" | custom-call | flops 905969664 | bytes 1048576 | tf_op jit(solution)/shard_map/pallas_call | solution.py:252
  10.5 3.3 %collective-permute-start.14 = (bf16[4,8,72,128]{3,2,1,0:T(8,128)(2,1)S(1)}, bf16[4,8,72,128]{3,2,1,0:T(8,128)(2,1)S(1)}, u32[]{:S(2)}, u32[]{:S(2)}) collective-permute-start(bf16[4,8,72,128]{3,2,1,0:T(8,128)(2,1)S(1)} %get-tuple-element.18), channel_id=1, source_target_pairs={{0,32},{1,33},{2,34},{3,35},{4,36},{5,37},{6,38},{7,39},{8,40},{9,... | collective-permute-start | bytes 1769480 | tf_op jit(solution)/shard_map/ppermute | solution.py:53
  19.6 3.5 %collective-permute-start = (bf16[4,72,128]{2,1,0:T(8,128)(2,1)S(1)}, bf16[4,72,128]{2,1,0:T(8,128)(2,1)S(1)}, u32[]{:S(2)}, u32[]{:S(2)}) collective-permute-start(bf16[4,72,128]{2,1,0:T(8,128)(2,1)S(1)} %shard_map.67.refs_0_.x_ref), channel_id=1, source_target_pairs={{0,12},{1,13},{2,14},{3,15},{4,8},{5,9},{6,10},{7,11},{8,4},{9,5},... | collective-permute-start | bytes 221192 | tf_op jit(solution)/shard_map/ppermute | solution.py:49
  25.0 3.4 %collective-permute-start.1 = (bf16[2,4,72,128]{3,2,1,0:T(8,128)(2,1)S(1)}, bf16[2,4,72,128]{3,2,1,0:T(8,128)(2,1)S(1)}, u32[]{:S(2)}, u32[]{:S(2)}) collective-permute-start(bf16[2,4,72,128]{3,2,1,0:T(8,128)(2,1)S(1)} %pad_maximum_fusion.2), channel_id=1, source_target_pairs={{0,24},{1,25},{2,26},{3,27},{4,28},{5,29},{6,30},{7,31},{8,16},{9,... | collective-permute-start | bytes 442376 | tf_op jit(solution)/shard_map/ppermute | solution.py:49
  28.4 3.5 %collective-permute-done.1 = bf16[2,4,72,128]{3,2,1,0:T(8,128)(2,1)S(1)} collective-permute-done((bf16[2,4,72,128]{3,2,1,0:T(8,128)(2,1)S(1)}, bf16[2,4,72,128]{3,2,1,0:T(8,128)(2,1)S(1)}, u32[]{:S(2)}, u32[]{:S(2)}) %collective-permute-start.1) | collective-permute-done | bytes 147488 | tf_op jit(solution)/shard_map/ppermute | solution.py:49
  32.6 5.3 %collective-permute-start.2 = (bf16[4,72,128]{2,1,0:T(8,128)(2,1)S(1)}, bf16[4,72,128]{2,1,0:T(8,128)(2,1)S(1)}, u32[]{:S(2)}, u32[]{:S(2)}) collective-permute-start(bf16[4,72,128]{2,1,0:T(8,128)(2,1)S(1)} %shard_map.68), channel_id=1, source_target_pairs={{0,4},{1,5},{2,6},{3,7},{4,0},{5,1},{6,2},{7,3},{8,12},{9,13},{10,... | collective-permute-start | bytes 221192 | tf_op jit(solution)/shard_map/ppermute | solution.py:49
  39.8 2.5 %collective-permute-start.21 = (bf16[8,72,128]{2,1,0:T(8,128)(2,1)S(1)}, bf16[8,72,128]{2,1,0:T(8,128)(2,1)S(1)}, u32[]{:S(2)}, u32[]{:S(2)}) collective-permute-start(bf16[8,72,128]{2,1,0:T(8,128)(2,1)S(1)} %get-tuple-element.25), channel_id=1, source_target_pairs={{0,2},{1,3},{2,0},{3,1},{4,6},{5,7},{6,4},{7,5},{8,10},{9,11},{10,... | collective-permute-start | bytes 442376 | tf_op jit(solution)/shard_map/ppermute | solution.py:43
  42.5 3.7 %collective-permute-start.4 = (bf16[8,72,128]{2,1,0:T(8,128)(2,1)S(1)}, bf16[8,72,128]{2,1,0:T(8,128)(2,1)S(1)}, u32[]{:S(2)}, u32[]{:S(2)}) collective-permute-start(bf16[8,72,128]{2,1,0:T(8,128)(2,1)S(1)} %get-tuple-element.29), channel_id=1, source_target_pairs={{0,2},{1,3},{2,0},{3,1},{4,6},{5,7},{6,4},{7,5},{8,10},{9,11},{10,... | collective-permute-start | bytes 442376 | tf_op jit(solution)/shard_map/ppermute | solution.py:43
  52.8 2.8 %collective-permute-start.7 = (bf16[4,8,72,128]{3,2,1,0:T(8,128)(2,1)S(1)}, bf16[4,8,72,128]{3,2,1,0:T(8,128)(2,1)S(1)}, u32[]{:S(2)}, u32[]{:S(2)}) collective-permute-start(bf16[4,8,72,128]{3,2,1,0:T(8,128)(2,1)S(1)} %pad_maximum_fusion.rest_0_), channel_id=1, source_target_pairs={{0,128},{1,129},{2,130},{3,131},{4,132},{5,133},{6,134},{7,135},{8... | collective-permute-start | bytes 1769480 | tf_op jit(solution)/shard_map/ppermute | solution.py:37
  58.3 2.5 %collective-permute-done.24.d1_ref = bf16[4,72,128]{2,1,0:T(8,128)(2,1)S(1)} collective-permute-done((bf16[4,72,128]{2,1,0:T(8,128)(2,1)S(1)}, bf16[4,72,128]{2,1,0:T(8,128)(2,1)S(1)}, u32[]{:S(2)}, u32[]{:S(2)}) %collective-permute-start.24) | collective-permute-done | bytes 73760 | tf_op jit(solution)/shard_map/ppermute | solution.py:49
  60.9 4.5 %collective-permute-start.9 = (bf16[4,8,72,128]{3,2,1,0:T(8,128)(2,1)S(1)}, bf16[4,8,72,128]{3,2,1,0:T(8,128)(2,1)S(1)}, u32[]{:S(2)}, u32[]{:S(2)}) collective-permute-start(bf16[4,8,72,128]{3,2,1,0:T(8,128)(2,1)S(1)} %pad_maximum_fusion.rest_0_), channel_id=1, source_target_pairs={{0,32},{1,33},{2,34},{3,35},{4,36},{5,37},{6,38},{7,39},{8,40},{9,... | collective-permute-start | bytes 1769480 | tf_op jit(solution)/shard_map/ppermute | solution.py:53
  65.7 5.3 %collective-permute-done.26.d3_ref = bf16[4,72,128]{2,1,0:T(8,128)(2,1)S(1)} collective-permute-done((bf16[4,72,128]{2,1,0:T(8,128)(2,1)S(1)}, bf16[4,72,128]{2,1,0:T(8,128)(2,1)S(1)}, u32[]{:S(2)}, u32[]{:S(2)}) %collective-permute-start.26) | collective-permute-done | bytes 73760 | tf_op jit(solution)/shard_map/ppermute | solution.py:49
  71.8 3.9 %collective-permute-done.27 = bf16[4,72,128]{2,1,0:T(8,128)(2,1)S(1)} collective-permute-done((bf16[4,72,128]{2,1,0:T(8,128)(2,1)S(1)}, bf16[4,72,128]{2,1,0:T(8,128)(2,1)S(1)}, u32[]{:S(2)}, u32[]{:S(2)}) %collective-permute-start.27) | collective-permute-done | bytes 73760 | tf_op jit(solution)/shard_map/ppermute | solution.py:49
  75.8 2.3 %collective-permute-start.29 = (bf16[8,72,128]{2,1,0:T(8,128)(2,1)S(1)}, bf16[8,72,128]{2,1,0:T(8,128)(2,1)S(1)}, u32[]{:S(2)}, u32[]{:S(2)}) collective-permute-start(bf16[8,72,128]{2,1,0:T(8,128)(2,1)S(1)} %get-tuple-element.27), channel_id=1, source_target_pairs={{0,2},{1,3},{2,0},{3,1},{4,6},{5,7},{6,4},{7,5},{8,10},{9,11},{10,... | collective-permute-start | bytes 442376 | tf_op jit(solution)/shard_map/ppermute | solution.py:43
  80.1 6.0 %collective-permute-start.10 = (bf16[4,8,72,128]{3,2,1,0:T(8,128)(2,1)S(1)}, bf16[4,8,72,128]{3,2,1,0:T(8,128)(2,1)S(1)}, u32[]{:S(2)}, u32[]{:S(2)}) collective-permute-start(bf16[4,8,72,128]{3,2,1,0:T(8,128)(2,1)S(1)} %collective-permute-done.6.rest_1_), channel_id=1, source_target_pairs={{0,32},{1,33},{2,34},{3,35},{4,36},{5,37},{6,38},{7,39},{8,40},{9,... | collective-permute-start | bytes 1769480 | tf_op jit(solution)/shard_map/ppermute | solution.py:53
  86.0 2.3 %collective-permute-start.11 = (bf16[4,8,72,128]{3,2,1,0:T(8,128)(2,1)S(1)}, bf16[4,8,72,128]{3,2,1,0:T(8,128)(2,1)S(1)}, u32[]{:S(2)}, u32[]{:S(2)}) collective-permute-start(bf16[4,8,72,128]{3,2,1,0:T(8,128)(2,1)S(1)} %collective-permute-done.7.rest_2_), channel_id=1, source_target_pairs={{0,32},{1,33},{2,34},{3,35},{4,36},{5,37},{6,38},{7,39},{8,40},{9,... | collective-permute-start | bytes 1769480 | tf_op jit(solution)/shard_map/ppermute | solution.py:53
  92.4 2.5 %collective-permute-start.12 = (bf16[4,8,72,128]{3,2,1,0:T(8,128)(2,1)S(1)}, bf16[4,8,72,128]{3,2,1,0:T(8,128)(2,1)S(1)}, u32[]{:S(2)}, u32[]{:S(2)}) collective-permute-start(bf16[4,8,72,128]{3,2,1,0:T(8,128)(2,1)S(1)} %collective-permute-done.8.rest_3_), channel_id=1, source_target_pairs={{0,32},{1,33},{2,34},{3,35},{4,36},{5,37},{6,38},{7,39},{8,40},{9,... | collective-permute-start | bytes 1769480 | tf_op jit(solution)/shard_map/ppermute | solution.py:53
  95.0 2.6 %collective-permute-done.31.rest_1_ = bf16[4,8,72,128]{3,2,1,0:T(8,128)(2,1)S(1)} collective-permute-done((bf16[4,8,72,128]{3,2,1,0:T(8,128)(2,1)S(1)}, bf16[4,8,72,128]{3,2,1,0:T(8,128)(2,1)S(1)}, u32[]{:S(2)}, u32[]{:S(2)}) %collective-permute-start.31) | collective-permute-done | bytes 589856 | tf_op jit(solution)/shard_map/ppermute | solution.py:37
  97.5 2.5 %collective-permute-start.35 = (bf16[4,8,72,128]{3,2,1,0:T(8,128)(2,1)S(1)}, bf16[4,8,72,128]{3,2,1,0:T(8,128)(2,1)S(1)}, u32[]{:S(2)}, u32[]{:S(2)}) collective-permute-start(bf16[4,8,72,128]{3,2,1,0:T(8,128)(2,1)S(1)} %collective-permute-done.31.rest_1_), channel_id=1, source_target_pairs={{0,32},{1,33},{2,34},{3,35},{4,36},{5,37},{6,38},{7,39},{8,40},{9,... | collective-permute-start | bytes 1769480 | tf_op jit(solution)/shard_map/ppermute | solution.py:53
  100.1 5.2 %collective-permute-done.32.rest_2_ = bf16[4,8,72,128]{3,2,1,0:T(8,128)(2,1)S(1)} collective-permute-done((bf16[4,8,72,128]{3,2,1,0:T(8,128)(2,1)S(1)}, bf16[4,8,72,128]{3,2,1,0:T(8,128)(2,1)S(1)}, u32[]{:S(2)}, u32[]{:S(2)}) %collective-permute-start.32) | collective-permute-done | bytes 589856 | tf_op jit(solution)/shard_map/ppermute | solution.py:37
  111.3 2.4 %shard_map.71.base_ref = f32[32,192,192]{2,1,0:T(8,128)S(1)} custom-call(s32[32]{0:T(128)S(1)} %copy-done.4, bf16[32,192,192]{2,1,0:T(8,128)(2,1)S(1)} %shard_map.65.m_ref, bf16[32,192,192]{2,1,0:T(8,128)(2,1)S(1)} %shard_map.70.v_ref), custom_call_target="tpu_custom_call" | custom-call | flops 452984832 | bytes 1048576 | tf_op jit(solution)/shard_map/pallas_call | solution.py:275
  113.7 4.0 %shard_map.69.own_ref = bf16[32,4,72,128]{3,2,1,0:T(8,128)(2,1)S(1)} custom-call(s32[2,32]{1,0:T(2,128)S(1)} %bitcast.35, s32[4]{0:T(128)S(1)} %pad_add_fusion.at_in.at_ref, bf16[32,192,192]{2,1,0:T(8,128)(2,1)S(1)} %get-tuple-element.14.p_ref, bf16[4,8,72,128]{3,2,1,0:T(8,128)(2,1)S(1)} %pad_maximum_fusion.rest_0_, ...), custom_call_target="tpu_custom_call" | custom-call | flops 452984832 | bytes 1048576 | tf_op jit(solution)/shard_map/pallas_call | solution.py:306
  117.7 5.9 %shard_map.74 = bf16[32,36864]{1,0:T(8,128)(2,1)} custom-call(s32[2,32]{1,0:T(2,128)S(1)} %bitcast.36, s32[32]{0:T(128)S(1)} %copy-done.4, s32[4]{0:T(128)S(1)} %pad_add_fusion.at_in.at_ref, bf16[32,192,192]{2,1,0:T(8,128)(2,1)S(1)} %shard_map.64.s_ref, bf16[32,4,72,128]{3,2,1,0:T(8,128)(2,1)S(1)} %shard_map.69.own_ref, ...), custom_call_target="tpu_custom_call" | custom-call | flops 905969664 | bytes 1048576 | tf_op jit(solution)/shard_map/pallas_call | solution.py:377
  (90 shorter events, 36.7 us)
Async XLA Ops:
  14.3 23.6 %collective-permute-start.13 = (bf16[4,8,72,128]{3,2,1,0:T(8,128)(2,1)S(1)}, bf16[4,8,72,128]{3,2,1,0:T(8,128)(2,1)S(1)}, u32[]{:S(2)}, u32[]{:S(2)}) collective-permute-start(bf16[4,8,72,128]{3,2,1,0:T(8,128)(2,1)S(1)} %get-tuple-element.16), channel_id=1, source_target_pairs={{0,32},{1,33},{2,34},{3,35},{4,36},{5,37},{6,38},{7,39},{8,40},{9,... | collective-permute-start | bytes 1769480 | tf_op jit(solution)/shard_map/ppermute | solution.py:53
  15.6 22.3 %collective-permute-start.15 = (bf16[4,8,72,128]{3,2,1,0:T(8,128)(2,1)S(1)}, bf16[4,8,72,128]{3,2,1,0:T(8,128)(2,1)S(1)}, u32[]{:S(2)}, u32[]{:S(2)}) collective-permute-start(bf16[4,8,72,128]{3,2,1,0:T(8,128)(2,1)S(1)} %add_convert_fusion.3), channel_id=1, source_target_pairs={{0,64},{1,65},{2,66},{3,67},{4,68},{5,69},{6,70},{7,71},{8,72},{9,... | collective-permute-start | bytes 1769480 | tf_op jit(solution)/shard_map/ppermute | solution.py:37
  16.4 21.5 %collective-permute-start.17 = (bf16[4,8,72,128]{3,2,1,0:T(8,128)(2,1)S(1)}, bf16[4,8,72,128]{3,2,1,0:T(8,128)(2,1)S(1)}, u32[]{:S(2)}, u32[]{:S(2)}) collective-permute-start(bf16[4,8,72,128]{3,2,1,0:T(8,128)(2,1)S(1)} %add_convert_fusion.2), channel_id=1, source_target_pairs={{0,192},{1,193},{2,194},{3,195},{4,196},{5,197},{6,198},{7,199},{8... | collective-permute-start | bytes 1769480 | tf_op jit(solution)/shard_map/ppermute | solution.py:37
  17.7 20.2 %collective-permute-start.19 = (bf16[4,8,72,128]{3,2,1,0:T(8,128)(2,1)S(1)}, bf16[4,8,72,128]{3,2,1,0:T(8,128)(2,1)S(1)}, u32[]{:S(2)}, u32[]{:S(2)}) collective-permute-start(bf16[4,8,72,128]{3,2,1,0:T(8,128)(2,1)S(1)} %add_convert_fusion.1), channel_id=1, source_target_pairs={{0,128},{1,129},{2,130},{3,131},{4,132},{5,133},{6,134},{7,135},{8... | collective-permute-start | bytes 1769480 | tf_op jit(solution)/shard_map/ppermute | solution.py:37
  32.6 9.7 %collective-permute-start.2 = (bf16[4,72,128]{2,1,0:T(8,128)(2,1)S(1)}, bf16[4,72,128]{2,1,0:T(8,128)(2,1)S(1)}, u32[]{:S(2)}, u32[]{:S(2)}) collective-permute-start(bf16[4,72,128]{2,1,0:T(8,128)(2,1)S(1)} %shard_map.68), channel_id=1, source_target_pairs={{0,4},{1,5},{2,6},{3,7},{4,0},{5,1},{6,2},{7,3},{8,12},{9,13},{10,... | collective-permute-start | bytes 221192 | tf_op jit(solution)/shard_map/ppermute | solution.py:49
  38.3 7.9 %collective-permute-start.20 = (bf16[8,72,128]{2,1,0:T(8,128)(2,1)S(1)}, bf16[8,72,128]{2,1,0:T(8,128)(2,1)S(1)}, u32[]{:S(2)}, u32[]{:S(2)}) collective-permute-start(bf16[8,72,128]{2,1,0:T(8,128)(2,1)S(1)} %get-tuple-element.23), channel_id=1, source_target_pairs={{0,1},{1,0},{2,3},{3,2},{4,5},{5,4},{6,7},{7,6},{8,9},{9,8},{10,11... | collective-permute-start | bytes 442376 | tf_op jit(solution)/shard_map/ppermute | solution.py:43
  42.5 7.8 %collective-permute-start.4 = (bf16[8,72,128]{2,1,0:T(8,128)(2,1)S(1)}, bf16[8,72,128]{2,1,0:T(8,128)(2,1)S(1)}, u32[]{:S(2)}, u32[]{:S(2)}) collective-permute-start(bf16[8,72,128]{2,1,0:T(8,128)(2,1)S(1)} %get-tuple-element.29), channel_id=1, source_target_pairs={{0,2},{1,3},{2,0},{3,1},{4,6},{5,7},{6,4},{7,5},{8,10},{9,11},{10,... | collective-permute-start | bytes 442376 | tf_op jit(solution)/shard_map/ppermute | solution.py:43
  52.3 23.5 %collective-permute-start.6 = (bf16[4,8,72,128]{3,2,1,0:T(8,128)(2,1)S(1)}, bf16[4,8,72,128]{3,2,1,0:T(8,128)(2,1)S(1)}, u32[]{:S(2)}, u32[]{:S(2)}) collective-permute-start(bf16[4,8,72,128]{3,2,1,0:T(8,128)(2,1)S(1)} %pad_maximum_fusion.rest_0_), channel_id=1, source_target_pairs={{0,64},{1,65},{2,66},{3,67},{4,68},{5,69},{6,70},{7,71},{8,72},{9,... | collective-permute-start | bytes 1769480 | tf_op jit(solution)/shard_map/ppermute | solution.py:37
  52.8 25.3 %collective-permute-start.7 = (bf16[4,8,72,128]{3,2,1,0:T(8,128)(2,1)S(1)}, bf16[4,8,72,128]{3,2,1,0:T(8,128)(2,1)S(1)}, u32[]{:S(2)}, u32[]{:S(2)}) collective-permute-start(bf16[4,8,72,128]{3,2,1,0:T(8,128)(2,1)S(1)} %pad_maximum_fusion.rest_0_), channel_id=1, source_target_pairs={{0,128},{1,129},{2,130},{3,131},{4,132},{5,133},{6,134},{7,135},{8... | collective-permute-start | bytes 1769480 | tf_op jit(solution)/shard_map/ppermute | solution.py:37
  57.2 8.2 %collective-permute-start.25 = (bf16[4,72,128]{2,1,0:T(8,128)(2,1)S(1)}, bf16[4,72,128]{2,1,0:T(8,128)(2,1)S(1)}, u32[]{:S(2)}, u32[]{:S(2)}) collective-permute-start(bf16[4,72,128]{2,1,0:T(8,128)(2,1)S(1)} %add_convert_fusion.5.d0_ref), channel_id=1, source_target_pairs={{0,20},{1,21},{2,22},{3,23},{4,16},{5,17},{6,18},{7,19},{8,28},{9,... | collective-permute-start | bytes 221192 | tf_op jit(solution)/shard_map/ppermute | solution.py:49
  57.2 32.4 %collective-permute-start.8 = (bf16[4,8,72,128]{3,2,1,0:T(8,128)(2,1)S(1)}, bf16[4,8,72,128]{3,2,1,0:T(8,128)(2,1)S(1)}, u32[]{:S(2)}, u32[]{:S(2)}) collective-permute-start(bf16[4,8,72,128]{3,2,1,0:T(8,128)(2,1)S(1)} %pad_maximum_fusion.rest_0_), channel_id=1, source_target_pairs={{0,192},{1,193},{2,194},{3,195},{4,196},{5,197},{6,198},{7,199},{8... | collective-permute-start | bytes 1769480 | tf_op jit(solution)/shard_map/ppermute | solution.py:37
  60.9 30.5 %collective-permute-start.9 = (bf16[4,8,72,128]{3,2,1,0:T(8,128)(2,1)S(1)}, bf16[4,8,72,128]{3,2,1,0:T(8,128)(2,1)S(1)}, u32[]{:S(2)}, u32[]{:S(2)}) collective-permute-start(bf16[4,8,72,128]{3,2,1,0:T(8,128)(2,1)S(1)} %pad_maximum_fusion.rest_0_), channel_id=1, source_target_pairs={{0,32},{1,33},{2,34},{3,35},{4,36},{5,37},{6,38},{7,39},{8,40},{9,... | collective-permute-start | bytes 1769480 | tf_op jit(solution)/shard_map/ppermute | solution.py:53
  75.8 10.2 %collective-permute-start.29 = (bf16[8,72,128]{2,1,0:T(8,128)(2,1)S(1)}, bf16[8,72,128]{2,1,0:T(8,128)(2,1)S(1)}, u32[]{:S(2)}, u32[]{:S(2)}) collective-permute-start(bf16[8,72,128]{2,1,0:T(8,128)(2,1)S(1)} %get-tuple-element.27), channel_id=1, source_target_pairs={{0,2},{1,3},{2,0},{3,1},{4,6},{5,7},{6,4},{7,5},{8,10},{9,11},{10,... | collective-permute-start | bytes 442376 | tf_op jit(solution)/shard_map/ppermute | solution.py:43
  78.1 10.2 %collective-permute-start.30 = (bf16[8,72,128]{2,1,0:T(8,128)(2,1)S(1)}, bf16[8,72,128]{2,1,0:T(8,128)(2,1)S(1)}, u32[]{:S(2)}, u32[]{:S(2)}) collective-permute-start(bf16[8,72,128]{2,1,0:T(8,128)(2,1)S(1)} %get-tuple-element.27), channel_id=1, source_target_pairs={{0,3},{1,2},{2,1},{3,0},{4,7},{5,6},{6,5},{7,4},{8,11},{9,10},{10,... | collective-permute-start | bytes 442376 | tf_op jit(solution)/shard_map/ppermute | solution.py:43
  80.1 12.3 %collective-permute-start.10 = (bf16[4,8,72,128]{3,2,1,0:T(8,128)(2,1)S(1)}, bf16[4,8,72,128]{3,2,1,0:T(8,128)(2,1)S(1)}, u32[]{:S(2)}, u32[]{:S(2)}) collective-permute-start(bf16[4,8,72,128]{3,2,1,0:T(8,128)(2,1)S(1)} %collective-permute-done.6.rest_1_), channel_id=1, source_target_pairs={{0,32},{1,33},{2,34},{3,35},{4,36},{5,37},{6,38},{7,39},{8,40},{9,... | collective-permute-start | bytes 1769480 | tf_op jit(solution)/shard_map/ppermute | solution.py:53
  86.0 8.9 %collective-permute-start.11 = (bf16[4,8,72,128]{3,2,1,0:T(8,128)(2,1)S(1)}, bf16[4,8,72,128]{3,2,1,0:T(8,128)(2,1)S(1)}, u32[]{:S(2)}, u32[]{:S(2)}) collective-permute-start(bf16[4,8,72,128]{3,2,1,0:T(8,128)(2,1)S(1)} %collective-permute-done.7.rest_2_), channel_id=1, source_target_pairs={{0,32},{1,33},{2,34},{3,35},{4,36},{5,37},{6,38},{7,39},{8,40},{9,... | collective-permute-start | bytes 1769480 | tf_op jit(solution)/shard_map/ppermute | solution.py:53
  88.4 9.1 %collective-permute-start.31 = (bf16[4,8,72,128]{3,2,1,0:T(8,128)(2,1)S(1)}, bf16[4,8,72,128]{3,2,1,0:T(8,128)(2,1)S(1)}, u32[]{:S(2)}, u32[]{:S(2)}) collective-permute-start(bf16[4,8,72,128]{3,2,1,0:T(8,128)(2,1)S(1)} %pad_maximum_fusion.1.rest_0_), channel_id=1, source_target_pairs={{0,64},{1,65},{2,66},{3,67},{4,68},{5,69},{6,70},{7,71},{8,72},{9,... | collective-permute-start | bytes 1769480 | tf_op jit(solution)/shard_map/ppermute | solution.py:37
  89.6 15.7 %collective-permute-start.32 = (bf16[4,8,72,128]{3,2,1,0:T(8,128)(2,1)S(1)}, bf16[4,8,72,128]{3,2,1,0:T(8,128)(2,1)S(1)}, u32[]{:S(2)}, u32[]{:S(2)}) collective-permute-start(bf16[4,8,72,128]{3,2,1,0:T(8,128)(2,1)S(1)} %pad_maximum_fusion.1.rest_0_), channel_id=1, source_target_pairs={{0,128},{1,129},{2,130},{3,131},{4,132},{5,133},{6,134},{7,135},{8... | collective-permute-start | bytes 1769480 | tf_op jit(solution)/shard_map/ppermute | solution.py:37
  91.4 16.6 %collective-permute-start.33 = (bf16[4,8,72,128]{3,2,1,0:T(8,128)(2,1)S(1)}, bf16[4,8,72,128]{3,2,1,0:T(8,128)(2,1)S(1)}, u32[]{:S(2)}, u32[]{:S(2)}) collective-permute-start(bf16[4,8,72,128]{3,2,1,0:T(8,128)(2,1)S(1)} %pad_maximum_fusion.1.rest_0_), channel_id=1, source_target_pairs={{0,192},{1,193},{2,194},{3,195},{4,196},{5,197},{6,198},{7,199},{8... | collective-permute-start | bytes 1769480 | tf_op jit(solution)/shard_map/ppermute | solution.py:37
  92.4 21.3 %collective-permute-start.12 = (bf16[4,8,72,128]{3,2,1,0:T(8,128)(2,1)S(1)}, bf16[4,8,72,128]{3,2,1,0:T(8,128)(2,1)S(1)}, u32[]{:S(2)}, u32[]{:S(2)}) collective-permute-start(bf16[4,8,72,128]{3,2,1,0:T(8,128)(2,1)S(1)} %collective-permute-done.8.rest_3_), channel_id=1, source_target_pairs={{0,32},{1,33},{2,34},{3,35},{4,36},{5,37},{6,38},{7,39},{8,40},{9,... | collective-permute-start | bytes 1769480 | tf_op jit(solution)/shard_map/ppermute | solution.py:53
  94.9 22.8 %collective-permute-start.34 = (bf16[4,8,72,128]{3,2,1,0:T(8,128)(2,1)S(1)}, bf16[4,8,72,128]{3,2,1,0:T(8,128)(2,1)S(1)}, u32[]{:S(2)}, u32[]{:S(2)}) collective-permute-start(bf16[4,8,72,128]{3,2,1,0:T(8,128)(2,1)S(1)} %pad_maximum_fusion.1.rest_0_), channel_id=1, source_target_pairs={{0,32},{1,33},{2,34},{3,35},{4,36},{5,37},{6,38},{7,39},{8,40},{9,... | collective-permute-start | bytes 1769480 | tf_op jit(solution)/shard_map/ppermute | solution.py:53
  97.5 20.1 %collective-permute-start.35 = (bf16[4,8,72,128]{3,2,1,0:T(8,128)(2,1)S(1)}, bf16[4,8,72,128]{3,2,1,0:T(8,128)(2,1)S(1)}, u32[]{:S(2)}, u32[]{:S(2)}) collective-permute-start(bf16[4,8,72,128]{3,2,1,0:T(8,128)(2,1)S(1)} %collective-permute-done.31.rest_1_), channel_id=1, source_target_pairs={{0,32},{1,33},{2,34},{3,35},{4,36},{5,37},{6,38},{7,39},{8,40},{9,... | collective-permute-start | bytes 1769480 | tf_op jit(solution)/shard_map/ppermute | solution.py:53
  105.3 12.4 %collective-permute-start.36 = (bf16[4,8,72,128]{3,2,1,0:T(8,128)(2,1)S(1)}, bf16[4,8,72,128]{3,2,1,0:T(8,128)(2,1)S(1)}, u32[]{:S(2)}, u32[]{:S(2)}) collective-permute-start(bf16[4,8,72,128]{3,2,1,0:T(8,128)(2,1)S(1)} %collective-permute-done.32.rest_2_), channel_id=1, source_target_pairs={{0,32},{1,33},{2,34},{3,35},{4,36},{5,37},{6,38},{7,39},{8,40},{9,... | collective-permute-start | bytes 1769480 | tf_op jit(solution)/shard_map/ppermute | solution.py:53
  107.9 9.8 %collective-permute-start.37 = (bf16[4,8,72,128]{3,2,1,0:T(8,128)(2,1)S(1)}, bf16[4,8,72,128]{3,2,1,0:T(8,128)(2,1)S(1)}, u32[]{:S(2)}, u32[]{:S(2)}) collective-permute-start(bf16[4,8,72,128]{3,2,1,0:T(8,128)(2,1)S(1)} %collective-permute-done.33.rest_3_), channel_id=1, source_target_pairs={{0,32},{1,33},{2,34},{3,35},{4,36},{5,37},{6,38},{7,39},{8,40},{9,... | collective-permute-start | bytes 1769480 | tf_op jit(solution)/shard_map/ppermute | solution.py:53
  (20 other events, 129.6 us)

commit v4 on v3

--- a/solution.py
+++ b/solution.py
@@ -1,3 +1,4 @@
+import functools
 import jax
 import jax.numpy as jnp
 from jax import lax
@@ -329,9 +330,10 @@
     )(*parts, *near)
 
 
-def finish_kernel(ends_in, rank_in, at_in, s_ref, own_ref, base_ref, *rest):
-    group_refs, out_ref, held_ref = rest[:8], rest[8], rest[9]
-    flat_ref, left_ref, right_ref, rows_ref, sem, ends_ref, rank_ref, at_ref, facts_sem = rest[10:]
+def finish_kernel(ends_in, rank_in, at_in, s_ref, own_ref, base_ref, *rest, count):
+    group_refs, rest = rest[:count], rest[count:]
+    out_ref, held_ref = rest[:2]
+    flat_ref, left_ref, right_ref, rows_ref, sem, ends_ref, rank_ref, at_ref, facts_sem = rest[2:]
     groups = s_ref.shape[0] // 8
     copies = [
         pltpu.make_async_copy(a, b, facts_sem.at[n])
@@ -339,8 +341,11 @@
     ]
     for copy in copies:
         copy.start()
-    for n in range(8):
-        held_ref[n * 32 : (n + 1) * 32] = group_refs[n][...].reshape(32, QP, 128)
+    at_slot = 0
+    for ref in group_refs:
+        slots = ref.shape[0] * ref.shape[1]
+        held_ref[at_slot : at_slot + slots] = ref[...].reshape(slots, QP, 128)
+        at_slot += slots
     right_ref[...] = jnp.zeros_like(right_ref)
     for copy in copies:
         copy.wait()
@@ -375,8 +380,8 @@
 def finish(ends, rank, at, s, own, base, groups):
     pairs = s.shape[0]
     return call(
-        finish_kernel,
-        [ANY] * 3 + [VMEM] * 11,
+        functools.partial(finish_kernel, count=len(groups)),
+        [ANY] * 3 + [VMEM] * (3 + len(groups)),
         jax.ShapeDtypeStruct((pairs, R * R), BF16),
         HBM,
         [
@@ -402,13 +407,15 @@
     return total.astype(BF16)
 
 
-def sent_to_all(mine):
+def sent_to_all(mine, tag):
     both = jnp.concatenate([mine, stage_z(mine, 1)], axis=0)
     group = [both] + [stage_b(both, d) for d in (1, 2, 3)]
     group = jnp.stack(group, axis=0)
-    groups = [group] + [stage_a(group, d) for d in (2, 1, 3)]
-    groups = [groups[0], groups[2], groups[1], groups[3]]
-    return groups + [stage_c(groups[n]) for n in range(4)]
+    cuts = [(1, 0, 4), (2, 0, 4), (3, 0, 4)] if tag == "x" else [(1, 0, 4), (2, 0, 2), (2, 2, 4), (3, 0, 4)]
+    groups = [group]
+    for d, low, high in cuts:
+        groups.append(stage_a(group[low:high], d))
+    return groups + [stage_c(g) for g in groups]
 
 
 def whole_step(pair_list, rank_bucket, amplitudes, intersects, integrals, exchange_blocks):
@@ -420,7 +427,7 @@
     far = stage_z(pair, EVEN[3])
     near = [pair[0], pair[1], far[1], far[0]]
     quarters = choose(at, near)
-    blocks = sent_to_all(quarters)
+    blocks = sent_to_all(quarters, "x")
 
     m = relay(amplitudes)
     s = relay(intersects)
@@ -437,7 +444,7 @@
     near[0] = copied(near[0])
     coupled = couple(parts, near)
     own = own_of(ends, at, p, blocks)
-    groups = sent_to_all(coupled)
+    groups = sent_to_all(coupled, "g")
     return finish(ends, rank_bucket, at, s, own, base, groups)
 
 

time: 124 us -> 123 us (level)
  waiting for transfers between devices: 34.4 us -> 31.8 us
  starting transfers between devices: 62 us -> 63.4 us
    ppermute x8, starting transfers between devices: 14.7 us -> 17 us  [stage_z(): lax.ppermute(array, AXES, pairs_of(lambda x, c, z, y: (x, c, z ^ d, y)))]
    ppermute x8, waiting for transfers between devices: 17.1 us -> 15.6 us  [stage_z(): lax.ppermute(array, AXES, pairs_of(lambda x, c, z, y: (x, c, z ^ d, y)))]
    ppermute x12 -> x13, starting transfers between devices: 24.1 us -> 23.2 us  [stage_c(): lax.ppermute(array, AXES, pairs_of(lambda x, c, z, y: (x, c ^ 1, z, y)))]
    ppermute x9 -> x10, starting transfers between devices: 11.3 us -> 12 us  [stage_a(): lax.ppermute(array, AXES, pairs_of(lambda x, c, z, y: (x ^ d, c, z, y) if...]
    ppermute x9 -> x10, waiting for transfers between devices: 9.52 us -> 8.91 us  [stage_a(): lax.ppermute(array, AXES, pairs_of(lambda x, c, z, y: (x ^ d, c, z, y) if...]
  transfers between devices with their start and end apart: 38 -> 40, of which waited for: 15 -> 13; matrix products, arithmetic and copies ran while one was open for 1% -> 1% of each run, Pallas kernels for 8% -> 8%
where the time goes in v4:
time: 123 us
  starting transfers between devices  63.4 us (52%)
  waiting for transfers between devices  31.8 us (26%)
  Pallas kernels  24 us (20%)
  local copies, waits for them, and re-layouts  1.75 us (1%)
  other arithmetic  1.34 us (1%)
    ppermute x13, starting transfers between devices, stage_c(): lax.ppermute(array, AXES, pairs_of(lambda x, c, z, y: (x, c ^ 1, z, y)))  23.2 us
    ppermute x8, starting transfers between devices, stage_z(): lax.ppermute(array, AXES, pairs_of(lambda x, c, z, y: (x, c, z ^ d, y)))  17 us
    ppermute x8, waiting for transfers between devices, stage_z(): lax.ppermute(array, AXES, pairs_of(lambda x, c, z, y: (x, c, z ^ d, y)))  15.6 us
    ppermute x10, starting transfers between devices, stage_a(): lax.ppermute(array, AXES, pairs_of(lambda x, c, z, y: (x ^ d, c, z, y) if...  12 us
    ppermute x9, starting transfers between devices, stage_b(): lax.ppermute(array, AXES, pairs_of(lambda x, c, z, y: (x, c, z, y ^ d) if...  11.2 us
    ppermute x10, waiting for transfers between devices, stage_a(): lax.ppermute(array, AXES, pairs_of(lambda x, c, z, y: (x ^ d, c, z, y) if...  8.91 us
    pallas_call x1, Pallas kernels, finish(): call(functools.partial(finish_kernel, count=len(groups)), [ANY] * 3 + [VM...  5.91 us
    pallas_call x3, Pallas kernels, relay(): call(relay_kernel, [VMEM], jax.ShapeDtypeStruct((pairs, R, R), BF16), VME...  5.81 us
  transfers between devices with their start and end apart: 40, of which 13 were waited for; matrix products, arithmetic and copies ran while one was open for 1% of the time, Pallas kernels for 8%

profile of v4, /device:TPU:1, one launch (start us, length us, event | category | flops | bytes accessed | tf_op | source)
XLA Modules:
  0.0 122.7 jit_solution(14003425631076877433)
XLA Ops:
  3.6 1.9 %shard_map.65.m_ref = bf16[32,192,192]{2,1,0:T(8,128)(2,1)S(1)} custom-call(bf16[32,36864]{1,0:T(8,128)(2,1)S(1)} %copy-done.1), custom_call_target="tpu_custom_call" | custom-call | flops 16777216 | bytes 1048576 | tf_op jit(solution)/shard_map/pallas_call | solution.py:144
  5.7 4.8 %shard_map.66 = (bf16[32,192,192]{2,1,0:T(8,128)(2,1)S(1)}, bf16[4,8,72,128]{3,2,1,0:T(8,128)(2,1)S(1)}, bf16[4,8,72,128]{3,2,1,0:T(8,128)(2,1)S(1)}, bf16[4,8,7...) custom-call(s32[2,32]{1,0:T(2,128)S(1)} %bitcast.34, ...), custom_call_target="tpu_custom_call" | custom-call | flops 905969664 | bytes 1048576 | tf_op jit(solution)/shard_map/pallas_call | solution.py:253
  10.5 3.3 %collective-permute-start.14 = (bf16[4,8,72,128]{3,2,1,0:T(8,128)(2,1)S(1)}, bf16[4,8,72,128]{3,2,1,0:T(8,128)(2,1)S(1)}, u32[]{:S(2)}, u32[]{:S(2)}) collective-permute-start(bf16[4,8,72,128]{3,2,1,0:T(8,128)(2,1)S(1)} %get-tuple-element.18), channel_id=1, source_target_pairs={{0,32},{1,33},{2,34},{3,35},{4,36},{5,37},{6,38},{7,39},{8,40},{9,... | collective-permute-start | bytes 1769480 | tf_op jit(solution)/shard_map/ppermute | solution.py:54
  19.6 3.5 %collective-permute-start = (bf16[4,72,128]{2,1,0:T(8,128)(2,1)S(1)}, bf16[4,72,128]{2,1,0:T(8,128)(2,1)S(1)}, u32[]{:S(2)}, u32[]{:S(2)}) collective-permute-start(bf16[4,72,128]{2,1,0:T(8,128)(2,1)S(1)} %shard_map.67.refs_0_.x_ref), channel_id=1, source_target_pairs={{0,12},{1,13},{2,14},{3,15},{4,8},{5,9},{6,10},{7,11},{8,4},{9,5},... | collective-permute-start | bytes 221192 | tf_op jit(solution)/shard_map/ppermute | solution.py:50
  25.0 3.4 %collective-permute-start.1 = (bf16[2,4,72,128]{3,2,1,0:T(8,128)(2,1)S(1)}, bf16[2,4,72,128]{3,2,1,0:T(8,128)(2,1)S(1)}, u32[]{:S(2)}, u32[]{:S(2)}) collective-permute-start(bf16[2,4,72,128]{3,2,1,0:T(8,128)(2,1)S(1)} %pad_maximum_fusion.4), channel_id=1, source_target_pairs={{0,24},{1,25},{2,26},{3,27},{4,28},{5,29},{6,30},{7,31},{8,16},{9,... | collective-permute-start | bytes 442376 | tf_op jit(solution)/shard_map/ppermute | solution.py:50
  28.5 3.5 %collective-permute-done.1 = bf16[2,4,72,128]{3,2,1,0:T(8,128)(2,1)S(1)} collective-permute-done((bf16[2,4,72,128]{3,2,1,0:T(8,128)(2,1)S(1)}, bf16[2,4,72,128]{3,2,1,0:T(8,128)(2,1)S(1)}, u32[]{:S(2)}, u32[]{:S(2)}) %collective-permute-start.1) | collective-permute-done | bytes 147488 | tf_op jit(solution)/shard_map/ppermute | solution.py:50
  32.6 5.3 %collective-permute-start.2 = (bf16[4,72,128]{2,1,0:T(8,128)(2,1)S(1)}, bf16[4,72,128]{2,1,0:T(8,128)(2,1)S(1)}, u32[]{:S(2)}, u32[]{:S(2)}) collective-permute-start(bf16[4,72,128]{2,1,0:T(8,128)(2,1)S(1)} %shard_map.68), channel_id=1, source_target_pairs={{0,4},{1,5},{2,6},{3,7},{4,0},{5,1},{6,2},{7,3},{8,12},{9,13},{10,... | collective-permute-start | bytes 221192 | tf_op jit(solution)/shard_map/ppermute | solution.py:50
  39.8 2.5 %collective-permute-start.21 = (bf16[8,72,128]{2,1,0:T(8,128)(2,1)S(1)}, bf16[8,72,128]{2,1,0:T(8,128)(2,1)S(1)}, u32[]{:S(2)}, u32[]{:S(2)}) collective-permute-start(bf16[8,72,128]{2,1,0:T(8,128)(2,1)S(1)} %get-tuple-element.25), channel_id=1, source_target_pairs={{0,2},{1,3},{2,0},{3,1},{4,6},{5,7},{6,4},{7,5},{8,10},{9,11},{10,... | collective-permute-start | bytes 442376 | tf_op jit(solution)/shard_map/ppermute | solution.py:44
  42.5 3.7 %collective-permute-start.4 = (bf16[8,72,128]{2,1,0:T(8,128)(2,1)S(1)}, bf16[8,72,128]{2,1,0:T(8,128)(2,1)S(1)}, u32[]{:S(2)}, u32[]{:S(2)}) collective-permute-start(bf16[8,72,128]{2,1,0:T(8,128)(2,1)S(1)} %get-tuple-element.29), channel_id=1, source_target_pairs={{0,2},{1,3},{2,0},{3,1},{4,6},{5,7},{6,4},{7,5},{8,10},{9,11},{10,... | collective-permute-start | bytes 442376 | tf_op jit(solution)/shard_map/ppermute | solution.py:44
  52.8 2.8 %collective-permute-start.7 = (bf16[4,8,72,128]{3,2,1,0:T(8,128)(2,1)S(1)}, bf16[4,8,72,128]{3,2,1,0:T(8,128)(2,1)S(1)}, u32[]{:S(2)}, u32[]{:S(2)}) collective-permute-start(bf16[4,8,72,128]{3,2,1,0:T(8,128)(2,1)S(1)} %pad_maximum_fusion.rest_0_), channel_id=1, source_target_pairs={{0,128},{1,129},{2,130},{3,131},{4,132},{5,133},{6,134},{7,135},{8... | collective-permute-start | bytes 1769480 | tf_op jit(solution)/shard_map/ppermute | solution.py:38
  56.2 2.1 %collective-permute-start.24 = (bf16[4,72,128]{2,1,0:T(8,128)(2,1)S(1)}, bf16[4,72,128]{2,1,0:T(8,128)(2,1)S(1)}, u32[]{:S(2)}, u32[]{:S(2)}) collective-permute-start(bf16[4,72,128]{2,1,0:T(8,128)(2,1)S(1)} %add_convert_fusion.5.d0_ref), channel_id=1, source_target_pairs={{0,12},{1,13},{2,14},{3,15},{4,8},{5,9},{6,10},{7,11},{8,4},{9,5},... | collective-permute-start | bytes 221192 | tf_op jit(solution)/shard_map/ppermute | solution.py:50
  58.3 3.1 %collective-permute-done.24.d1_ref = bf16[4,72,128]{2,1,0:T(8,128)(2,1)S(1)} collective-permute-done((bf16[4,72,128]{2,1,0:T(8,128)(2,1)S(1)}, bf16[4,72,128]{2,1,0:T(8,128)(2,1)S(1)}, u32[]{:S(2)}, u32[]{:S(2)}) %collective-permute-start.24) | collective-permute-done | bytes 73760 | tf_op jit(solution)/shard_map/ppermute | solution.py:50
  61.4 4.1 %collective-permute-start.9 = (bf16[4,8,72,128]{3,2,1,0:T(8,128)(2,1)S(1)}, bf16[4,8,72,128]{3,2,1,0:T(8,128)(2,1)S(1)}, u32[]{:S(2)}, u32[]{:S(2)}) collective-permute-start(bf16[4,8,72,128]{3,2,1,0:T(8,128)(2,1)S(1)} %pad_maximum_fusion.rest_0_), channel_id=1, source_target_pairs={{0,32},{1,33},{2,34},{3,35},{4,36},{5,37},{6,38},{7,39},{8,40},{9,... | collective-permute-start | bytes 1769480 | tf_op jit(solution)/shard_map/ppermute | solution.py:54
  66.3 4.8 %collective-permute-done.26.d3_ref = bf16[4,72,128]{2,1,0:T(8,128)(2,1)S(1)} collective-permute-done((bf16[4,72,128]{2,1,0:T(8,128)(2,1)S(1)}, bf16[4,72,128]{2,1,0:T(8,128)(2,1)S(1)}, u32[]{:S(2)}, u32[]{:S(2)}) %collective-permute-start.26) | collective-permute-done | bytes 73760 | tf_op jit(solution)/shard_map/ppermute | solution.py:50
  73.1 2.4 %collective-permute-done.27 = bf16[4,72,128]{2,1,0:T(8,128)(2,1)S(1)} collective-permute-done((bf16[4,72,128]{2,1,0:T(8,128)(2,1)S(1)}, bf16[4,72,128]{2,1,0:T(8,128)(2,1)S(1)}, u32[]{:S(2)}, u32[]{:S(2)}) %collective-permute-start.27) | collective-permute-done | bytes 73760 | tf_op jit(solution)/shard_map/ppermute | solution.py:50
  75.5 2.4 %collective-permute-start.29 = (bf16[8,72,128]{2,1,0:T(8,128)(2,1)S(1)}, bf16[8,72,128]{2,1,0:T(8,128)(2,1)S(1)}, u32[]{:S(2)}, u32[]{:S(2)}) collective-permute-start(bf16[8,72,128]{2,1,0:T(8,128)(2,1)S(1)} %get-tuple-element.27), channel_id=1, source_target_pairs={{0,2},{1,3},{2,0},{3,1},{4,6},{5,7},{6,4},{7,5},{8,10},{9,11},{10,... | collective-permute-start | bytes 442376 | tf_op jit(solution)/shard_map/ppermute | solution.py:44
  78.8 5.5 %collective-permute-start.10 = (bf16[4,8,72,128]{3,2,1,0:T(8,128)(2,1)S(1)}, bf16[4,8,72,128]{3,2,1,0:T(8,128)(2,1)S(1)}, u32[]{:S(2)}, u32[]{:S(2)}) collective-permute-start(bf16[4,8,72,128]{3,2,1,0:T(8,128)(2,1)S(1)} %collective-permute-done.6.rest_1_), channel_id=1, source_target_pairs={{0,32},{1,33},{2,34},{3,35},{4,36},{5,37},{6,38},{7,39},{8,40},{9,... | collective-permute-start | bytes 1769480 | tf_op jit(solution)/shard_map/ppermute | solution.py:54
  84.3 3.0 %collective-permute-start.11 = (bf16[4,8,72,128]{3,2,1,0:T(8,128)(2,1)S(1)}, bf16[4,8,72,128]{3,2,1,0:T(8,128)(2,1)S(1)}, u32[]{:S(2)}, u32[]{:S(2)}) collective-permute-start(bf16[4,8,72,128]{3,2,1,0:T(8,128)(2,1)S(1)} %collective-permute-done.7.rest_2_), channel_id=1, source_target_pairs={{0,32},{1,33},{2,34},{3,35},{4,36},{5,37},{6,38},{7,39},{8,40},{9,... | collective-permute-start | bytes 1769480 | tf_op jit(solution)/shard_map/ppermute | solution.py:54
  95.9 2.1 %collective-permute-done.31.rest_1_ = bf16[4,8,72,128]{3,2,1,0:T(8,128)(2,1)S(1)} collective-permute-done((bf16[4,8,72,128]{3,2,1,0:T(8,128)(2,1)S(1)}, bf16[4,8,72,128]{3,2,1,0:T(8,128)(2,1)S(1)}, u32[]{:S(2)}, u32[]{:S(2)}) %collective-permute-start.31) | collective-permute-done | bytes 589856 | tf_op jit(solution)/shard_map/ppermute | solution.py:38
  99.4 6.8 %collective-permute-done.34.rest_4_ = bf16[4,8,72,128]{3,2,1,0:T(8,128)(2,1)S(1)} collective-permute-done((bf16[4,8,72,128]{3,2,1,0:T(8,128)(2,1)S(1)}, bf16[4,8,72,128]{3,2,1,0:T(8,128)(2,1)S(1)}, u32[]{:S(2)}, u32[]{:S(2)}) %collective-permute-start.34) | collective-permute-done | bytes 589856 | tf_op jit(solution)/shard_map/ppermute | solution.py:38
  108.2 1.9 %shard_map.70.v_ref = bf16[32,192,192]{2,1,0:T(8,128)(2,1)S(1)} custom-call(bf16[32,36864]{1,0:T(8,128)(2,1)S(1)} %copy-done.2), custom_call_target="tpu_custom_call" | custom-call | flops 16777216 | bytes 1048576 | tf_op jit(solution)/shard_map/pallas_call | solution.py:144
  110.1 2.4 %shard_map.71.base_ref = f32[32,192,192]{2,1,0:T(8,128)S(1)} custom-call(s32[32]{0:T(128)S(1)} %copy-done.4, bf16[32,192,192]{2,1,0:T(8,128)(2,1)S(1)} %shard_map.65.m_ref, bf16[32,192,192]{2,1,0:T(8,128)(2,1)S(1)} %shard_map.70.v_ref), custom_call_target="tpu_custom_call" | custom-call | flops 452984832 | bytes 1048576 | tf_op jit(solution)/shard_map/pallas_call | solution.py:276
  112.5 4.0 %shard_map.69.own_ref = bf16[32,4,72,128]{3,2,1,0:T(8,128)(2,1)S(1)} custom-call(s32[2,32]{1,0:T(2,128)S(1)} %bitcast.35, s32[4]{0:T(128)S(1)} %pad_add_fusion.at_in.at_ref, bf16[32,192,192]{2,1,0:T(8,128)(2,1)S(1)} %get-tuple-element.14.p_ref, bf16[4,8,72,128]{3,2,1,0:T(8,128)(2,1)S(1)} %pad_maximum_fusion.rest_0_, ...), custom_call_target="tpu_custom_call" | custom-call | flops 452984832 | bytes 1048576 | tf_op jit(solution)/shard_map/pallas_call | solution.py:307
  116.6 5.9 %shard_map.74 = bf16[32,36864]{1,0:T(8,128)(2,1)} custom-call(s32[2,32]{1,0:T(2,128)S(1)} %bitcast.36, s32[32]{0:T(128)S(1)} %copy-done.4, s32[4]{0:T(128)S(1)} %pad_add_fusion.at_in.at_ref, bf16[32,192,192]{2,1,0:T(8,128)(2,1)S(1)} %shard_map.64.s_ref, bf16[32,4,72,128]{3,2,1,0:T(8,128)(2,1)S(1)} %shard_map.69.own_ref, ...), custom_call_target="tpu_custom_call" | custom-call | flops 905969664 | bytes 1048576 | tf_op jit(solution)/shard_map/pallas_call | solution.py:382
  (96 shorter events, 37.1 us)
Async XLA Ops:
  14.3 23.6 %collective-permute-start.13 = (bf16[4,8,72,128]{3,2,1,0:T(8,128)(2,1)S(1)}, bf16[4,8,72,128]{3,2,1,0:T(8,128)(2,1)S(1)}, u32[]{:S(2)}, u32[]{:S(2)}) collective-permute-start(bf16[4,8,72,128]{3,2,1,0:T(8,128)(2,1)S(1)} %get-tuple-element.16), channel_id=1, source_target_pairs={{0,32},{1,33},{2,34},{3,35},{4,36},{5,37},{6,38},{7,39},{8,40},{9,... | collective-permute-start | bytes 1769480 | tf_op jit(solution)/shard_map/ppermute | solution.py:54
  15.6 22.3 %collective-permute-start.15 = (bf16[4,8,72,128]{3,2,1,0:T(8,128)(2,1)S(1)}, bf16[4,8,72,128]{3,2,1,0:T(8,128)(2,1)S(1)}, u32[]{:S(2)}, u32[]{:S(2)}) collective-permute-start(bf16[4,8,72,128]{3,2,1,0:T(8,128)(2,1)S(1)} %add_convert_fusion.3), channel_id=1, source_target_pairs={{0,64},{1,65},{2,66},{3,67},{4,68},{5,69},{6,70},{7,71},{8,72},{9,... | collective-permute-start | bytes 1769480 | tf_op jit(solution)/shard_map/ppermute | solution.py:38
  16.4 21.5 %collective-permute-start.17 = (bf16[4,8,72,128]{3,2,1,0:T(8,128)(2,1)S(1)}, bf16[4,8,72,128]{3,2,1,0:T(8,128)(2,1)S(1)}, u32[]{:S(2)}, u32[]{:S(2)}) collective-permute-start(bf16[4,8,72,128]{3,2,1,0:T(8,128)(2,1)S(1)} %add_convert_fusion.2), channel_id=1, source_target_pairs={{0,192},{1,193},{2,194},{3,195},{4,196},{5,197},{6,198},{7,199},{8... | collective-permute-start | bytes 1769480 | tf_op jit(solution)/shard_map/ppermute | solution.py:38
  17.7 20.2 %collective-permute-start.19 = (bf16[4,8,72,128]{3,2,1,0:T(8,128)(2,1)S(1)}, bf16[4,8,72,128]{3,2,1,0:T(8,128)(2,1)S(1)}, u32[]{:S(2)}, u32[]{:S(2)}) collective-permute-start(bf16[4,8,72,128]{3,2,1,0:T(8,128)(2,1)S(1)} %add_convert_fusion.1), channel_id=1, source_target_pairs={{0,128},{1,129},{2,130},{3,131},{4,132},{5,133},{6,134},{7,135},{8... | collective-permute-start | bytes 1769480 | tf_op jit(solution)/shard_map/ppermute | solution.py:38
  32.6 9.7 %collective-permute-start.2 = (bf16[4,72,128]{2,1,0:T(8,128)(2,1)S(1)}, bf16[4,72,128]{2,1,0:T(8,128)(2,1)S(1)}, u32[]{:S(2)}, u32[]{:S(2)}) collective-permute-start(bf16[4,72,128]{2,1,0:T(8,128)(2,1)S(1)} %shard_map.68), channel_id=1, source_target_pairs={{0,4},{1,5},{2,6},{3,7},{4,0},{5,1},{6,2},{7,3},{8,12},{9,13},{10,... | collective-permute-start | bytes 221192 | tf_op jit(solution)/shard_map/ppermute | solution.py:50
  48.3 7.9 %collective-permute-start.23 = (bf16[4,72,128]{2,1,0:T(8,128)(2,1)S(1)}, bf16[4,72,128]{2,1,0:T(8,128)(2,1)S(1)}, u32[]{:S(2)}, u32[]{:S(2)}) collective-permute-start(bf16[4,72,128]{2,1,0:T(8,128)(2,1)S(1)} %slice.43), channel_id=1, source_target_pairs={{0,4},{1,5},{2,6},{3,7},{4,0},{5,1},{6,2},{7,3},{8,12},{9,13},{10,... | collective-permute-start | bytes 221192 | tf_op jit(solution)/shard_map/ppermute | solution.py:50
  52.3 25.6 %collective-permute-start.6 = (bf16[4,8,72,128]{3,2,1,0:T(8,128)(2,1)S(1)}, bf16[4,8,72,128]{3,2,1,0:T(8,128)(2,1)S(1)}, u32[]{:S(2)}, u32[]{:S(2)}) collective-permute-start(bf16[4,8,72,128]{3,2,1,0:T(8,128)(2,1)S(1)} %pad_maximum_fusion.rest_0_), channel_id=1, source_target_pairs={{0,64},{1,65},{2,66},{3,67},{4,68},{5,69},{6,70},{7,71},{8,72},{9,... | collective-permute-start | bytes 1769480 | tf_op jit(solution)/shard_map/ppermute | solution.py:38
  52.8 25.4 %collective-permute-start.7 = (bf16[4,8,72,128]{3,2,1,0:T(8,128)(2,1)S(1)}, bf16[4,8,72,128]{3,2,1,0:T(8,128)(2,1)S(1)}, u32[]{:S(2)}, u32[]{:S(2)}) collective-permute-start(bf16[4,8,72,128]{3,2,1,0:T(8,128)(2,1)S(1)} %pad_maximum_fusion.rest_0_), channel_id=1, source_target_pairs={{0,128},{1,129},{2,130},{3,131},{4,132},{5,133},{6,134},{7,135},{8... | collective-permute-start | bytes 1769480 | tf_op jit(solution)/shard_map/ppermute | solution.py:38
  55.7 23.2 %collective-permute-start.8 = (bf16[4,8,72,128]{3,2,1,0:T(8,128)(2,1)S(1)}, bf16[4,8,72,128]{3,2,1,0:T(8,128)(2,1)S(1)}, u32[]{:S(2)}, u32[]{:S(2)}) collective-permute-start(bf16[4,8,72,128]{3,2,1,0:T(8,128)(2,1)S(1)} %pad_maximum_fusion.rest_0_), channel_id=1, source_target_pairs={{0,192},{1,193},{2,194},{3,195},{4,196},{5,197},{6,198},{7,199},{8... | collective-permute-start | bytes 1769480 | tf_op jit(solution)/shard_map/ppermute | solution.py:38
  61.4 28.2 %collective-permute-start.9 = (bf16[4,8,72,128]{3,2,1,0:T(8,128)(2,1)S(1)}, bf16[4,8,72,128]{3,2,1,0:T(8,128)(2,1)S(1)}, u32[]{:S(2)}, u32[]{:S(2)}) collective-permute-start(bf16[4,8,72,128]{3,2,1,0:T(8,128)(2,1)S(1)} %pad_maximum_fusion.rest_0_), channel_id=1, source_target_pairs={{0,32},{1,33},{2,34},{3,35},{4,36},{5,37},{6,38},{7,39},{8,40},{9,... | collective-permute-start | bytes 1769480 | tf_op jit(solution)/shard_map/ppermute | solution.py:54
  75.5 8.8 %collective-permute-start.29 = (bf16[8,72,128]{2,1,0:T(8,128)(2,1)S(1)}, bf16[8,72,128]{2,1,0:T(8,128)(2,1)S(1)}, u32[]{:S(2)}, u32[]{:S(2)}) collective-permute-start(bf16[8,72,128]{2,1,0:T(8,128)(2,1)S(1)} %get-tuple-element.27), channel_id=1, source_target_pairs={{0,2},{1,3},{2,0},{3,1},{4,6},{5,7},{6,4},{7,5},{8,10},{9,11},{10,... | collective-permute-start | bytes 442376 | tf_op jit(solution)/shard_map/ppermute | solution.py:44
  77.9 9.5 %collective-permute-start.30 = (bf16[8,72,128]{2,1,0:T(8,128)(2,1)S(1)}, bf16[8,72,128]{2,1,0:T(8,128)(2,1)S(1)}, u32[]{:S(2)}, u32[]{:S(2)}) collective-permute-start(bf16[8,72,128]{2,1,0:T(8,128)(2,1)S(1)} %get-tuple-element.27), channel_id=1, source_target_pairs={{0,3},{1,2},{2,1},{3,0},{4,7},{5,6},{6,5},{7,4},{8,11},{9,10},{10,... | collective-permute-start | bytes 442376 | tf_op jit(solution)/shard_map/ppermute | solution.py:44
  78.3 10.6 %collective-permute-start.28 = (bf16[8,72,128]{2,1,0:T(8,128)(2,1)S(1)}, bf16[8,72,128]{2,1,0:T(8,128)(2,1)S(1)}, u32[]{:S(2)}, u32[]{:S(2)}) collective-permute-start(bf16[8,72,128]{2,1,0:T(8,128)(2,1)S(1)} %get-tuple-element.27), channel_id=1, source_target_pairs={{0,1},{1,0},{2,3},{3,2},{4,5},{5,4},{6,7},{7,6},{8,9},{9,8},{10,11... | collective-permute-start | bytes 442376 | tf_op jit(solution)/shard_map/ppermute | solution.py:44
  78.8 12.3 %collective-permute-start.10 = (bf16[4,8,72,128]{3,2,1,0:T(8,128)(2,1)S(1)}, bf16[4,8,72,128]{3,2,1,0:T(8,128)(2,1)S(1)}, u32[]{:S(2)}, u32[]{:S(2)}) collective-permute-start(bf16[4,8,72,128]{3,2,1,0:T(8,128)(2,1)S(1)} %collective-permute-done.6.rest_1_), channel_id=1, source_target_pairs={{0,32},{1,33},{2,34},{3,35},{4,36},{5,37},{6,38},{7,39},{8,40},{9,... | collective-permute-start | bytes 1769480 | tf_op jit(solution)/shard_map/ppermute | solution.py:54
  84.3 8.7 %collective-permute-start.11 = (bf16[4,8,72,128]{3,2,1,0:T(8,128)(2,1)S(1)}, bf16[4,8,72,128]{3,2,1,0:T(8,128)(2,1)S(1)}, u32[]{:S(2)}, u32[]{:S(2)}) collective-permute-start(bf16[4,8,72,128]{3,2,1,0:T(8,128)(2,1)S(1)} %collective-permute-done.7.rest_2_), channel_id=1, source_target_pairs={{0,32},{1,33},{2,34},{3,35},{4,36},{5,37},{6,38},{7,39},{8,40},{9,... | collective-permute-start | bytes 1769480 | tf_op jit(solution)/shard_map/ppermute | solution.py:54
  88.9 9.1 %collective-permute-start.31 = (bf16[4,8,72,128]{3,2,1,0:T(8,128)(2,1)S(1)}, bf16[4,8,72,128]{3,2,1,0:T(8,128)(2,1)S(1)}, u32[]{:S(2)}, u32[]{:S(2)}) collective-permute-start(bf16[4,8,72,128]{3,2,1,0:T(8,128)(2,1)S(1)} %pad_maximum_fusion.1.rest_0_), channel_id=1, source_target_pairs={{0,64},{1,65},{2,66},{3,67},{4,68},{5,69},{6,70},{7,71},{8,72},{9,... | collective-permute-start | bytes 1769480 | tf_op jit(solution)/shard_map/ppermute | solution.py:38
  89.6 16.6 %collective-permute-start.34 = (bf16[4,8,72,128]{3,2,1,0:T(8,128)(2,1)S(1)}, bf16[4,8,72,128]{3,2,1,0:T(8,128)(2,1)S(1)}, u32[]{:S(2)}, u32[]{:S(2)}) collective-permute-start(bf16[4,8,72,128]{3,2,1,0:T(8,128)(2,1)S(1)} %pad_maximum_fusion.1.rest_0_), channel_id=1, source_target_pairs={{0,192},{1,193},{2,194},{3,195},{4,196},{5,197},{6,198},{7,199},{8... | collective-permute-start | bytes 1769480 | tf_op jit(solution)/shard_map/ppermute | solution.py:38
  91.1 25.4 %collective-permute-start.35 = (bf16[4,8,72,128]{3,2,1,0:T(8,128)(2,1)S(1)}, bf16[4,8,72,128]{3,2,1,0:T(8,128)(2,1)S(1)}, u32[]{:S(2)}, u32[]{:S(2)}) collective-permute-start(bf16[4,8,72,128]{3,2,1,0:T(8,128)(2,1)S(1)} %pad_maximum_fusion.1.rest_0_), channel_id=1, source_target_pairs={{0,32},{1,33},{2,34},{3,35},{4,36},{5,37},{6,38},{7,39},{8,40},{9,... | collective-permute-start | bytes 1769480 | tf_op jit(solution)/shard_map/ppermute | solution.py:54
  93.0 13.6 %collective-permute-start.33 = (bf16[2,8,72,128]{3,2,1,0:T(8,128)(2,1)S(1)}, bf16[2,8,72,128]{3,2,1,0:T(8,128)(2,1)S(1)}, u32[]{:S(2)}, u32[]{:S(2)}) collective-permute-start(bf16[2,8,72,128]{3,2,1,0:T(8,128)(2,1)S(1)} %pad_maximum_fusion.3), channel_id=1, source_target_pairs={{0,128},{1,129},{2,130},{3,131},{4,132},{5,133},{6,134},{7,135},{8... | collective-permute-start | bytes 884744 | tf_op jit(solution)/shard_map/ppermute | solution.py:38
  94.1 12.7 %collective-permute-start.32 = (bf16[2,8,72,128]{3,2,1,0:T(8,128)(2,1)S(1)}, bf16[2,8,72,128]{3,2,1,0:T(8,128)(2,1)S(1)}, u32[]{:S(2)}, u32[]{:S(2)}) collective-permute-start(bf16[2,8,72,128]{3,2,1,0:T(8,128)(2,1)S(1)} %pad_maximum_fusion.2), channel_id=1, source_target_pairs={{0,128},{1,129},{2,130},{3,131},{4,132},{5,133},{6,134},{7,135},{8... | collective-permute-start | bytes 884744 | tf_op jit(solution)/shard_map/ppermute | solution.py:38
  98.0 18.5 %collective-permute-start.36 = (bf16[4,8,72,128]{3,2,1,0:T(8,128)(2,1)S(1)}, bf16[4,8,72,128]{3,2,1,0:T(8,128)(2,1)S(1)}, u32[]{:S(2)}, u32[]{:S(2)}) collective-permute-start(bf16[4,8,72,128]{3,2,1,0:T(8,128)(2,1)S(1)} %collective-permute-done.31.rest_1_), channel_id=1, source_target_pairs={{0,32},{1,33},{2,34},{3,35},{4,36},{5,37},{6,38},{7,39},{8,40},{9,... | collective-permute-start | bytes 1769480 | tf_op jit(solution)/shard_map/ppermute | solution.py:54
  106.2 10.4 %collective-permute-start.39 = (bf16[4,8,72,128]{3,2,1,0:T(8,128)(2,1)S(1)}, bf16[4,8,72,128]{3,2,1,0:T(8,128)(2,1)S(1)}, u32[]{:S(2)}, u32[]{:S(2)}) collective-permute-start(bf16[4,8,72,128]{3,2,1,0:T(8,128)(2,1)S(1)} %collective-permute-done.34.rest_4_), channel_id=1, source_target_pairs={{0,32},{1,33},{2,34},{3,35},{4,36},{5,37},{6,38},{7,39},{8,40},{9,... | collective-permute-start | bytes 1769480 | tf_op jit(solution)/shard_map/ppermute | solution.py:54
  106.5 10.0 %collective-permute-start.38 = (bf16[2,8,72,128]{3,2,1,0:T(8,128)(2,1)S(1)}, bf16[2,8,72,128]{3,2,1,0:T(8,128)(2,1)S(1)}, u32[]{:S(2)}, u32[]{:S(2)}) collective-permute-start(bf16[2,8,72,128]{3,2,1,0:T(8,128)(2,1)S(1)} %collective-permute-done.33.rest_3_), channel_id=1, source_target_pairs={{0,32},{1,33},{2,34},{3,35},{4,36},{5,37},{6,38},{7,39},{8,40},{9,... | collective-permute-start | bytes 884744 | tf_op jit(solution)/shard_map/ppermute | solution.py:54
  106.7 9.8 %collective-permute-start.37 = (bf16[2,8,72,128]{3,2,1,0:T(8,128)(2,1)S(1)}, bf16[2,8,72,128]{3,2,1,0:T(8,128)(2,1)S(1)}, u32[]{:S(2)}, u32[]{:S(2)}) collective-permute-start(bf16[2,8,72,128]{3,2,1,0:T(8,128)(2,1)S(1)} %collective-permute-done.32.rest_2_), channel_id=1, source_target_pairs={{0,32},{1,33},{2,34},{3,35},{4,36},{5,37},{6,38},{7,39},{8,40},{9,... | collective-permute-start | bytes 884744 | tf_op jit(solution)/shard_map/ppermute | solution.py:54
  (22 other events, 122.8 us)
